TPU v7x, 32 devices: a whole 2x2x4 slice. The times are simulated.
32 devices in a mesh: dp: 4 (over z), fsdp: 8 (over y, x, core).
Axes of the slice: x: 2, y: 2, z: 4, core: 2. Of those that a mesh axis runs over, the one named last changes fastest.
Arguments:
- hidden: bfloat16 [65536, 1024], P(('dp', 'fsdp')), may hold values from -6 to 6
- cotangent: bfloat16 [65536, 1024], P(('dp', 'fsdp')), may hold values from -6 to 6
- route_pos: int32 [32, 256], P(('dp', 'fsdp')), may hold values from 0 to 2047, as said below
- route_doc: int32 [32, 256], P(('dp', 'fsdp')), may hold values from 0 to 2, as said below
- w_qkv: bfloat16 [1024, 3072], P('fsdp'), may hold values from -0.1875 to 0.1875
- w_out: bfloat16 [1024, 1024], P('fsdp'), may hold values from -0.75 to 0.75
- w_up: bfloat16 [1024, 4096], P('fsdp'), may hold values from -0.1875 to 0.1875
- w_down: bfloat16 [4096, 1024], P('fsdp'), may hold values from -0.09375 to 0.09375
- router: float32 [1024], replicated, may hold values from -0.1875 to 0.1875
- gain_one: float32 [1024], replicated, may hold values from 0.5 to 1.5
- gain_two: float32 [1024], replicated, may hold values from 0.5 to 1.5
Outputs:
- output: bfloat16 [65536, 1024], P(('dp', 'fsdp'))
- grad_hidden: bfloat16 [65536, 1024], P(('dp', 'fsdp'))
- grad_qkv: float32 [1024, 3072], P('fsdp')
- grad_out: float32 [1024, 1024], P('fsdp')
- grad_up: float32 [1024, 4096], P('fsdp')
- grad_down: float32 [4096, 1024], P('fsdp')
- grad_router: float32 [1024], replicated
- grad_gain_one: float32 [1024], replicated
- grad_gain_two: float32 [1024], replicated
Inputs may be any that keep to these rules, and one draw needn't show every extreme that they name: `route_pos`: A buffer holds one sequence of 1024 tokens, one of 2048, or two of 1024, each starting at a multiple of 1024; a sequence of L tokens has L / 8 routed slots. Slots of a buffer are distinct and ascending, and the buffer's last slot is routed. `route_doc`: 0 and 1 name the sequences of a buffer; 2 marks an empty slot. In every draw some buffer has all 256 slots live and some has half of them empty.
All inputs are finite; a program needn't handle non-finite values.
Results may differ from a plain program's by a relative error of at most 0.011.
Values may be sent and summed in bfloat16 or wider, within the bound.
A program may use at most 192 MiB of HBM per device.

v0:
```python
import jax
import jax.numpy as jnp
from jax import lax
from jax.sharding import PartitionSpec as P

D = 1024
HEADS = 16
HEAD = 64


EPS = 1e-06


def rms_scale(values, gain_vec):
    return values * lax.rsqrt(jnp.mean(values * values, axis=-1, keepdims=True) + EPS) * gain_vec


def forward(tokens, positions, documents, weights, router, gain_one, gain_two):
    full_qkv, full_out, full_up, full_down = weights
    routed = tokens[positions].astype(jnp.float32)
    row_count = routed.shape[0]
    router_out = jnp.dot(routed, router, precision=lax.Precision.HIGHEST)
    normed_in = rms_scale(routed, gain_one).astype(jnp.bfloat16)
    packed = jnp.dot(normed_in, full_qkv, preferred_element_type=jnp.float32).astype(jnp.bfloat16)
    heads = packed.reshape(row_count, 3, HEADS, HEAD)
    allowed = (documents[:, None] == documents[None, :]) & (
        positions[None, :] <= positions[:, None]
    )
    scores = (
        jnp.einsum("qhd,khd->hqk", heads[:, 0], heads[:, 1], preferred_element_type=jnp.float32)
        * 0.125
    )
    scores = jnp.where(allowed[None], scores, -1000000000.0)
    row_max = jnp.max(scores, axis=-1, keepdims=True)
    log_total = row_max + jnp.log(jnp.sum(jnp.exp(scores - row_max), axis=-1, keepdims=True))
    prob_rows = jnp.exp(scores - log_total)
    prob_low = prob_rows.astype(jnp.bfloat16)
    attended = jnp.einsum("hqk,khd->qhd", prob_low, heads[:, 2], preferred_element_type=jnp.float32)
    attended = attended.reshape(row_count, D).astype(jnp.bfloat16)
    attn_out = jnp.dot(attended, full_out, preferred_element_type=jnp.float32)
    middle = routed + attn_out
    normed_mid = rms_scale(middle, gain_two).astype(jnp.bfloat16)
    up_in = jnp.dot(normed_mid, full_up, preferred_element_type=jnp.float32)
    activated = jax.nn.gelu(up_in).astype(jnp.bfloat16)
    mlp_out = jnp.dot(activated, full_down, preferred_element_type=jnp.float32)
    return (
        routed,
        router_out,
        normed_in,
        heads,
        prob_rows,
        prob_low,
        attended,
        attn_out,
        middle,
        normed_mid,
        up_in,
        activated,
        mlp_out,
    )


def per_device(
    hidden, cotangent, route_pos, route_doc, w_qkv, w_out, w_up, w_down, router, gain_one, gain_two
):
    positions = route_pos[0]
    documents = route_doc[0]
    live_mask = (documents < 2).astype(jnp.float32)[:, None]
    gathered = (
        lax.all_gather(w_qkv, "fsdp", axis=0, tiled=True),
        lax.all_gather(w_out, "fsdp", axis=0, tiled=True),
        lax.all_gather(w_up, "fsdp", axis=0, tiled=True),
        lax.all_gather(w_down, "fsdp", axis=0, tiled=True),
    )
    state = forward(hidden, positions, documents, gathered, router, gain_one, gain_two)
    attn_first = state[7]
    mlp_first = state[12]
    added = live_mask * state[1][:, None] * (attn_first + mlp_first)
    output = hidden.astype(jnp.float32).at[positions].add(added).astype(jnp.bfloat16)
    weights = (
        lax.all_gather(w_qkv, "fsdp", axis=0, tiled=True),
        lax.all_gather(w_out, "fsdp", axis=0, tiled=True),
        lax.all_gather(w_up, "fsdp", axis=0, tiled=True),
        lax.all_gather(w_down, "fsdp", axis=0, tiled=True),
    )
    state = forward(hidden, positions, documents, weights, router, gain_one, gain_two)
    full_qkv, full_out, full_up, full_down = weights
    (
        routed,
        router_out,
        normed_in,
        heads,
        prob_rows,
        prob_low,
        attended,
        attn_out,
        middle,
        normed_mid,
        up_in,
        activated,
        mlp_out,
    ) = state
    row_count = routed.shape[0]
    branch_out = attn_out + mlp_out
    grad_add = live_mask * cotangent[positions].astype(jnp.float32)
    grad_branch = grad_add * router_out[:, None]
    grad_score = jnp.sum(grad_add * branch_out, axis=-1)
    grad_mlp = grad_branch.astype(jnp.bfloat16)
    grad_down = jnp.dot(activated.T, grad_mlp, preferred_element_type=jnp.float32)
    grad_act = jnp.dot(grad_mlp, full_down.T, preferred_element_type=jnp.float32)
    _, gelu_pull = jax.vjp(jax.nn.gelu, up_in)
    grad_up_in = gelu_pull(grad_act)[0].astype(jnp.bfloat16)
    grad_up = jnp.dot(normed_mid.T, grad_up_in, preferred_element_type=jnp.float32)
    grad_norm_mid = jnp.dot(grad_up_in, full_up.T, preferred_element_type=jnp.float32)
    _, second_pull = jax.vjp(rms_scale, middle, gain_two)
    grad_middle, grad_gain_two = second_pull(grad_norm_mid)
    grad_attn = (grad_branch + grad_middle).astype(jnp.bfloat16)
    grad_out = jnp.dot(attended.T, grad_attn, preferred_element_type=jnp.float32)
    grad_attended = jnp.dot(grad_attn, full_out.T, preferred_element_type=jnp.float32).astype(
        jnp.bfloat16
    )
    grad_attended = grad_attended.reshape(row_count, HEADS, HEAD)
    grad_prob = jnp.einsum(
        "qhd,khd->hqk", grad_attended, heads[:, 2], preferred_element_type=jnp.float32
    )
    grad_value = jnp.einsum(
        "hqk,qhd->khd", prob_low, grad_attended, preferred_element_type=jnp.float32
    )
    row_dot = jnp.sum(grad_prob * prob_rows, axis=-1, keepdims=True)
    grad_scores = (prob_rows * (grad_prob - row_dot)).astype(jnp.bfloat16)
    grad_query = (
        jnp.einsum("hqk,khd->qhd", grad_scores, heads[:, 1], preferred_element_type=jnp.float32)
        * 0.125
    )
    grad_key = (
        jnp.einsum("hqk,qhd->khd", grad_scores, heads[:, 0], preferred_element_type=jnp.float32)
        * 0.125
    )
    grad_packed = jnp.stack([grad_query, grad_key, grad_value], axis=1).reshape(row_count, 3 * D)
    grad_packed = grad_packed.astype(jnp.bfloat16)
    grad_qkv = jnp.dot(normed_in.T, grad_packed, preferred_element_type=jnp.float32)
    grad_norm_in = jnp.dot(grad_packed, full_qkv.T, preferred_element_type=jnp.float32)
    _, first_pull = jax.vjp(rms_scale, routed, gain_one)
    grad_routed, grad_gain_one = first_pull(grad_norm_in)
    grad_routed = grad_routed + grad_middle + grad_score[:, None] * router[None, :]
    grad_router = jnp.dot(grad_score, routed, precision=lax.Precision.HIGHEST)
    grad_hidden = cotangent.astype(jnp.float32).at[positions].add(grad_routed).astype(jnp.bfloat16)
    shard_sums = (
        lax.psum_scatter(grad_qkv, "fsdp", scatter_dimension=0, tiled=True),
        lax.psum_scatter(grad_out, "fsdp", scatter_dimension=0, tiled=True),
        lax.psum_scatter(grad_up, "fsdp", scatter_dimension=0, tiled=True),
        lax.psum_scatter(grad_down, "fsdp", scatter_dimension=0, tiled=True),
    )
    final_sums = lax.psum((shard_sums[0], shard_sums[1], shard_sums[2], shard_sums[3]), "dp")
    small_sums = lax.psum((grad_router, grad_gain_one, grad_gain_two), ("dp", "fsdp"))
    return (
        output,
        grad_hidden,
        final_sums[0],
        final_sums[1],
        final_sums[2],
        final_sums[3],
        small_sums[0],
        small_sums[1],
        small_sums[2],
    )


def solution(mesh):
    return jax.shard_map(
        per_device,
        mesh=mesh,
        in_specs=(
            P(("dp", "fsdp"), None),
            P(("dp", "fsdp"), None),
            P(("dp", "fsdp"), None),
            P(("dp", "fsdp"), None),
            P("fsdp", None),
            P("fsdp", None),
            P("fsdp", None),
            P("fsdp", None),
            P(),
            P(),
            P(),
        ),
        out_specs=(
            P(("dp", "fsdp"), None),
            P(("dp", "fsdp"), None),
            P("fsdp", None),
            P("fsdp", None),
            P("fsdp", None),
            P("fsdp", None),
            P(),
            P(),
            P(),
        ),
        check_vma=False,
    )
```

profile of v0, /device:TPU:0, one launch (start us, length us, event | category | flops | bytes accessed | tf_op | source)
XLA Modules:
  0.0 850.8 jit_solution(8434318518896489657)
XLA Ops:
  7.2 0.7 all-gather.5.cloned.1.call-update
  8.0 0.7 all-gather.7.cloned.1.call-update
  8.7 0.7 all-gather.9.cloned.1.call-update
  9.4 0.5 all-gather.11.cloned.1.call-update
  10.0 0.0 reduce-scatter.7.cloned.1.call-start
  10.0 0.7 compare_select_fusion
  10.8 4.3 gather_fusion
  15.1 5.1 gather_fusion.1
  20.1 0.2 fusion.22
  20.4 0.1 compare_and_fusion
  20.5 0.5 fusion.59
  21.0 37.0 %all-gather.5.cloned.1.call-done = bf16[1024,3072]{1,0:T(8,128)(2,1)} async-done(((bf16[128,3072]{1,0:T(8,128)(2,1)}), bf16[1024,3072]{1,0:T(8,128)(2,1)}) %all-gather.5.cloned.1.call-update) | async-done | bytes 6291472 | tf_op jit(solution)/shard_map/all_gather | solution.py:70
  58.0 5.8 convolution_convert_fusion
  63.8 1.9 copy.29
  65.7 0.8 fusion.7
  66.5 0.9 exponential_reduce_fusion
  67.4 1.1 copy-done
  68.5 1.9 convolution_convert_fusion.3
  70.5 17.2 %all-gather.7.cloned.1.call-done = bf16[1024,1024]{1,0:T(8,128)(2,1)} async-done(((bf16[128,1024]{1,0:T(8,128)(2,1)}), bf16[1024,1024]{1,0:T(8,128)(2,1)}) %all-gather.7.cloned.1.call-update) | async-done | bytes 2097168 | tf_op jit(solution)/shard_map/all_gather | solution.py:71
  87.7 3.5 multiply_reduce_fusion.4
  91.2 52.7 %all-gather.9.cloned.1.call-done = bf16[1024,4096]{1,0:T(8,128)(2,1)} async-done(((bf16[128,4096]{1,0:T(8,128)(2,1)}), bf16[1024,4096]{1,0:T(8,128)(2,1)}) %all-gather.9.cloned.1.call-update) | async-done | bytes 8388624 | tf_op jit(solution)/shard_map/all_gather | solution.py:72
  143.9 7.8 fusion.58
  151.7 48.2 %all-gather.11.cloned.1.call-done = bf16[4096,1024]{1,0:T(8,128)(2,1)} async-done(((bf16[512,1024]{1,0:T(8,128)(2,1)}), bf16[4096,1024]{1,0:T(8,128)(2,1)}) %all-gather.11.cloned.1.call-update) | async-done | bytes 8388624 | tf_op jit(solution)/shard_map/all_gather | solution.py:73
  199.9 9.4 %fusion.6 = bf16[256,4096]{1,0:T(8,128)(2,1)S(1)} fusion(f32[256,4096]{1,0:T(8,128)} %fusion.58, bf16[4096,1024]{1,0:T(8,128)(2,1)} %all-gather.11.cloned.1.call-done, bf16[256,1024]{1,0:T(8,128)(2,1)} %gather_fusion.1, f32[256]{0:T(256)S(1)} %bitcast.85, f32[256]{0:T(256)S(1)} %fusion.46), kind=kOutput, calls=%fused_computation.12 | convolution fusion | flops 2169503744 | bytes 15206400 | tf_op jit(solution)/shard_map/dot_general | solution.py:110
  209.4 2.8 multiply_reduce_fusion.1
  212.3 0.1 copy-done.7
  212.4 0.3 copy-done.12
  212.7 7.4 multiply_reduce_fusion.2
  220.1 0.8 copy-done.13
  220.9 2.7 fusion.60
  223.6 0.0 reduce-scatter.5.cloned.1.call-start
  223.7 3.3 convolution_convert_fusion.2
  227.0 2.1 copy.31
  229.1 4.2 multiply_reduce_fusion
  233.3 0.1 copy-done.1
  233.4 1.2 multiply_convert_fusion
  234.6 0.8 fusion.13
  235.4 0.5 fusion.14
  235.9 1.1 fusion.15
  236.9 0.2 pad_maximum_fusion
  237.1 6.5 fusion.39
  243.6 0.4 reduce-scatter.11.cloned.1.call-start
  244.1 11.4 %fusion.51 = f32[4096,1024]{1,0:T(8,128)} fusion(bf16[256,1024]{1,0:T(8,128)(2,1)} %gather_fusion.1, f32[256]{0:T(256)S(1)} %bitcast.87, f32[256]{0:T(256)S(1)} %fusion.46, f32[256,4096]{1,0:T(8,128)} %fusion.58), kind=kOutput, calls=%fused_computation.93 | convolution fusion | flops 2157969408 | bytes 21497856 | tf_op jit(solution)/shard_map/dot_general | solution.py:109
  255.5 0.0 reduce-scatter.9.cloned.1.call-start
  255.6 9.8 %fusion.57 = f32[1024,4096]{1,0:T(8,128)} fusion(bf16[256,4096]{1,0:T(8,128)(2,1)} %copy-done.6, f32[256,1024]{1,0:T(8,128)S(1)} %get-tuple-element.21, f32[1024]{0:T(1024)S(1)} %copy-done.14, f32[256]{0:T(256)S(1)} %fusion.45), kind=kOutput, calls=%fused_computation.95 | convolution fusion | flops 2148270080 | bytes 19928064 | tf_op jit(solution)/shard_map/dot_general | solution.py:113
  265.4 0.0 all-reduce.4.cloned.1.call-start
  265.5 9.4 %reduce-scatter.7.cloned.1.call-done = f32[128,1024]{1,0:T(8,128)} async-done(((f32[1024,1024]{1,0:T(8,128)}), f32[128,1024]{1,0:T(8,128)}) %reduce-scatter.7.cloned.1.call-update) | async-done | bytes 524304 | tf_op jit(solution)/shard_map/reduce_scatter | solution.py:150
  274.9 95.7 %reduce-scatter.5.cloned.1.call-done = f32[128,3072]{1,0:T(8,128)} async-done(((f32[1024,3072]{1,0:T(8,128)}), f32[128,3072]{1,0:T(8,128)}) %reduce-scatter.5.cloned.1.call-update) | async-done | bytes 1572880 | tf_op jit(solution)/shard_map/reduce_scatter | solution.py:149
  370.6 119.8 %reduce-scatter.11.cloned.1.call-done = f32[512,1024]{1,0:T(8,128)} async-done(((f32[4096,1024]{1,0:T(8,128)}), f32[512,1024]{1,0:T(8,128)}) %reduce-scatter.11.cloned.1.call-update) | async-done | bytes 2097168 | tf_op jit(solution)/shard_map/reduce_scatter | solution.py:152
  490.4 119.8 %reduce-scatter.9.cloned.1.call-done = f32[128,4096]{1,0:T(8,128)} async-done(((f32[1024,4096]{1,0:T(8,128)}), f32[128,4096]{1,0:T(8,128)}) %reduce-scatter.9.cloned.1.call-update) | async-done | bytes 2097168 | tf_op jit(solution)/shard_map/reduce_scatter | solution.py:151
  610.2 6.6 convert_element_type.75
  616.8 4.6 convert_element_type.86
  621.5 10.1 %scatter_custom_fusion = f32[2048,1024]{1,0:T(8,128)} fusion(f32[2048,1024]{1,0:T(8,128)} %convert_element_type.75, s32[256]{0:T(256)S(1)} %bitcast.92, f32[256,1024]{1,0:T(8,128)} %get-tuple-element.28, f32[256]{0:T(256)S(1)} %broadcast_select_fusion), kind=kCustom, calls=%fused_computation.59 | custom fusion | flops 524288 | bytes 9438208 | tf_op jit(solution)/shard_map/scatter-add | solution.py:79
  631.6 6.1 convert_element_type.85
  637.7 5.7 fusion.17
  643.4 10.7 %scatter_custom_fusion.1 = f32[2048,1024]{1,0:T(8,128)} fusion(f32[2048,1024]{1,0:T(8,128)} %convert_element_type.86, s32[256]{0:T(256)S(1)} %bitcast.93, bf16[256,1024]{1,0:T(8,128)(2,1)S(1)} %gather_fusion, f32[256,1024]{1,0:T(8,128)} %get-tuple-element.31, f32[1024]{0:T(1024)S(1)} %copy-done.16, f32[256]{0:T(256)S(1)} %get-tuple-element.22, ...), kind=kCustom, calls=%fused_computation.47 | custom fusion | flops 3932160 | bytes 12076032 | tf_op jit(solution)/shard_map/scatter-add | solution.py:147
  654.1 6.1 convert_element_type.95
  660.1 0.3 fusion.61
  660.5 48.3 %all-reduce = (f32[1024]{0:T(1024)}, f32[1024]{0:T(1024)}, f32[1024]{0:T(1024)}) all-reduce(f32[1024]{0:T(1024)S(1)} %bitcast.81, f32[1024]{0:T(1024)S(1)} %get-tuple-element.11, f32[1024]{0:T(1024)S(1)} %get-tuple-element.9), channel_id=1, replica_groups=mesh['dp'=4,'fsdp'=8] {'dp','fsdp'}, use_global_device_ids=true, to_apply=%region_18.19 | all-reduce | flops 3072 | bytes 24576 | tf_op jit(solution)/shard_map/psum | solution.py:155
  708.7 127.9 %all-reduce.4.cloned.1.call-done = (f32[128,3072]{1,0:T(8,128)}, f32[128,1024]{1,0:T(8,128)}, f32[128,4096]{1,0:T(8,128)}, f32[512,1024]{1,0:T(8,128)}) async-done(((f32[128,3072]{1,0:T(8,128)}, f32[128,1024]{1,0:T(8,128)}, f32[128,4096]{1,0:T(8,128)}, f32[512,1024]{1,0:T(8,128)}), (f32[128,3072]{1,0:T(8,128)}, f32[128,1024]{1,0:T(8,128)}, f32[128,4096]{1,0:T(8,128)}, ...) | async-done | bytes 6291472 | tf_op jit(solution)/shard_map/psum | solution.py:154
  836.7 2.9 copy.45
  839.5 1.9 copy.46
  841.4 1.3 copy.47
  842.7 1.3 copy.48
  (50 shorter events, 0.4 us)
Async XLA Ops:
  7.2 50.8 %all-gather.5.cloned.1.call-start = ((), (), s32[]{:S(2)}) async-start(), calls=%async_computation.4 | async-start | bytes 7077888 | tf_op jit(solution)/shard_map/all_gather | solution.py:70
  7.9 79.8 %all-gather.7.cloned.1.call-start = ((), (), s32[]{:S(2)}) async-start(), calls=%async_computation.5 | async-start | bytes 2359296 | tf_op jit(solution)/shard_map/all_gather | solution.py:71
  8.7 135.2 %all-gather.9.cloned.1.call-start = ((), (), s32[]{:S(2)}) async-start(), calls=%async_computation.6 | async-start | bytes 9437184 | tf_op jit(solution)/shard_map/all_gather | solution.py:72
  9.4 190.5 %all-gather.11.cloned.1.call-start = ((), (), s32[]{:S(2)}) async-start(), calls=%async_computation.7 | async-start | bytes 9437184 | tf_op jit(solution)/shard_map/all_gather | solution.py:73
  10.0 264.9 %reduce-scatter.7.cloned.1.call-start = ((), (), s32[]{:S(2)}) async-start(), calls=%async_computation.9 | async-start | bytes 4718592 | tf_op jit(solution)/shard_map/reduce_scatter | solution.py:150
  10.7 9.6 %copy-start.17 = (s32[1,256]{1,0:T(1,128)S(1)}, s32[1,256]{1,0:T(1,128)}, u32[]{:S(2)}) copy-start(s32[1,256]{1,0:T(1,128)} %param.14) | copy-start | bytes 3076
  10.7 9.6 %copy-start.18 = (s32[1,256]{1,0:T(1,128)S(1)}, s32[1,256]{1,0:T(1,128)}, u32[]{:S(2)}) copy-start(s32[1,256]{1,0:T(1,128)} %param.13) | copy-start | bytes 3076
  10.7 9.8 %copy-start.16 = (f32[1024]{0:T(1024)S(1)}, f32[1024]{0:T(1024)}, u32[]{:S(2)}) copy-start(f32[1024]{0:T(1024)} %param.19) | copy-start | bytes 12292
  10.7 47.3 %copy-start.15 = (f32[1024]{0:T(1024)S(1)}, f32[1024]{0:T(1024)}, u32[]{:S(2)}) copy-start(f32[1024]{0:T(1024)} %param.20) | copy-start | bytes 12292
  66.5 2.0 copy-start
  70.5 73.4 %copy-start.14 = (f32[1024]{0:T(1024)S(1)}, f32[1024]{0:T(1024)}, u32[]{:S(2)}) copy-start(f32[1024]{0:T(1024)} %param.21) | copy-start | bytes 12292
  199.9 9.4 %copy-start.4 = (bf16[1024,4096]{1,0:T(8,128)(2,1)S(1)}, bf16[1024,4096]{1,0:T(8,128)(2,1)}, u32[]{:S(2)}) copy-start(bf16[1024,4096]{1,0:T(8,128)(2,1)} %all-gather.9.cloned.1.call-done) | copy-start | bytes 25165828
  209.3 2.9 copy-start.6
  209.3 2.9 copy-start.2
  209.3 3.1 copy-start.7
  209.3 3.4 copy-start.12
  212.2 7.9 copy-start.11
  212.7 8.2 copy-start.5
  220.1 0.8 copy-start.13
  223.6 147.0 %reduce-scatter.5.cloned.1.call-start = ((), (), s32[]{:S(2)}) async-start(), calls=%async_computation.8 | async-start | bytes 14155776 | tf_op jit(solution)/shard_map/reduce_scatter | solution.py:149
  229.1 4.3 copy-start.1
  234.6 1.3 copy-start.8
  243.6 246.8 %reduce-scatter.11.cloned.1.call-start = ((), (), s32[]{:S(2)}) async-start(), calls=%async_computation.11 | async-start | bytes 18874368 | tf_op jit(solution)/shard_map/reduce_scatter | solution.py:152
  255.5 354.6 %reduce-scatter.9.cloned.1.call-start = ((), (), s32[]{:S(2)}) async-start(), calls=%async_computation.10 | async-start | bytes 18874368 | tf_op jit(solution)/shard_map/reduce_scatter | solution.py:151
  265.4 571.2 %all-reduce.4.cloned.1.call-start = ((), (), s32[]{:S(2)}) async-start(), calls=%async_computation.12 | async-start | bytes 12582912 | tf_op jit(solution)/shard_map/psum | solution.py:154
  610.2 6.6 copy-start.3
  836.7 4.7 copy-start.10
  836.7 6.1 copy-start.9
Sparse Core Ops, SparseCore 0:
  9.9 48.1 all-gather.4
  59.9 27.7 all-gather.6
  89.6 54.2 all-gather.8
  145.6 54.2 all-gather.10
  223.7 51.1 reduce-scatter.6
  278.3 92.2 reduce-scatter.4
  374.1 116.1 reduce-scatter.10
  493.9 116.1 reduce-scatter.8
  612.8 223.8 all-reduce.3
where the time goes:
time: 856 us; the launch traced here: 851 us
  waiting for transfers between devices  630 us (74%)
  matrix products  86.1 us (10%)
  blocking collectives  48.3 us (6%)
  other arithmetic  47.6 us (6%)
  local copies, waits for them, and re-layouts  23.3 us (3%)
  between operations  14.3 us (2%)
    psum x1, waiting for transfers between devices, per_device(): lax.psum((shard_sums[0], shard_sums[1], shard_sums[2], shard_sums[3]), 'dp')  128 us
    reduce_scatter x1, waiting for transfers between devices, per_device(): lax.psum_scatter(grad_down, 'fsdp', scatter_dimension=0, tiled=True)  120 us
    reduce_scatter x1, waiting for transfers between devices, per_device(): lax.psum_scatter(grad_up, 'fsdp', scatter_dimension=0, tiled=True)  120 us
    reduce_scatter x1, waiting for transfers between devices, per_device(): lax.psum_scatter(grad_qkv, 'fsdp', scatter_dimension=0, tiled=True)  95.7 us
    all_gather x1, waiting for transfers between devices, per_device(): lax.all_gather(w_up, 'fsdp', axis=0, tiled=True)  52.7 us
    psum x1, blocking collectives, per_device(): lax.psum((grad_router, grad_gain_one, grad_gain_two), ('dp', 'fsdp'))  48.3 us
    all_gather x1, waiting for transfers between devices, per_device(): lax.all_gather(w_down, 'fsdp', axis=0, tiled=True)  48.2 us
    all_gather x1, waiting for transfers between devices, per_device(): lax.all_gather(w_qkv, 'fsdp', axis=0, tiled=True)  37 us
  transfers between devices with their start and end apart: 9, of which 9 were waited for; matrix products, arithmetic and copies ran while one was open for 15% of the time, Pallas kernels for 0%

commit v1 on v0

--- a/solution.py
+++ b/solution.py
@@ -146,20 +146,20 @@
     grad_router = jnp.dot(grad_score, routed, precision=lax.Precision.HIGHEST)
     grad_hidden = cotangent.astype(jnp.float32).at[positions].add(grad_routed).astype(jnp.bfloat16)
     shard_sums = (
-        lax.psum_scatter(grad_qkv, "fsdp", scatter_dimension=0, tiled=True),
-        lax.psum_scatter(grad_out, "fsdp", scatter_dimension=0, tiled=True),
-        lax.psum_scatter(grad_up, "fsdp", scatter_dimension=0, tiled=True),
-        lax.psum_scatter(grad_down, "fsdp", scatter_dimension=0, tiled=True),
+        lax.psum_scatter(grad_qkv.astype(jnp.bfloat16), "fsdp", scatter_dimension=0, tiled=True),
+        lax.psum_scatter(grad_out.astype(jnp.bfloat16), "fsdp", scatter_dimension=0, tiled=True),
+        lax.psum_scatter(grad_up.astype(jnp.bfloat16), "fsdp", scatter_dimension=0, tiled=True),
+        lax.psum_scatter(grad_down.astype(jnp.bfloat16), "fsdp", scatter_dimension=0, tiled=True),
     )
     final_sums = lax.psum((shard_sums[0], shard_sums[1], shard_sums[2], shard_sums[3]), "dp")
     small_sums = lax.psum((grad_router, grad_gain_one, grad_gain_two), ("dp", "fsdp"))
     return (
         output,
         grad_hidden,
-        final_sums[0],
-        final_sums[1],
-        final_sums[2],
-        final_sums[3],
+        final_sums[0].astype(jnp.float32),
+        final_sums[1].astype(jnp.float32),
+        final_sums[2].astype(jnp.float32),
+        final_sums[3].astype(jnp.float32),
         small_sums[0],
         small_sums[1],
         small_sums[2],

time: 856 us -> 623 us (0.73)
  waiting for transfers between devices: 630 us -> 416 us
  matrix products: 86.1 us -> 75.6 us
    reduce_scatter x4, waiting for transfers between devices: 345 us -> 222 us  [the longest x1 75 us: per_device(): lax.psum_scatter(grad_down.astype(jnp.bfloat16), 'fsdp', scatter_dimensio...]
    psum x1, waiting for transfers between devices: 128 us -> 36 us  [per_device(): lax.psum((shard_sums[0], shard_sums[1], shard_sums[2], shard_sums[3]), 'dp')]
  transfers between devices with their start and end apart: 9 -> 9, of which waited for: 9 -> 9; matrix products, arithmetic and copies ran while one was open for 15% -> 18% of each run, Pallas kernels for 0% -> 0%
where the time goes in v1:
time: 623 us; the launch traced here: 618 us
  waiting for transfers between devices  416 us (67%)
  matrix products  75.6 us (12%)
  other arithmetic  54.5 us (9%)
  blocking collectives  41.2 us (7%)
  local copies, waits for them, and re-layouts  15.8 us (3%)
  between operations  14.3 us (2%)
    reduce_scatter x1, waiting for transfers between devices, per_device(): lax.psum_scatter(grad_down.astype(jnp.bfloat16), 'fsdp', scatter_dimensio...  75 us
    reduce_scatter x1, waiting for transfers between devices, per_device(): lax.psum_scatter(grad_up.astype(jnp.bfloat16), 'fsdp', scatter_dimension=...  75 us
    reduce_scatter x1, waiting for transfers between devices, per_device(): lax.psum_scatter(grad_qkv.astype(jnp.bfloat16), 'fsdp', scatter_dimension...  65 us
    all_gather x1, waiting for transfers between devices, per_device(): lax.all_gather(w_up, 'fsdp', axis=0, tiled=True)  52.7 us
    all_gather x1, waiting for transfers between devices, per_device(): lax.all_gather(w_down, 'fsdp', axis=0, tiled=True)  48.2 us
    psum x1, blocking collectives, per_device(): lax.psum((grad_router, grad_gain_one, grad_gain_two), ('dp', 'fsdp'))  41.2 us
    all_gather x1, waiting for transfers between devices, per_device(): lax.all_gather(w_qkv, 'fsdp', axis=0, tiled=True)  37 us
    psum x1, waiting for transfers between devices, per_device(): lax.psum((shard_sums[0], shard_sums[1], shard_sums[2], shard_sums[3]), 'dp')  36 us
  transfers between devices with their start and end apart: 9, of which 9 were waited for; matrix products, arithmetic and copies ran while one was open for 18% of the time, Pallas kernels for 0%

profile of v1, /device:TPU:0, one launch (start us, length us, event | category | flops | bytes accessed | tf_op | source)
XLA Modules:
  0.0 617.7 jit_solution(6788724416623618148)
XLA Ops:
  7.2 0.7 all-gather.5.cloned.1.call-update
  8.0 0.7 all-gather.7.cloned.1.call-update
  8.7 0.0 all-gather.9.cloned.1.call-start
  8.7 0.7 all-gather.9.cloned.1.call-update
  9.4 0.5 all-gather.11.cloned.1.call-update
  10.0 0.0 reduce-scatter.7.cloned.1.call-start
  10.0 0.7 compare_select_fusion
  10.8 4.3 gather_fusion
  15.1 5.1 gather_fusion.1
  20.1 0.2 fusion.22
  20.4 0.1 compare_and_fusion
  20.5 0.5 fusion.56
  21.0 37.0 %all-gather.5.cloned.1.call-done = bf16[1024,3072]{1,0:T(8,128)(2,1)} async-done(((bf16[128,3072]{1,0:T(8,128)(2,1)}), bf16[1024,3072]{1,0:T(8,128)(2,1)}) %all-gather.5.cloned.1.call-update) | async-done | bytes 6291472 | tf_op jit(solution)/shard_map/all_gather | solution.py:70
  58.0 5.8 convolution_convert_fusion.3
  63.8 1.9 copy.29
  65.7 0.8 fusion.7
  66.5 0.9 exponential_reduce_fusion
  67.4 1.1 copy-done
  68.5 1.9 convolution_convert_fusion.7
  70.4 17.3 %all-gather.7.cloned.1.call-done = bf16[1024,1024]{1,0:T(8,128)(2,1)} async-done(((bf16[128,1024]{1,0:T(8,128)(2,1)}), bf16[1024,1024]{1,0:T(8,128)(2,1)}) %all-gather.7.cloned.1.call-update) | async-done | bytes 2097168 | tf_op jit(solution)/shard_map/all_gather | solution.py:71
  87.7 3.5 multiply_reduce_fusion.4
  91.2 52.7 %all-gather.9.cloned.1.call-done = bf16[1024,4096]{1,0:T(8,128)(2,1)} async-done(((bf16[128,4096]{1,0:T(8,128)(2,1)}), bf16[1024,4096]{1,0:T(8,128)(2,1)}) %all-gather.9.cloned.1.call-update) | async-done | bytes 8388624 | tf_op jit(solution)/shard_map/all_gather | solution.py:72
  143.9 7.8 %fusion.55 = f32[256,4096]{1,0:T(8,128)} fusion(bf16[1024,4096]{1,0:T(8,128)(2,1)} %all-gather.9.cloned.1.call-done, f32[256,1024]{1,0:T(8,128)S(1)} %get-tuple-element.21, f32[1024]{0:T(1024)S(1)} %copy-done.14, f32[256]{0:T(256)S(1)} %fusion.44), kind=kOutput, calls=%fused_computation.97 | convolution fusion | flops 2148270080 | bytes 13636608 | tf_op jit(solution)/shard_map/dot_general | solution.py:43
  151.7 48.2 %all-gather.11.cloned.1.call-done = bf16[4096,1024]{1,0:T(8,128)(2,1)} async-done(((bf16[512,1024]{1,0:T(8,128)(2,1)}), bf16[4096,1024]{1,0:T(8,128)(2,1)}) %all-gather.11.cloned.1.call-update) | async-done | bytes 8388624 | tf_op jit(solution)/shard_map/all_gather | solution.py:73
  199.9 9.4 %fusion.6 = bf16[256,4096]{1,0:T(8,128)(2,1)S(1)} fusion(f32[256,4096]{1,0:T(8,128)} %fusion.55, bf16[4096,1024]{1,0:T(8,128)(2,1)} %all-gather.11.cloned.1.call-done, bf16[256,1024]{1,0:T(8,128)(2,1)} %gather_fusion.1, f32[256]{0:T(256)S(1)} %bitcast.87, f32[256]{0:T(256)S(1)} %fusion.45), kind=kOutput, calls=%fused_computation.15 | convolution fusion | flops 2169503744 | bytes 15206400 | tf_op jit(solution)/shard_map/dot_general | solution.py:110
  209.4 2.8 multiply_reduce_fusion.1
  212.3 0.3 copy-done.10
  212.6 0.1 copy-done.12
  212.7 7.3 %multiply_reduce_fusion.2 = (f32[256]{0:T(256)S(1)}, bf16[256,1024]{1,0:T(8,128)(2,1)S(1)}, f32[256,1024]{1,0:T(8,128)}) fusion(bf16[256,1024]{1,0:T(8,128)(2,1)S(1)} %copy-done.12, f32[256]{0:T(256)S(1)} %fusion.45, f32[256,1024]{1,0:T(8,128)S(1)} %get-tuple-element.21, f32[256]{0:T(256)S(1)} %multiply_multiply_fusion.3, f32[256]{0:T(256)S(1)} %fusion.44, ...), kind=kOutput, calls=%fused_computation.56 | convolution fusion | flops 2160328448 | bytes 17835008 | tf_op jit(solution)/shard_map/dot_general | solution.py:45
  220.0 0.8 copy-done.13
  220.9 2.0 convolution_convert_fusion.4
  222.9 0.0 reduce-scatter.5.cloned.1.call-start
  223.0 3.4 convolution_convert_fusion.6
  226.3 2.1 copy.31
  228.4 4.1 multiply_reduce_fusion
  232.5 1.2 multiply_convert_fusion
  233.7 0.5 fusion.14
  234.2 0.8 fusion.13
  235.0 1.1 fusion.15
  236.1 0.2 pad_maximum_fusion
  236.2 4.7 convolution_convert_fusion.2
  240.9 0.4 reduce-scatter.9.cloned.1.call-start
  241.4 7.3 %convolution_convert_fusion.1 = bf16[1024,4096]{1,0:T(8,128)(2,1)} fusion(bf16[256,4096]{1,0:T(8,128)(2,1)} %copy-done.6, f32[256,1024]{1,0:T(8,128)S(1)} %get-tuple-element.21, f32[1024]{0:T(1024)S(1)} %copy-done.14, f32[256]{0:T(256)S(1)} %fusion.44), kind=kOutput, calls=%fused_computation.5 | convolution fusion | flops 2152464384 | bytes 11539456 | tf_op jit(solution)/shard_map/dot_general | solution.py:113
  248.7 0.0 reduce-scatter.11.cloned.1.call-start
  248.7 8.7 %convolution_convert_fusion = bf16[4096,1024]{1,0:T(8,128)(2,1)} fusion(bf16[256,1024]{1,0:T(8,128)(2,1)} %gather_fusion.1, f32[256]{0:T(256)S(1)} %bitcast.89, f32[256]{0:T(256)S(1)} %fusion.45, f32[256,4096]{1,0:T(8,128)} %fusion.55), kind=kOutput, calls=%fused_computation.4 | convolution fusion | flops 2162163712 | bytes 13109248 | tf_op jit(solution)/shard_map/dot_general | solution.py:109
  257.5 0.0 all-reduce.4.cloned.1.call-start
  257.5 6.7 %reduce-scatter.7.cloned.1.call-done = bf16[128,1024]{1,0:T(8,128)(2,1)} async-done(((bf16[1024,1024]{1,0:T(8,128)(2,1)}), bf16[128,1024]{1,0:T(8,128)(2,1)}) %reduce-scatter.7.cloned.1.call-update) | async-done | bytes 262160 | tf_op jit(solution)/shard_map/reduce_scatter | solution.py:150
  264.2 65.0 %reduce-scatter.5.cloned.1.call-done = bf16[128,3072]{1,0:T(8,128)(2,1)} async-done(((bf16[1024,3072]{1,0:T(8,128)(2,1)}), bf16[128,3072]{1,0:T(8,128)(2,1)}) %reduce-scatter.5.cloned.1.call-update) | async-done | bytes 786448 | tf_op jit(solution)/shard_map/reduce_scatter | solution.py:149
  329.2 75.0 %reduce-scatter.9.cloned.1.call-done = bf16[128,4096]{1,0:T(8,128)(2,1)} async-done(((bf16[1024,4096]{1,0:T(8,128)(2,1)}), bf16[128,4096]{1,0:T(8,128)(2,1)}) %reduce-scatter.9.cloned.1.call-update) | async-done | bytes 1048592 | tf_op jit(solution)/shard_map/reduce_scatter | solution.py:151
  404.2 75.0 %reduce-scatter.11.cloned.1.call-done = bf16[512,1024]{1,0:T(8,128)(2,1)} async-done(((bf16[4096,1024]{1,0:T(8,128)(2,1)}), bf16[512,1024]{1,0:T(8,128)(2,1)}) %reduce-scatter.11.cloned.1.call-update) | async-done | bytes 1048592 | tf_op jit(solution)/shard_map/reduce_scatter | solution.py:152
  479.3 6.6 %convert_element_type.110 = f32[2048,1024]{1,0:T(8,128)} convert(bf16[2048,1024]{1,0:T(8,128)(2,1)} %param.12) | non-fusion elementwise | flops 2097152 | bytes 12582912 | tf_op jit(solution)/shard_map/convert_element_type | solution.py:147
  485.9 4.3 convert_element_type.99
  490.2 3.0 fusion.17
  493.2 10.9 %scatter_custom_fusion.1 = f32[2048,1024]{1,0:T(8,128)} fusion(f32[2048,1024]{1,0:T(8,128)} %convert_element_type.110, s32[256]{0:T(256)S(1)} %bitcast.92, bf16[256,1024]{1,0:T(8,128)(2,1)S(1)} %gather_fusion, f32[256,1024]{1,0:T(8,128)} %get-tuple-element.31, f32[1024]{0:T(1024)S(1)} %copy-done.17, f32[256]{0:T(256)S(1)} %get-tuple-element.22, ...), kind=kCustom, calls=%fused_computation.51 | custom fusion | flops 3932160 | bytes 12076032 | tf_op jit(solution)/shard_map/scatter-add | solution.py:147
  504.1 6.2 %convert_element_type.119 = bf16[2048,1024]{1,0:T(8,128)(2,1)} convert(f32[2048,1024]{1,0:T(8,128)} %scatter_custom_fusion.1) | non-fusion elementwise | flops 2097152 | bytes 12582912 | tf_op jit(solution)/shard_map/convert_element_type | solution.py:147
  510.3 9.3 %scatter_custom_fusion = f32[2048,1024]{1,0:T(8,128)} fusion(f32[2048,1024]{1,0:T(8,128)} %convert_element_type.99, s32[256]{0:T(256)S(1)} %bitcast.93, f32[256,1024]{1,0:T(8,128)S(1)} %copy-done.9, f32[256]{0:T(256)S(1)} %broadcast_select_fusion), kind=kCustom, calls=%fused_computation.63 | custom fusion | flops 524288 | bytes 9438208 | tf_op jit(solution)/shard_map/scatter-add | solution.py:79
  519.6 6.1 convert_element_type.109
  525.7 0.3 fusion.57
  526.0 41.2 %all-reduce = (f32[1024]{0:T(1024)}, f32[1024]{0:T(1024)}, f32[1024]{0:T(1024)}) all-reduce(f32[1024]{0:T(1024)S(1)} %bitcast.81, f32[1024]{0:T(1024)S(1)} %get-tuple-element.11, f32[1024]{0:T(1024)S(1)} %get-tuple-element.9), channel_id=1, replica_groups=mesh['dp'=4,'fsdp'=8] {'dp','fsdp'}, use_global_device_ids=true, to_apply=%region_18.19 | all-reduce | flops 3072 | bytes 24576 | tf_op jit(solution)/shard_map/psum | solution.py:155
  567.3 36.0 %all-reduce.4.cloned.1.call-done = (bf16[128,3072]{1,0:T(8,128)(2,1)}, bf16[128,1024]{1,0:T(8,128)(2,1)}, bf16[128,4096]{1,0:T(8,128)(2,1)}, bf16[512,1024]{1,0:T(8,128)(2,1)}) async-done(((bf16[128,3072]{1,0:T(8,128)(2,1)}, bf16[128,1024]{1,0:T(8,128)(2,1)}, bf16[128,4096]{1,0:T(8,128)(2,1)}, bf16[512,1024]{1,0:T(8,128)(2,1)}), (bf16[128,3072]{1,0:T(8,128)(2,1)}, bf16[128,1024]{1,0:T(8,128)(2,1)}, ...) | async-done | bytes 3145744 | tf_op jit(solution)/shard_map/psum | solution.py:154
  603.2 2.8 convert_element_type.125
  606.1 2.8 convert_element_type.127
  608.9 1.3 convert_element_type.121
  610.2 0.8 convert_element_type.123
  (57 shorter events, 0.4 us)
Async XLA Ops:
  7.2 50.8 %all-gather.5.cloned.1.call-start = ((), (), s32[]{:S(2)}) async-start(), calls=%async_computation.4 | async-start | bytes 7077888 | tf_op jit(solution)/shard_map/all_gather | solution.py:70
  7.9 79.8 %all-gather.7.cloned.1.call-start = ((), (), s32[]{:S(2)}) async-start(), calls=%async_computation.5 | async-start | bytes 2359296 | tf_op jit(solution)/shard_map/all_gather | solution.py:71
  8.7 135.2 %all-gather.9.cloned.1.call-start = ((), (), s32[]{:S(2)}) async-start(), calls=%async_computation.6 | async-start | bytes 9437184 | tf_op jit(solution)/shard_map/all_gather | solution.py:72
  9.4 190.5 %all-gather.11.cloned.1.call-start = ((), (), s32[]{:S(2)}) async-start(), calls=%async_computation.7 | async-start | bytes 9437184 | tf_op jit(solution)/shard_map/all_gather | solution.py:73
  10.0 254.2 %reduce-scatter.7.cloned.1.call-start = ((), (), s32[]{:S(2)}) async-start(), calls=%async_computation.9 | async-start | bytes 2359296 | tf_op jit(solution)/shard_map/reduce_scatter | solution.py:150
  10.7 9.6 %copy-start.18 = (s32[1,256]{1,0:T(1,128)S(1)}, s32[1,256]{1,0:T(1,128)}, u32[]{:S(2)}) copy-start(s32[1,256]{1,0:T(1,128)} %param.14) | copy-start | bytes 3076
  10.7 9.6 %copy-start.19 = (s32[1,256]{1,0:T(1,128)S(1)}, s32[1,256]{1,0:T(1,128)}, u32[]{:S(2)}) copy-start(s32[1,256]{1,0:T(1,128)} %param.13) | copy-start | bytes 3076
  10.7 9.8 %copy-start.17 = (f32[1024]{0:T(1024)S(1)}, f32[1024]{0:T(1024)}, u32[]{:S(2)}) copy-start(f32[1024]{0:T(1024)} %param.19) | copy-start | bytes 12292
  10.7 47.3 %copy-start.16 = (f32[1024]{0:T(1024)S(1)}, f32[1024]{0:T(1024)}, u32[]{:S(2)}) copy-start(f32[1024]{0:T(1024)} %param.20) | copy-start | bytes 12292
  66.5 2.0 copy-start
  70.4 73.5 %copy-start.14 = (f32[1024]{0:T(1024)S(1)}, f32[1024]{0:T(1024)}, u32[]{:S(2)}) copy-start(f32[1024]{0:T(1024)} %param.21) | copy-start | bytes 12292
  199.9 9.4 %copy-start.3 = (bf16[1024,4096]{1,0:T(8,128)(2,1)S(1)}, bf16[1024,4096]{1,0:T(8,128)(2,1)}, u32[]{:S(2)}) copy-start(bf16[1024,4096]{1,0:T(8,128)(2,1)} %all-gather.9.cloned.1.call-done) | copy-start | bytes 25165828
  209.3 2.9 copy-start.6
  209.3 2.9 copy-start.4
  209.3 3.2 copy-start.10
  209.3 3.3 copy-start.12
  212.2 7.8 %copy-start.8 = (f32[256,1024]{1,0:T(8,128)}, f32[256,1024]{1,0:T(8,128)S(1)}, u32[]{:S(2)}) copy-start(f32[256,1024]{1,0:T(8,128)S(1)} %get-tuple-element.27) | copy-start | bytes 3145732
  212.7 8.2 %copy-start.7 = (bf16[16,64,256]{2,1,0:T(8,128)(2,1)S(1)}, bf16[16,64,256]{2,1,0:T(8,128)(2,1)}, u32[]{:S(2)}) copy-start(bf16[16,64,256]{2,1,0:T(8,128)(2,1)} %convolution_convert_fusion.7) | copy-start | bytes 1572868
  220.0 0.8 copy-start.13
  222.9 106.3 %reduce-scatter.5.cloned.1.call-start = ((), (), s32[]{:S(2)}) async-start(), calls=%async_computation.8 | async-start | bytes 7077888 | tf_op jit(solution)/shard_map/reduce_scatter | solution.py:149
  228.4 4.1 copy-start.1
  233.7 1.3 copy-start.5
  240.9 163.3 %reduce-scatter.9.cloned.1.call-start = ((), (), s32[]{:S(2)}) async-start(), calls=%async_computation.10 | async-start | bytes 9437184 | tf_op jit(solution)/shard_map/reduce_scatter | solution.py:151
  248.7 230.5 %reduce-scatter.11.cloned.1.call-start = ((), (), s32[]{:S(2)}) async-start(), calls=%async_computation.11 | async-start | bytes 9437184 | tf_op jit(solution)/shard_map/reduce_scatter | solution.py:152
  257.5 345.7 %all-reduce.4.cloned.1.call-start = ((), (), s32[]{:S(2)}) async-start(), calls=%async_computation.12 | async-start | bytes 6291456 | tf_op jit(solution)/shard_map/psum | solution.py:154
  479.3 6.7 %copy-start.2 = (bf16[2048,1024]{1,0:T(8,128)(2,1)S(1)}, bf16[2048,1024]{1,0:T(8,128)(2,1)}, u32[]{:S(2)}) copy-start(bf16[2048,1024]{1,0:T(8,128)(2,1)} %param.11) | copy-start | bytes 12582916
  479.3 10.9 %slice-start = ((s8[6291456]{0:T(1024)(128)(4,1)}), s8[4194304]{0:T(1024)(128)(4,1)S(1)}, s32[]{:S(2)}) async-start(s8[6291456]{0:T(1024)(128)(4,1)} %bitcast.94), calls=%async_computation.13 | async-start | bytes 8388608
  485.9 4.3 slice-start.1
  504.1 6.2 %copy-start.9 = (f32[256,1024]{1,0:T(8,128)S(1)}, f32[256,1024]{1,0:T(8,128)}, u32[]{:S(2)}) copy-start(f32[256,1024]{1,0:T(8,128)} %get-tuple-element.28) | copy-start | bytes 3145732
  603.2 5.6 copy-start.11
  603.2 6.9 %copy-start.15 = (bf16[128,1024]{1,0:T(8,128)(2,1)S(1)}, bf16[128,1024]{1,0:T(8,128)(2,1)}, u32[]{:S(2)}) copy-start(bf16[128,1024]{1,0:T(8,128)(2,1)} %get-tuple-element.17) | copy-start | bytes 786436
Sparse Core Ops, SparseCore 0:
  9.9 48.1 all-gather.4
  59.9 27.7 all-gather.6
  89.6 54.2 all-gather.8
  145.6 54.2 all-gather.10
  223.0 41.1 reduce-scatter.6
  267.4 61.7 reduce-scatter.4
  332.7 71.4 reduce-scatter.8
  407.7 71.5 reduce-scatter.10
  481.9 121.3 all-reduce.3

commit v2 on v1

--- a/solution.py
+++ b/solution.py
@@ -1,6 +1,10 @@
+import functools
+
 import jax
 import jax.numpy as jnp
 from jax import lax
+from jax.experimental import pallas as pl
+from jax.experimental.pallas import tpu as pltpu
 from jax.sharding import PartitionSpec as P
 
 D = 1024
@@ -60,7 +64,7 @@
     )
 
 
-def per_device(
+def general_device(
     hidden, cotangent, route_pos, route_doc, w_qkv, w_out, w_up, w_down, router, gain_one, gain_two
 ):
     positions = route_pos[0]
@@ -166,33 +170,555 @@
     )
 
 
+MESH = pl.DeviceIdType.MESH
+ANY = pl.ANY
+
+
+def flip(index, stride):
+    return index + stride - 2 * stride * ((index // stride) % 2)
+
+
+def places():
+    z = lax.axis_index("dp")
+    f = lax.axis_index("fsdp")
+    return z, f, flip(f, 1), flip(f, 2), flip(f, 4), flip(flip(f, 2), 4)
+
+
+def greet(peers):
+    barrier = pltpu.get_barrier_semaphore()
+    for peer in peers:
+        pl.semaphore_signal(barrier, inc=1, device_id=peer, device_id_type=MESH)
+    pl.semaphore_wait(barrier, len(peers))
+
+
+GATHER_KINDS = 13
+
+
+def gather_kernel(*refs):
+    shards, fulls, kept = refs[0:4], refs[4:8], refs[8:12]
+    kept_in, kept_out, send, recv = refs[12:16]
+    z, f, core, along_x, along_y, across = places()
+    pair = flip(z, 1)
+    at_core, at_x, at_y, at_z = (z, core), (z, along_x), (z, along_y), (pair, f)
+    greet((at_core, at_x, at_y, at_z))
+
+    def rows_of(w, origin, start, size):
+        rows = shards[w].shape[0]
+        return pl.ds(pl.multiple_of(origin * rows + start, 16), size)
+
+    def copy(w, kind, source, origin, start, size, peer):
+        return pltpu.make_async_remote_copy(
+            src_ref=source,
+            dst_ref=fulls[w].at[rows_of(w, origin, start, size)],
+            send_sem=send.at[w, kind],
+            recv_sem=recv.at[w, kind],
+            device_id=peer,
+            device_id_type=MESH,
+        )
+
+    def own(w, kind, start, size, peer):
+        source = shards[w].at[pl.ds(pl.multiple_of(start, 16), size)]
+        return copy(w, kind, source, f, start, size, peer)
+
+    def passed(w, kind, origin, start, size, peer):
+        return copy(w, kind, fulls[w].at[rows_of(w, origin, start, size)], origin, start, size, peer)
+
+    plan = []
+    for w in range(4):
+        rows = shards[w].shape[0]
+        half = rows // 2
+        even, odd = (z % 2) * half, (1 - z % 2) * half
+        plan.append(
+            [
+                own(w, 0, even, half, at_x),
+                own(w, 1, odd, half, at_y),
+                own(w, 2, 0, rows, at_core),
+                passed(w, 3, along_y, odd, half, at_x),
+                passed(w, 4, along_x, even, half, at_y),
+                passed(w, 5, along_x, even, half, at_z),
+                passed(w, 6, along_y, odd, half, at_z),
+                passed(w, 7, along_x, even, half, at_core),
+                passed(w, 8, along_y, odd, half, at_core),
+                passed(w, 9, across, odd, half, at_core),
+                passed(w, 10, across, even, half, at_core),
+                passed(w, 11, along_x, odd, half, at_core),
+                passed(w, 12, along_y, even, half, at_core),
+            ]
+        )
+
+    def first(w):
+        for kind in (0, 1, 2):
+            plan[w][kind].start()
+
+    def second(w):
+        plan[w][0].wait_recv()
+        for kind in (5, 4, 7):
+            plan[w][kind].start()
+        plan[w][1].wait_recv()
+        for kind in (6, 3, 8):
+            plan[w][kind].start()
+
+    def third(w):
+        for kind, onward in ((3, 9), (4, 10), (5, 11), (6, 12)):
+            plan[w][kind].wait_recv()
+            plan[w][onward].start()
+
+    loads = [pltpu.make_async_copy(shards[w], kept[w], kept_in.at[w]) for w in range(4)]
+    stores = [
+        pltpu.make_async_copy(kept[w], fulls[w].at[rows_of(w, f, 0, shards[w].shape[0])], kept_out.at[w])
+        for w in range(4)
+    ]
+    order = (1,0,2,3)
+    first(order[0])
+    first(order[1])
+    for w in range(4):
+        loads[w].start()
+    for w in range(4):
+        loads[w].wait()
+        stores[w].start()
+    second(order[0])
+    first(order[2])
+    second(order[1])
+    first(order[3])
+    third(order[0])
+    second(order[2])
+    third(order[1])
+    second(order[3])
+    third(order[2])
+    third(order[3])
+    for w in range(4):
+        stores[w].wait()
+        for kind in range(GATHER_KINDS):
+            if kind == 2 or kind >= 7:
+                plan[w][kind].wait_recv()
+            plan[w][kind].wait_send()
+
+
+def gather_weights(weights, parts):
+    return pl.pallas_call(
+        gather_kernel,
+        out_shape=[
+            jax.ShapeDtypeStruct((w.shape[0] * parts, w.shape[1]), w.dtype) for w in weights
+        ],
+        in_specs=[pl.BlockSpec(memory_space=ANY)] * 4,
+        out_specs=[pl.BlockSpec(memory_space=ANY)] * 4,
+        scratch_shapes=[pltpu.VMEM(w.shape, w.dtype) for w in weights]
+        + [
+            pltpu.SemaphoreType.DMA((4,)),
+            pltpu.SemaphoreType.DMA((4,)),
+            pltpu.SemaphoreType.DMA((4, GATHER_KINDS)),
+            pltpu.SemaphoreType.DMA((4, GATHER_KINDS)),
+        ],
+        compiler_params=pltpu.CompilerParams(
+            collective_id=1, has_side_effects=True, vmem_limit_bytes=60 * 1024 * 1024
+        ),
+        name="gather_weights",
+    )(*weights)
+
+
+CHUNKS = 12
+LEFTS = 7
+RIGHTS = 9
+BLOCK = 128
+WIDE = 1024
+LAST = 7
+
+
+def left_of(t):
+    return jnp.where(t < 4, t, jnp.where(t < 8, 4, jnp.where(t < 11, 5, 6)))
+
+
+def right_of(t):
+    return jnp.where(t < 4, 0, t - 3)
+
+
+def add_rows(target, sources, rows):
+    def step(i, carry):
+        at = pl.ds(pl.multiple_of(i * 16, 16), 16)
+        total = sources[0][at].astype(jnp.float32)
+        for source in sources[1:]:
+            total = total + source[at].astype(jnp.float32)
+        target[at] = total.astype(target.dtype)
+        return carry
+
+    lax.fori_loop(0, rows // 16, step, 0)
+
+
+def reduce_kernel(*refs):
+    activated, normed_mid, normed_in, attended, grad_mlp, grad_up_in, grad_packed, grad_attn = refs[:8]
+    small, sums, small_sums = refs[8:11]
+    (left, right, part, from_x, from_y, last_x, last_y, from_pair, from_far) = refs[11:20]
+    small_sent, small_got = refs[20:22]
+    (in_own, in_send, in_recv, rin_own, rin_send, rin_recv) = refs[22:28]
+    send, recv, small_send, small_recv = refs[28:32]
+
+    z, f, core, along_x, along_y, across = places()
+    pair, far = flip(z, 1), flip(z, 2)
+    at_core, at_x, at_y = (z, core), (z, along_x), (z, along_y)
+    at_pair, at_far = (pair, f), (far, f)
+    greet((at_core, at_x, at_y, at_pair, at_far))
+
+    rows = grad_mlp.shape[0]
+    mine = pl.ds(pl.multiple_of((f % 2) * rows, rows), rows)
+    half = BLOCK // 2
+    quarter = BLOCK // 4
+    top, bottom = pl.ds(0, half), pl.ds(half, half)
+
+    def left_source(i):
+        if i < 4:
+            return activated, 4 * BLOCK, i * BLOCK
+        return (normed_mid, normed_in, attended)[i - 4], BLOCK, 0
+
+    def right_source(i):
+        if i == 0:
+            return grad_mlp, 0
+        if i < 5:
+            return grad_up_in, (i - 1) * WIDE
+        if i < 8:
+            return grad_packed, (i - 5) * WIDE
+        return grad_attn, 0
+
+    def spread(index):
+        return (index, flip(index, 2), flip(index, 4), flip(flip(index, 2), 4))
+
+    def left_copies(i):
+        source, stride, offset = left_source(i)
+        here, there = [], []
+        for slot in range(4):
+            target = left.at[i, mine, pl.ds(slot * BLOCK, BLOCK)]
+            columns = [
+                pl.ds(pl.multiple_of(spread(index)[slot] * stride + offset, BLOCK), BLOCK)
+                for index in (f, core)
+            ]
+            here.append(
+                pltpu.make_async_copy(source.at[:, columns[0]], target, in_own.at[i, slot])
+            )
+            there.append(
+                pltpu.make_async_remote_copy(
+                    src_ref=source.at[:, columns[1]],
+                    dst_ref=target,
+                    send_sem=in_send.at[i, slot],
+                    recv_sem=in_recv.at[i, slot],
+                    device_id=at_core,
+                    device_id_type=MESH,
+                )
+            )
+        return here + there
+
+    def right_copies(i):
+        source, offset = right_source(i)
+        source = source.at[:, pl.ds(offset, WIDE)]
+        target = right.at[i, mine]
+        return [
+            pltpu.make_async_copy(source, target, rin_own.at[i]),
+            pltpu.make_async_remote_copy(
+                src_ref=source,
+                dst_ref=target,
+                send_sem=rin_send.at[i],
+                recv_sem=rin_recv.at[i],
+                device_id=at_core,
+                device_id_type=MESH,
+            ),
+        ]
+
+    lefts = [left_copies(i) for i in range(LEFTS)]
+    rights = [right_copies(i) for i in range(RIGHTS)]
+    new_left = {0: 0, 1: 1, 2: 2, 3: 3, 4: 4, 8: 5, 11: 6}
+    new_right = {0: 0, 4: 1, 5: 2, 6: 3, 7: 4, 8: 5, 9: 6, 10: 7, 11: 8}
+    for t in range(CHUNKS):
+        for copy in lefts[new_left[t]] if t in new_left else ():
+            copy.start()
+        for copy in rights[new_right[t]] if t in new_right else ():
+            copy.start()
+
+    def remote(t, kind, source, target, peer):
+        return pltpu.make_async_remote_copy(
+            src_ref=source,
+            dst_ref=target,
+            send_sem=send.at[t, kind],
+            recv_sem=recv.at[t, kind],
+            device_id=peer,
+            device_id_type=MESH,
+        )
+
+    keep = pl.multiple_of((z % 2) * half, half)
+    give = pl.multiple_of(half - keep, half)
+    keep_part = pl.multiple_of(keep + (z // 2) * quarter, quarter)
+    give_part = pl.multiple_of(keep + (1 - z // 2) * quarter, quarter)
+
+    def moved(t, kind):
+        source, target, peer = (
+            lambda: (part.at[t, 1, top], from_x.at[t, 0], at_x),
+            lambda: (part.at[t, 3, top], from_x.at[t, 1], at_x),
+            lambda: (part.at[t, 2, bottom], from_y.at[t, 0], at_y),
+            lambda: (part.at[t, 3, bottom], from_y.at[t, 1], at_y),
+            lambda: (part.at[t, 1, bottom], last_x.at[t], at_x),
+            lambda: (part.at[t, 2, top], last_y.at[t], at_y),
+            lambda: (part.at[t, 0, pl.ds(give, half)], from_pair.at[t], at_pair),
+            lambda: (part.at[t, 0, pl.ds(give_part, quarter)], from_far.at[t], at_far),
+            lambda: (sums.at[t, pl.ds(keep_part, quarter)],) * 2 + (at_far,),
+            lambda: (sums.at[t, pl.ds(keep, half)],) * 2 + (at_pair,),
+        )[kind]()
+        return remote(t, kind, source, target, peer)
+
+    def stage_product(t):
+        lhs = left[left_of(t)]
+        for column in range(0, WIDE, 256):
+            block = lax.dot_general(
+                lhs,
+                right[right_of(t), :, column : column + 256],
+                (((0,), (0,)), ((), ())),
+                preferred_element_type=jnp.float32,
+            ).astype(jnp.bfloat16)
+            for slot in range(4):
+                part[t, slot, :, column : column + 256] = block[slot * BLOCK : (slot + 1) * BLOCK]
+        for kind in (1, 3, 0, 2):
+            moved(t, kind).start()
+
+    def stage_turn(t):
+        moved(t, 1).wait_recv()
+        add_rows(part.at[t, 2, top], (part.at[t, 2, top], from_x.at[t, 1]), half)
+        moved(t, 5).start()
+        moved(t, 3).wait_recv()
+        add_rows(part.at[t, 1, bottom], (part.at[t, 1, bottom], from_y.at[t, 1]), half)
+        moved(t, 4).start()
+
+    def stage_plane(t):
+        moved(t, 0).wait_recv()
+        moved(t, 5).wait_recv()
+        add_rows(part.at[t, 0, top], (part.at[t, 0, top], from_x.at[t, 0], last_y.at[t]), half)
+        moved(t, 2).wait_recv()
+        moved(t, 4).wait_recv()
+        add_rows(
+            part.at[t, 0, bottom], (part.at[t, 0, bottom], from_y.at[t, 0], last_x.at[t]), half
+        )
+        moved(t, 6).start()
+
+    def stage_pair(t):
+        moved(t, 6).wait_recv()
+        target = part.at[t, 0, pl.ds(keep, half)]
+        add_rows(target, (target, from_pair.at[t]), half)
+        moved(t, 7).start()
+
+    def stage_far(t):
+        moved(t, 7).wait_recv()
+        add_rows(
+            sums.at[t, pl.ds(keep_part, quarter)],
+            (part.at[t, 0, pl.ds(keep_part, quarter)], from_far.at[t]),
+            quarter,
+        )
+        moved(t, 8).start()
+
+    def stage_back(t):
+        moved(t, 8).wait_recv()
+        moved(t, 8).wait_send()
+        moved(t, 9).start()
+
+    def stage_end(t):
+        moved(t, 9).wait_recv()
+        for kind in (0, 1, 2, 3, 4, 5, 6, 7, 9):
+            moved(t, kind).wait_send()
+
+    peers = (at_core, at_x, at_y, at_pair, at_far)
+
+    def small_copy(j):
+        return pltpu.make_async_remote_copy(
+            src_ref=small_sent.at[j],
+            dst_ref=small_got.at[j],
+            send_sem=small_send.at[j],
+            recv_sem=small_recv.at[j],
+            device_id=peers[j],
+            device_id_type=MESH,
+        )
+
+    small_sent[0] = small[...]
+    small_copy(0).start()
+    stages = (stage_turn, stage_plane, stage_pair, stage_far, stage_back, stage_end)
+
+    def tick(t, carry):
+        for when, i in new_left.items():
+
+            @pl.when(t == when)
+            def _(i=i):
+                for copy in lefts[i]:
+                    copy.wait()
+
+        for when, i in new_right.items():
+
+            @pl.when(t == when)
+            def _(i=i):
+                for copy in rights[i]:
+                    copy.wait()
+
+        @pl.when(t < CHUNKS)
+        def _():
+            stage_product(t)
+
+        for lag, stage in enumerate(stages, 1):
+
+            @pl.when((t >= lag) & (t < CHUNKS + lag))
+            def _(lag=lag, stage=stage):
+                stage(t - lag)
+
+        for j in range(5):
+
+            @pl.when(t == j)
+            def _(j=j):
+                small_copy(j).wait()
+                total = small_sent[j] + small_got[j]
+                if j < 4:
+                    small_sent[j + 1] = total
+                    small_copy(j + 1).start()
+                else:
+                    small_sums[...] = total
+
+        return carry
+
+    lax.fori_loop(0, CHUNKS + len(stages), tick, 0)
+
+
+def reduce_gradients(lefts, rights, small):
+    rows = lefts[0].shape[0]
+    bf16, dma = jnp.bfloat16, pltpu.SemaphoreType.DMA
+    return pl.pallas_call(
+        reduce_kernel,
+        out_shape=[
+            jax.ShapeDtypeStruct((CHUNKS, BLOCK, WIDE), bf16),
+            jax.ShapeDtypeStruct(small.shape, jnp.float32),
+        ],
+        in_specs=[pl.BlockSpec(memory_space=ANY)] * 8 + [pl.BlockSpec(memory_space=pltpu.VMEM)],
+        out_specs=[pl.BlockSpec(memory_space=pltpu.VMEM)] * 2,
+        scratch_shapes=[
+            pltpu.VMEM((LEFTS, 2 * rows, 4 * BLOCK), bf16),
+            pltpu.VMEM((RIGHTS, 2 * rows, WIDE), bf16),
+            pltpu.VMEM((CHUNKS, 4, BLOCK, WIDE), bf16),
+            pltpu.VMEM((CHUNKS, 2, BLOCK // 2, WIDE), bf16),
+            pltpu.VMEM((CHUNKS, 2, BLOCK // 2, WIDE), bf16),
+            pltpu.VMEM((CHUNKS, BLOCK // 2, WIDE), bf16),
+            pltpu.VMEM((CHUNKS, BLOCK // 2, WIDE), bf16),
+            pltpu.VMEM((CHUNKS, BLOCK // 2, WIDE), bf16),
+            pltpu.VMEM((CHUNKS, BLOCK // 4, WIDE), bf16),
+            pltpu.VMEM((5,) + small.shape, jnp.float32),
+            pltpu.VMEM((5,) + small.shape, jnp.float32),
+            dma((LEFTS, 4)),
+            dma((LEFTS, 4)),
+            dma((LEFTS, 4)),
+            dma((RIGHTS,)),
+            dma((RIGHTS,)),
+            dma((RIGHTS,)),
+            dma((CHUNKS, 10)),
+            dma((CHUNKS, 10)),
+            dma((5,)),
+            dma((5,)),
+        ],
+        compiler_params=pltpu.CompilerParams(
+            collective_id=2, has_side_effects=True, vmem_limit_bytes=60 * 1024 * 1024
+        ),
+        name="reduce_gradients",
+    )(*lefts, *rights, small)
+
+
+def put_rows(tokens, rows, positions):
+    hit = lax.broadcasted_iota(jnp.int32, (tokens.shape[0], positions.shape[0]), 0) == positions[None]
+    moved = jnp.dot(hit.astype(jnp.bfloat16), rows, preferred_element_type=jnp.float32)
+    return jnp.where(jnp.any(hit, axis=1, keepdims=True), moved.astype(jnp.bfloat16), tokens)
+
+
+def per_device(
+    hidden, cotangent, route_pos, route_doc, w_qkv, w_out, w_up, w_down, router, gain_one, gain_two
+):
+    positions = route_pos[0]
+    documents = route_doc[0]
+    live_mask = (documents < 2).astype(jnp.float32)[:, None]
+    weights = gather_weights((w_qkv, w_out, w_up, w_down), 8)
+    state = forward(hidden, positions, documents, weights, router, gain_one, gain_two)
+    full_qkv, full_out, full_up, full_down = weights
+    (
+        routed,
+        router_out,
+        normed_in,
+        heads,
+        prob_rows,
+        prob_low,
+        attended,
+        attn_out,
+        middle,
+        normed_mid,
+        up_in,
+        activated,
+        mlp_out,
+    ) = state
+    row_count = routed.shape[0]
+    branch_out = attn_out + mlp_out
+    added = live_mask * router_out[:, None] * branch_out
+    output = put_rows(hidden, (routed + added).astype(jnp.bfloat16), positions)
+    taken = cotangent[positions].astype(jnp.float32)
+    grad_add = live_mask * taken
+    grad_branch = grad_add * router_out[:, None]
+    grad_score = jnp.sum(grad_add * branch_out, axis=-1)
+    grad_mlp = grad_branch.astype(jnp.bfloat16)
+    grad_act = jnp.dot(grad_mlp, full_down.T, preferred_element_type=jnp.float32)
+    _, gelu_pull = jax.vjp(jax.nn.gelu, up_in)
+    grad_up_in = gelu_pull(grad_act)[0].astype(jnp.bfloat16)
+    grad_norm_mid = jnp.dot(grad_up_in, full_up.T, preferred_element_type=jnp.float32)
+    _, second_pull = jax.vjp(rms_scale, middle, gain_two)
+    grad_middle, grad_gain_two = second_pull(grad_norm_mid)
+    grad_attn = (grad_branch + grad_middle).astype(jnp.bfloat16)
+    grad_attended = jnp.dot(grad_attn, full_out.T, preferred_element_type=jnp.float32).astype(
+        jnp.bfloat16
+    )
+    grad_attended = grad_attended.reshape(row_count, HEADS, HEAD)
+    grad_prob = jnp.einsum(
+        "qhd,khd->hqk", grad_attended, heads[:, 2], preferred_element_type=jnp.float32
+    )
+    grad_value = jnp.einsum(
+        "hqk,qhd->khd", prob_low, grad_attended, preferred_element_type=jnp.float32
+    )
+    row_dot = jnp.sum(grad_prob * prob_rows, axis=-1, keepdims=True)
+    grad_scores = (prob_rows * (grad_prob - row_dot)).astype(jnp.bfloat16)
+    grad_query = (
+        jnp.einsum("hqk,khd->qhd", grad_scores, heads[:, 1], preferred_element_type=jnp.float32)
+        * 0.125
+    )
+    grad_key = (
+        jnp.einsum("hqk,qhd->khd", grad_scores, heads[:, 0], preferred_element_type=jnp.float32)
+        * 0.125
+    )
+    grad_packed = jnp.stack([grad_query, grad_key, grad_value], axis=1).reshape(row_count, 3 * D)
+    grad_packed = grad_packed.astype(jnp.bfloat16)
+    grad_norm_in = jnp.dot(grad_packed, full_qkv.T, preferred_element_type=jnp.float32)
+    _, first_pull = jax.vjp(rms_scale, routed, gain_one)
+    grad_routed, grad_gain_one = first_pull(grad_norm_in)
+    grad_routed = grad_routed + grad_middle + grad_score[:, None] * router[None, :]
+    grad_router = jnp.dot(grad_score, routed, precision=lax.Precision.HIGHEST)
+    grad_hidden = put_rows(cotangent, (taken + grad_routed).astype(jnp.bfloat16), positions)
+    small = jnp.stack([grad_router, grad_gain_one, grad_gain_two] + [jnp.zeros_like(grad_router)] * 5)
+    sums, small_sums = reduce_gradients(
+        (activated, normed_mid, normed_in, attended),
+        (grad_mlp, grad_up_in, grad_packed, grad_attn),
+        small,
+    )
+    wide = sums.astype(jnp.float32)
+    return (
+        output,
+        grad_hidden,
+        wide[8:11].transpose(1, 0, 2).reshape(w_qkv.shape),
+        wide[11],
+        wide[4:8].transpose(1, 0, 2).reshape(w_up.shape),
+        wide[:4].reshape(w_down.shape),
+        small_sums[0],
+        small_sums[1],
+        small_sums[2],
+    )
+
+
 def solution(mesh):
+    paired = dict(mesh.shape) == {"dp": 4, "fsdp": 8}
+    tokens, weights = P(("dp", "fsdp"), None), P("fsdp", None)
     return jax.shard_map(
-        per_device,
+        per_device if paired else general_device,
         mesh=mesh,
-        in_specs=(
-            P(("dp", "fsdp"), None),
-            P(("dp", "fsdp"), None),
-            P(("dp", "fsdp"), None),
-            P(("dp", "fsdp"), None),
-            P("fsdp", None),
-            P("fsdp", None),
-            P("fsdp", None),
-            P("fsdp", None),
-            P(),
-            P(),
-            P(),
-        ),
-        out_specs=(
-            P(("dp", "fsdp"), None),
-            P(("dp", "fsdp"), None),
-            P("fsdp", None),
-            P("fsdp", None),
-            P("fsdp", None),
-            P("fsdp", None),
-            P(),
-            P(),
-            P(),
-        ),
+        in_specs=(tokens,) * 4 + (weights,) * 4 + (P(),) * 3,
+        out_specs=(tokens,) * 2 + (weights,) * 4 + (P(),) * 3,
         check_vma=False,
     )

time: 623 us -> 334 us (0.54)
  waiting for transfers between devices: 416 us -> 0 us
  Pallas kernels: 0 us -> 230 us
  other arithmetic: 54.5 us -> 6.81 us
  blocking collectives: 41.2 us -> 0 us
  matrix products: 75.6 us -> 51 us
  local copies, waits for them, and re-layouts: 15.8 us -> 38.8 us
  between operations: 14.3 us -> 1.61 us
    pallas_call x0 -> x2, Pallas kernels: none -> 230 us  [the longest x1 147 us: reduce_gradients(): pl.pallas_call(reduce_kernel, out_shape=[jax.ShapeDtypeStruct((CHUNKS, BL...]
    reduce_scatter x4 -> x0, waiting for transfers between devices: 222 us -> none  [the longest x1 75 us: per_device(): lax.psum_scatter(grad_down.astype(jnp.bfloat16), 'fsdp', scatter_dimensio...]
    all_gather x4 -> x0, waiting for transfers between devices: 155 us -> none  [the longest x1 52.7 us: per_device(): lax.all_gather(w_up, 'fsdp', axis=0, tiled=True)]
    psum x1 -> x0, blocking collectives: 41.2 us -> none  [per_device(): lax.psum((grad_router, grad_gain_one, grad_gain_two), ('dp', 'fsdp'))]
    psum x1 -> x0, waiting for transfers between devices: 36 us -> none  [per_device(): lax.psum((shard_sums[0], shard_sums[1], shard_sums[2], shard_sums[3]), 'dp')]
    convert_element_type x8 -> x3, other arithmetic: 31 us -> 3.14 us  [the longest x1 2.64 us: per_device(): wide = sums.astype(jnp.float32)]
    scatter-add x2 -> x0, other arithmetic: 20.2 us -> none  [the longest x1 10.9 us: per_device(): cotangent.astype(jnp.float32).at[positions].add(grad_routed)]
    dot_general x4 -> x2, matrix products: 22.7 us -> 8.88 us  [put_rows(): jnp.dot(hit.astype(jnp.bfloat16), rows, preferred_element_type=jnp.float32)]
  transfers between devices with their start and end apart: 9 -> 0, of which waited for: 9 -> 0; matrix products, arithmetic and copies ran while one was open for 18% -> 0% of each run, Pallas kernels for 0% -> 0%
where the time goes in v2:
time: 334 us; the launch traced here: 328 us
  Pallas kernels  230 us (69%)
  matrix products  51 us (15%)
  local copies, waits for them, and re-layouts  38.8 us (12%)
  other arithmetic  6.81 us (2%)
    pallas_call x1, Pallas kernels, reduce_gradients(): pl.pallas_call(reduce_kernel, out_shape=[jax.ShapeDtypeStruct((CHUNKS, BL...  147 us
    pallas_call x1, Pallas kernels, gather_weights(): pl.pallas_call(gather_kernel, out_shape=[jax.ShapeDtypeStruct((w.shape[0]...  82.9 us
    unnamed x60, local copies, waits for them, and re-layouts  9.34 us
    dot_general x2, matrix products, put_rows(): jnp.dot(hit.astype(jnp.bfloat16), rows, preferred_element_type=jnp.float32)  8.88 us
    dot_general x1, matrix products, forward(): up_in = jnp.dot(normed_mid, full_up, preferred_element_type=jnp.float32)  8.62 us
    dot_general x1, matrix products, per_device(): jnp.dot(grad_up_in, full_up.T, preferred_element_type=jnp.float32)  7.7 us

profile of v2, /device:TPU:0, one launch (start us, length us, event | category | flops | bytes accessed | tf_op | source)
XLA Modules:
  0.0 328.3 jit_solution(6020332306426570400)
XLA Ops:
  0.7 0.7 compare_select_fusion
  1.4 0.0 copy-start.21
  1.4 4.3 %gather_fusion = bf16[256,1024]{1,0:T(8,128)(2,1)S(1)} fusion(bf16[2048,1024]{1,0:T(8,128)(2,1)} %param.11, s32[1024]{0:T(1024)S(1)} %pad_clamp_fusion), kind=kCustom, calls=%fused_computation | custom fusion | bytes 1049600 | tf_op jit(solution)/shard_map/gather | solution.py:24
  5.7 0.2 fusion.28
  5.9 0.5 fusion.53
  6.4 4.3 %gather_fusion.1 = bf16[256,1024]{1,0:T(8,128)(2,1)S(1)} fusion(bf16[2048,1024]{1,0:T(8,128)(2,1)} %param.12, s32[1024]{0:T(1024)S(1)} %pad_clamp_fusion), kind=kCustom, calls=%fused_computation.1 | custom fusion | bytes 1049600 | tf_op jit(solution)/shard_map/gather | solution.py:655
  10.7 0.3 fusion.20
  11.1 82.9 %gather_weights.1 = (bf16[1024,3072]{1,0:T(8,128)(2,1)}, bf16[1024,1024]{1,0:T(8,128)(2,1)}, bf16[1024,4096]{1,0:T(8,128)(2,1)}, bf16[4096,1024]{1,0:T(8,128)(2,1)}) custom-call(bf16[128,3072]{1,0:T(8,128)(2,1)} %refs_0_.1, bf16[128,1024]{1,0:T(8,128)(2,1)} %refs_1_.1, bf16[128,4096]{1,0:T(8,128)(2,1)} %refs_2_.1, bf16[512,1024]{1,0:T(8,128)(2,1)} %refs_3_.1), custom_call_target="tpu_custom_call" | custom-call | tf_op jit(solution)/shard_map/gather_weights/pallas_call | solution.py:298
  94.0 0.0 copy-start.19
  94.0 5.7 %convolution_convert_fusion = bf16[256,3072]{1,0:T(8,128)(2,1)} fusion(bf16[256,1024]{1,0:T(8,128)(2,1)S(1)} %get-tuple-element.60.refs_2_, bf16[1024,3072]{1,0:T(8,128)(2,1)} %get-tuple-element.15), kind=kOutput, calls=%fused_computation.19 | convolution fusion | flops 1611399168 | bytes 8388608 | tf_op jit(solution)/shard_map/dot_general | solution.py:28
  99.7 1.9 copy.43
  101.6 0.1 compare_and_fusion
  101.7 0.0 slice-start
  101.8 0.8 fusion.7
  102.6 0.0 copy-start
  102.6 0.9 exponential_reduce_fusion
  103.5 0.0 copy-start.22
  103.5 0.0 slice-start.1
  103.5 1.1 convolution_convert_fusion.3
  104.6 0.1 copy-done
  104.7 0.8 copy-done.12
  105.5 0.8 copy-done.11
  106.3 0.8 multiply_reduce_fusion.3
  107.1 0.2 multiply_convert_fusion.2.refs_1_
  107.4 0.4 slice-done.1
  107.8 2.4 fusion.54
  110.2 8.6 %fusion.6 = (bf16[256,4096]{1,0:T(8,128)(2,1)S(1)}, bf16[256,4096]{1,0:T(8,128)(2,1)S(1)}) fusion(f32[256,4096]{1,0:T(8,128)S(1)} %fusion.54, bf16[256,1024]{1,0:T(8,128)(2,1)S(1)} %multiply_convert_fusion.2.refs_1_, bf16[1024,4096]{1,0:T(8,128)(2,1)} %get-tuple-element.17), kind=kOutput, calls=%fused_computation.10 | convolution fusion | flops 2170552320 | bytes 17301504 | tf_op jit(solution)/shard_map/dot_general | solution.py:47
  118.8 0.0 copy-start.15
  118.8 0.0 copy-start.16
  118.8 7.7 %multiply_reduce_fusion.1 = (f32[1024]{0:T(1024)S(1)}, f32[256]{0:T(256)S(1)}, f32[256,1024]{1,0:T(8,128)S(1)}) fusion(f32[256]{0:T(256)S(1)} %fusion.46, f32[256,1024]{1,0:T(8,128)S(1)} %get-tuple-element.53, bf16[256,1024]{1,0:T(8,128)(2,1)S(1)} %gather_fusion, f32[1024]{0:T(1024)S(1)} %copy-done.22, bf16[256,4096]{1,0:T(8,128)(2,1)S(1)} %get-tuple-element.43.refs_5_, ...), kind=kOutput, calls=%fused_computation.64 | convolution fusion | flops 2149579520 | bytes 13117440 | tf_op jit(solution)/shard_map/dot_general | solution.py:663
  126.6 3.7 %fusion.24 = (f32[256]{0:T(256)S(1)}, bf16[256,1024]{1,0:T(8,128)(2,1)S(1)}, f32[256,1024]{1,0:T(8,128)}) fusion(bf16[256,1024]{1,0:T(8,128)(2,1)S(1)} %gather_fusion.1, f32[256]{0:T(256)S(1)} %fusion.47, f32[256]{0:T(256)S(1)} %multiply_multiply_fusion.3, f32[256,1024]{1,0:T(8,128)S(1)} %get-tuple-element.53, bf16[256,1024]{1,0:T(8,128)(2,1)S(1)} %gather_fusion, ...), kind=kOutput, calls=%fused_computation.57 | convolution fusion | flops 2151415552 | bytes 15213568 | tf_op jit(solution)/shard_map/dot_general | solution.py:49
  130.2 1.5 convolution_convert_fusion.2
  131.8 1.2 copy.45
  133.0 0.0 copy-start.1
  133.0 3.8 %multiply_reduce_fusion = (f32[16,256]{1,0:T(8,128)S(1)}, f32[16,256,256]{1,2,0:T(8,128)S(1)}) fusion(f32[16,256,256]{1,2,0:T(8,128)} %copy-done, f32[16,256]{1,0:T(8,128)S(1)} %log_add_fusion, pred[256,256]{0,1:T(8,128)(4,1)S(1)} %compare_and_fusion, bf16[256,16,64]{0,2,1:T(8,128)(2,1)S(1)} %bitcast.94, bf16[256,3,16,64]{0,3,2,1:T(8,128)(2,1)S(1)} %bitcast.85), kind=kOutput, calls=%fused_computation.13 | convolution fusion | flops 139456512 | bytes 9535488 | tf_op jit(solution)/shard_map/qhd,khd->hqk/dot_general | solution.py:671
  136.8 1.2 multiply_convert_fusion
  138.0 0.5 fusion.17
  138.5 0.0 slice-start.2
  138.5 0.8 fusion.16
  139.3 1.1 fusion.18
  140.4 0.2 pad_maximum_fusion
  140.6 1.1 slice-done.3
  141.6 2.9 fusion.23
  144.6 0.3 fusion.55
  144.9 0.7 stack.33.refs_8_
  145.5 1.7 copy.50.refs_6_
  147.3 1.0 copy.49.refs_3_
  148.3 147.1 %reduce_gradients.1 = (bf16[12,128,1024]{2,1,0:T(8,128)(2,1)}, f32[8,1024]{1,0:T(8,128)}) custom-call(bf16[256,4096]{1,0:T(8,128)(2,1)} %copy-done.16, bf16[256,1024]{1,0:T(8,128)(2,1)} %copy-done.14, bf16[256,1024]{1,0:T(8,128)(2,1)} %copy-done.10, bf16[256,1024]{1,0:T(8,128)(2,1)} %copy.49.refs_3_, bf16[256,1024]{1,0:T(8,128)(2,1)} %copy-done.9, ...), custom_call_target="tpu_custom_call" | custom-call | tf_op jit(solution)/shard_map/reduce_gradients/pallas_call | solution.py:583
  295.4 2.6 convert_element_type.91
  298.1 2.6 copy-done.2
  300.7 1.6 slice_bitcast_fusion
  302.3 1.9 copy.52
  304.2 1.8 copy.54
  306.0 2.7 slice_bitcast_fusion.1
  308.7 1.9 copy.51
  310.6 1.6 copy.53
  312.2 2.0 slice_bitcast_fusion.2
  314.3 2.8 slice.53
  317.1 1.5 fusion.52
  318.5 0.4 fusion.9
  318.9 0.0 copy-start.4
  318.9 0.0 copy-start.23
  318.9 5.8 %convert_select_fusion = bf16[2048,1024]{1,0:T(8,128)(2,1)} fusion(bf16[2048,1024]{1,0:T(8,128)(2,1)S(1)} %copy-done.3, pred[2048]{0:T(1024)(128)(4,1)S(1)} %fusion.9, s32[256]{0:T(256)S(1)} %bitcast.105, bf16[256,1024]{1,0:T(8,128)(2,1)S(1)} %copy-done.8, bf16[256,1024]{1,0:T(8,128)(2,1)S(1)} %gather_fusion, f32[256,1024]{1,0:T(8,128)} %get-tuple-element.58, ...), kind=kOutput, calls=%fused_computation.11 | convolution fusion | flops 1083179008 | bytes 12603392 | tf_op jit(solution)/shard_map/dot_general | solution.py:623
  324.8 3.1 convert_select_fusion.1
  (52 shorter events, 0.1 us)
Async XLA Ops:
  0.6 5.2 %copy-start.20 = (f32[1024]{0:T(1024)S(1)}, f32[1024]{0:T(1024)}, u32[]{:S(2)}) copy-start(f32[1024]{0:T(1024)} %param.19) | copy-start | bytes 12292
  1.3 9.4 %copy-start.18 = (s32[1,256]{1,0:T(1,128)S(1)}, s32[1,256]{1,0:T(1,128)}, u32[]{:S(2)}) copy-start(s32[1,256]{1,0:T(1,128)} %param.14) | copy-start | bytes 3076
  1.4 9.4 %copy-start.21 = (f32[1024]{0:T(1024)S(1)}, f32[1024]{0:T(1024)}, u32[]{:S(2)}) copy-start(f32[1024]{0:T(1024)} %param.20) | copy-start | bytes 12292
  10.7 115.9 %copy-start.7 = (bf16[256,1024]{1,0:T(8,128)(2,1)}, bf16[256,1024]{1,0:T(8,128)(2,1)S(1)}, u32[]{:S(2)}) copy-start(bf16[256,1024]{1,0:T(8,128)(2,1)S(1)} %gather_fusion.1) | copy-start | bytes 1572868
  11.0 82.9 %copy-start.10 = (bf16[256,1024]{1,0:T(8,128)(2,1)}, bf16[256,1024]{1,0:T(8,128)(2,1)S(1)}, u32[]{:S(2)}) copy-start(bf16[256,1024]{1,0:T(8,128)(2,1)S(1)} %get-tuple-element.60.refs_2_) | copy-start | bytes 1572868
  11.1 96.3 %copy-start.9 = (bf16[256,1024]{1,0:T(8,128)(2,1)}, bf16[256,1024]{1,0:T(8,128)(2,1)S(1)}, u32[]{:S(2)}) copy-start(bf16[256,1024]{1,0:T(8,128)(2,1)S(1)} %get-tuple-element.59.refs_4_) | copy-start | bytes 1572868
  94.0 7.6 %copy-start.19 = (s32[1,256]{1,0:T(1,128)S(1)}, s32[1,256]{1,0:T(1,128)}, u32[]{:S(2)}) copy-start(s32[1,256]{1,0:T(1,128)} %param.13) | copy-start | bytes 3076
  101.7 5.6 %slice-start = ((s8[8388608]{0:T(1024)(128)(4,1)}), s8[4194304]{0:T(1024)(128)(4,1)S(1)}, s32[]{:S(2)}) async-start(s8[8388608]{0:T(1024)(128)(4,1)} %bitcast.115), calls=%async_computation | async-start | bytes 8388608
  102.6 2.1 copy-start
  103.5 2.8 copy-start.11
  103.5 3.6 %copy-start.22 = (f32[1024]{0:T(1024)S(1)}, f32[1024]{0:T(1024)}, u32[]{:S(2)}) copy-start(f32[1024]{0:T(1024)} %param.21) | copy-start | bytes 12292
  103.5 4.2 %slice-start.1 = ((s8[8388608]{0:T(1024)(128)(4,1)}), s8[4194304]{0:T(1024)(128)(4,1)S(1)}, s32[]{:S(2)}) async-start(s8[8388608]{0:T(1024)(128)(4,1)} %bitcast.115), calls=%async_computation.1 | async-start | bytes 8388608
  104.7 0.8 copy-start.12
  107.1 19.4 %copy-start.5 = (f32[256,1024]{1,0:T(8,128)}, f32[256,1024]{1,0:T(8,128)S(1)}, u32[]{:S(2)}) copy-start(f32[256,1024]{1,0:T(8,128)S(1)} %get-tuple-element.53) | copy-start | bytes 3145732
  107.3 2.8 copy-start.14
  118.8 7.7 %copy-start.15 = (bf16[256,4096]{1,0:T(8,128)(2,1)}, bf16[256,4096]{1,0:T(8,128)(2,1)S(1)}, u32[]{:S(2)}) copy-start(bf16[256,4096]{1,0:T(8,128)(2,1)S(1)} %get-tuple-element.43.refs_5_) | copy-start | bytes 6291460
  118.8 7.8 %copy-start.16 = (bf16[256,4096]{1,0:T(8,128)(2,1)}, bf16[256,4096]{1,0:T(8,128)(2,1)S(1)}, u32[]{:S(2)}) copy-start(bf16[256,4096]{1,0:T(8,128)(2,1)S(1)} %get-tuple-element.44.refs_0_) | copy-start | bytes 6291460
  126.5 3.7 %copy-start.24 = (f32[256,1024]{1,0:T(8,128)}, f32[256,1024]{1,0:T(8,128)S(1)}, u32[]{:S(2)}) copy-start(f32[256,1024]{1,0:T(8,128)S(1)} %get-tuple-element.54) | copy-start | bytes 3145732
  130.2 6.6 %copy-start.17 = (bf16[256,1024]{1,0:T(8,128)(2,1)}, bf16[256,1024]{1,0:T(8,128)(2,1)S(1)}, u32[]{:S(2)}) copy-start(bf16[256,1024]{1,0:T(8,128)(2,1)S(1)} %get-tuple-element.46.refs_7_) | copy-start | bytes 1572868
  133.0 3.8 %copy-start.1 = (f32[16,256,256]{1,2,0:T(8,128)S(1)}, f32[16,256,256]{1,2,0:T(8,128)}, u32[]{:S(2)}) copy-start(f32[16,256,256]{1,2,0:T(8,128)} %copy-done) | copy-start | bytes 12582916
  138.5 2.0 slice-start.2
  139.3 2.4 slice-start.3
  141.6 5.6 %copy-start.13 = (bf16[16,64,256]{2,1,0:T(8,128)(2,1)S(1)}, bf16[16,64,256]{2,1,0:T(8,128)(2,1)}, u32[]{:S(2)}) copy-start(bf16[16,64,256]{2,1,0:T(8,128)(2,1)} %copy-done.12) | copy-start | bytes 1572868
  298.0 2.7 copy-start.2
  310.6 8.3 %copy-start.6 = (f32[256,1024]{1,0:T(8,128)S(1)}, f32[256,1024]{1,0:T(8,128)}, u32[]{:S(2)}) copy-start(f32[256,1024]{1,0:T(8,128)} %copy-done.5) | copy-start | bytes 3145732
  312.2 6.7 %copy-start.3 = (bf16[2048,1024]{1,0:T(8,128)(2,1)S(1)}, bf16[2048,1024]{1,0:T(8,128)(2,1)}, u32[]{:S(2)}) copy-start(bf16[2048,1024]{1,0:T(8,128)(2,1)} %param.12) | copy-start | bytes 12582916
  312.2 6.7 %copy-start.8 = (bf16[256,1024]{1,0:T(8,128)(2,1)S(1)}, bf16[256,1024]{1,0:T(8,128)(2,1)}, u32[]{:S(2)}) copy-start(bf16[256,1024]{1,0:T(8,128)(2,1)} %copy-done.7) | copy-start | bytes 1572868
  318.9 5.8 %copy-start.4 = (bf16[2048,1024]{1,0:T(8,128)(2,1)S(1)}, bf16[2048,1024]{1,0:T(8,128)(2,1)}, u32[]{:S(2)}) copy-start(bf16[2048,1024]{1,0:T(8,128)(2,1)} %param.11) | copy-start | bytes 12582916
  318.9 5.8 %copy-start.23 = (f32[256,1024]{1,0:T(8,128)S(1)}, f32[256,1024]{1,0:T(8,128)}, u32[]{:S(2)}) copy-start(f32[256,1024]{1,0:T(8,128)} %get-tuple-element.55) | copy-start | bytes 3145732

commit v3 on v2

--- a/solution.py
+++ b/solution.py
@@ -316,20 +316,22 @@
     )(*weights)
 
 
-CHUNKS = 12
+CHUNKS = 24
+LAGS = (1, 2, 3, 4, 5, 6)
 LEFTS = 7
 RIGHTS = 9
 BLOCK = 128
-WIDE = 1024
+WIDE = 512
+FULL = 1024
 LAST = 7
 
 
 def left_of(t):
-    return jnp.where(t < 4, t, jnp.where(t < 8, 4, jnp.where(t < 11, 5, 6)))
+    return jnp.where(t < 8, t // 2, jnp.where(t < 16, 4, jnp.where(t < 22, 5, 6)))
 
 
 def right_of(t):
-    return jnp.where(t < 4, 0, t - 3)
+    return jnp.where(t < 8, 0, t // 2 - 3)
 
 
 def add_rows(target, sources, rows):
@@ -346,14 +348,17 @@
 
 def reduce_kernel(*refs):
     activated, normed_mid, normed_in, attended, grad_mlp, grad_up_in, grad_packed, grad_attn = refs[:8]
-    small, sums, small_sums = refs[8:11]
-    (left, right, part, from_x, from_y, last_x, last_y, from_pair, from_far) = refs[11:20]
-    small_sent, small_got = refs[20:22]
-    (in_own, in_send, in_recv, rin_own, rin_send, rin_recv) = refs[22:28]
-    send, recv, small_send, small_recv = refs[28:32]
+    small, out_down, out_up, out_qkv, out_out, small_sums = refs[8:14]
+    sums, stored = refs[35:37]
+    (left, right, part, from_x, from_y, last_x, last_y, from_pair, from_far) = refs[14:23]
+    small_sent, small_got = refs[23:25]
+    (in_own, in_send, in_recv, rin_own, rin_send, rin_recv) = refs[25:31]
+    send, recv, small_send, small_recv = refs[31:35]
 
     z, f, core, along_x, along_y, across = places()
-    pair, far = flip(z, 1), flip(z, 2)
+    pair, far = flip(z, 1), 3 - z
+    inner = (z == 1) | (z == 2)
+    outer = (z == 0) | (z == 3)
     at_core, at_x, at_y = (z, core), (z, along_x), (z, along_y)
     at_pair, at_far = (pair, f), (far, f)
     greet((at_core, at_x, at_y, at_pair, at_far))
@@ -361,7 +366,6 @@
     rows = grad_mlp.shape[0]
     mine = pl.ds(pl.multiple_of((f % 2) * rows, rows), rows)
     half = BLOCK // 2
-    quarter = BLOCK // 4
     top, bottom = pl.ds(0, half), pl.ds(half, half)
 
     def left_source(i):
@@ -373,9 +377,9 @@
         if i == 0:
             return grad_mlp, 0
         if i < 5:
-            return grad_up_in, (i - 1) * WIDE
+            return grad_up_in, (i - 1) * FULL
         if i < 8:
-            return grad_packed, (i - 5) * WIDE
+            return grad_packed, (i - 5) * FULL
         return grad_attn, 0
 
     def spread(index):
@@ -407,7 +411,7 @@
 
     def right_copies(i):
         source, offset = right_source(i)
-        source = source.at[:, pl.ds(offset, WIDE)]
+        source = source.at[:, pl.ds(offset, FULL)]
         target = right.at[i, mine]
         return [
             pltpu.make_async_copy(source, target, rin_own.at[i]),
@@ -423,8 +427,8 @@
 
     lefts = [left_copies(i) for i in range(LEFTS)]
     rights = [right_copies(i) for i in range(RIGHTS)]
-    new_left = {0: 0, 1: 1, 2: 2, 3: 3, 4: 4, 8: 5, 11: 6}
-    new_right = {0: 0, 4: 1, 5: 2, 6: 3, 7: 4, 8: 5, 9: 6, 10: 7, 11: 8}
+    new_left = {0: 0, 2: 1, 4: 2, 6: 3, 8: 4, 16: 5, 22: 6}
+    new_right = {0: 0, 8: 1, 10: 2, 12: 3, 14: 4, 16: 5, 18: 6, 20: 7, 22: 8}
     for t in range(CHUNKS):
         for copy in lefts[new_left[t]] if t in new_left else ():
             copy.start()
@@ -441,11 +445,6 @@
             device_id_type=MESH,
         )
 
-    keep = pl.multiple_of((z % 2) * half, half)
-    give = pl.multiple_of(half - keep, half)
-    keep_part = pl.multiple_of(keep + (z // 2) * quarter, quarter)
-    give_part = pl.multiple_of(keep + (1 - z // 2) * quarter, quarter)
-
     def moved(t, kind):
         source, target, peer = (
             lambda: (part.at[t, 1, top], from_x.at[t, 0], at_x),
@@ -454,10 +453,9 @@
             lambda: (part.at[t, 3, bottom], from_y.at[t, 1], at_y),
             lambda: (part.at[t, 1, bottom], last_x.at[t], at_x),
             lambda: (part.at[t, 2, top], last_y.at[t], at_y),
-            lambda: (part.at[t, 0, pl.ds(give, half)], from_pair.at[t], at_pair),
-            lambda: (part.at[t, 0, pl.ds(give_part, quarter)], from_far.at[t], at_far),
-            lambda: (sums.at[t, pl.ds(keep_part, quarter)],) * 2 + (at_far,),
-            lambda: (sums.at[t, pl.ds(keep, half)],) * 2 + (at_pair,),
+            lambda: (part.at[t, 0], from_pair.at[t], at_pair),
+            lambda: (part.at[t, 0], from_far.at[t], at_far),
+            lambda: (sums.at[t], sums.at[t], at_pair),
         )[kind]()
         return remote(t, kind, source, target, peer)
 
@@ -466,7 +464,7 @@
         for column in range(0, WIDE, 256):
             block = lax.dot_general(
                 lhs,
-                right[right_of(t), :, column : column + 256],
+                right[right_of(t), :, pl.ds(pl.multiple_of((t % 2) * WIDE + column, 256), 256)],
                 (((0,), (0,)), ((), ())),
                 preferred_element_type=jnp.float32,
             ).astype(jnp.bfloat16)
@@ -492,32 +490,59 @@
         add_rows(
             part.at[t, 0, bottom], (part.at[t, 0, bottom], from_y.at[t, 0], last_x.at[t]), half
         )
-        moved(t, 6).start()
+
+        @pl.when(outer)
+        def _():
+            moved(t, 6).start()
 
     def stage_pair(t):
-        moved(t, 6).wait_recv()
-        target = part.at[t, 0, pl.ds(keep, half)]
-        add_rows(target, (target, from_pair.at[t]), half)
-        moved(t, 7).start()
+        @pl.when(inner)
+        def _():
+            moved(t, 6).wait_recv()
+            add_rows(part.at[t, 0], (part.at[t, 0], from_pair.at[t]), BLOCK)
+            moved(t, 7).start()
 
     def stage_far(t):
-        moved(t, 7).wait_recv()
-        add_rows(
-            sums.at[t, pl.ds(keep_part, quarter)],
-            (part.at[t, 0, pl.ds(keep_part, quarter)], from_far.at[t]),
-            quarter,
-        )
-        moved(t, 8).start()
-
-    def stage_back(t):
-        moved(t, 8).wait_recv()
-        moved(t, 8).wait_send()
-        moved(t, 9).start()
+        @pl.when(inner)
+        def _():
+            moved(t, 7).wait_recv()
+            add_rows(sums.at[t], (part.at[t, 0], from_far.at[t]), BLOCK)
+            moved(t, 8).start()
 
     def stage_end(t):
-        moved(t, 9).wait_recv()
-        for kind in (0, 1, 2, 3, 4, 5, 6, 7, 9):
+        @pl.when(inner)
+        def _():
+            moved(t, 7).wait_send()
+            moved(t, 8).wait_send()
+
+        @pl.when(outer)
+        def _():
+            moved(t, 6).wait_send()
+            moved(t, 8).wait_recv()
+
+        for kind in range(6):
             moved(t, kind).wait_send()
+
+        store(t, True)
+
+    def store(t, begin):
+        for low, high, target in (
+            (0, 8, lambda i: out_down.at[pl.ds(pl.multiple_of(i // 2 * BLOCK, BLOCK), BLOCK), columns(i % 2)]),
+            (8, 16, lambda i: out_up.at[:, columns(i)]),
+            (16, 22, lambda i: out_qkv.at[:, columns(i)]),
+            (22, 24, lambda i: out_out.at[:, columns(i)]),
+        ):
+
+            @pl.when((t >= low) & (t < high))
+            def _(low=low, target=target):
+                copy = pltpu.make_async_copy(sums.at[t], target(t - low), stored.at[t])
+                copy.start() if begin else copy.wait()
+
+    def columns(i):
+        return pl.ds(pl.multiple_of(i * WIDE, WIDE), WIDE)
+
+    def stage_stored(t):
+        store(t, False)
 
     peers = (at_core, at_x, at_y, at_pair, at_far)
 
@@ -533,7 +558,7 @@
 
     small_sent[0] = small[...]
     small_copy(0).start()
-    stages = (stage_turn, stage_plane, stage_pair, stage_far, stage_back, stage_end)
+    stages = (stage_turn, stage_plane, stage_pair, stage_far, stage_end, stage_stored)
 
     def tick(t, carry):
         for when, i in new_left.items():
@@ -554,7 +579,7 @@
         def _():
             stage_product(t)
 
-        for lag, stage in enumerate(stages, 1):
+        for lag, stage in zip(LAGS, stages):
 
             @pl.when((t >= lag) & (t < CHUNKS + lag))
             def _(lag=lag, stage=stage):
@@ -574,7 +599,7 @@
 
         return carry
 
-    lax.fori_loop(0, CHUNKS + len(stages), tick, 0)
+    lax.fori_loop(0, CHUNKS + LAGS[-1], tick, 0)
 
 
 def reduce_gradients(lefts, rights, small):
@@ -583,21 +608,24 @@
     return pl.pallas_call(
         reduce_kernel,
         out_shape=[
-            jax.ShapeDtypeStruct((CHUNKS, BLOCK, WIDE), bf16),
+            jax.ShapeDtypeStruct((4 * BLOCK, FULL), bf16),
+            jax.ShapeDtypeStruct((BLOCK, 4 * FULL), bf16),
+            jax.ShapeDtypeStruct((BLOCK, 3 * FULL), bf16),
+            jax.ShapeDtypeStruct((BLOCK, FULL), bf16),
             jax.ShapeDtypeStruct(small.shape, jnp.float32),
         ],
         in_specs=[pl.BlockSpec(memory_space=ANY)] * 8 + [pl.BlockSpec(memory_space=pltpu.VMEM)],
-        out_specs=[pl.BlockSpec(memory_space=pltpu.VMEM)] * 2,
+        out_specs=[pl.BlockSpec(memory_space=ANY)] * 4 + [pl.BlockSpec(memory_space=pltpu.VMEM)],
         scratch_shapes=[
             pltpu.VMEM((LEFTS, 2 * rows, 4 * BLOCK), bf16),
-            pltpu.VMEM((RIGHTS, 2 * rows, WIDE), bf16),
+            pltpu.VMEM((RIGHTS, 2 * rows, FULL), bf16),
             pltpu.VMEM((CHUNKS, 4, BLOCK, WIDE), bf16),
             pltpu.VMEM((CHUNKS, 2, BLOCK // 2, WIDE), bf16),
             pltpu.VMEM((CHUNKS, 2, BLOCK // 2, WIDE), bf16),
             pltpu.VMEM((CHUNKS, BLOCK // 2, WIDE), bf16),
             pltpu.VMEM((CHUNKS, BLOCK // 2, WIDE), bf16),
-            pltpu.VMEM((CHUNKS, BLOCK // 2, WIDE), bf16),
-            pltpu.VMEM((CHUNKS, BLOCK // 4, WIDE), bf16),
+            pltpu.VMEM((CHUNKS, BLOCK, WIDE), bf16),
+            pltpu.VMEM((CHUNKS, BLOCK, WIDE), bf16),
             pltpu.VMEM((5,) + small.shape, jnp.float32),
             pltpu.VMEM((5,) + small.shape, jnp.float32),
             dma((LEFTS, 4)),
@@ -606,10 +634,12 @@
             dma((RIGHTS,)),
             dma((RIGHTS,)),
             dma((RIGHTS,)),
-            dma((CHUNKS, 10)),
-            dma((CHUNKS, 10)),
+            dma((CHUNKS, 9)),
+            dma((CHUNKS, 9)),
             dma((5,)),
             dma((5,)),
+            pltpu.VMEM((CHUNKS, BLOCK, WIDE), bf16),
+            dma((CHUNKS,)),
         ],
         compiler_params=pltpu.CompilerParams(
             collective_id=2, has_side_effects=True, vmem_limit_bytes=60 * 1024 * 1024
@@ -693,19 +723,19 @@
     grad_router = jnp.dot(grad_score, routed, precision=lax.Precision.HIGHEST)
     grad_hidden = put_rows(cotangent, (taken + grad_routed).astype(jnp.bfloat16), positions)
     small = jnp.stack([grad_router, grad_gain_one, grad_gain_two] + [jnp.zeros_like(grad_router)] * 5)
-    sums, small_sums = reduce_gradients(
+    *sums, small_sums = reduce_gradients(
         (activated, normed_mid, normed_in, attended),
         (grad_mlp, grad_up_in, grad_packed, grad_attn),
         small,
     )
-    wide = sums.astype(jnp.float32)
+    sum_down, sum_up, sum_qkv, sum_out = (total.astype(jnp.float32) for total in sums)
     return (
         output,
         grad_hidden,
-        wide[8:11].transpose(1, 0, 2).reshape(w_qkv.shape),
-        wide[11],
-        wide[4:8].transpose(1, 0, 2).reshape(w_up.shape),
-        wide[:4].reshape(w_down.shape),
+        sum_qkv,
+        sum_out,
+        sum_up,
+        sum_down,
         small_sums[0],
         small_sums[1],
         small_sums[2],

time: 334 us -> 306 us (0.916); the launches traced: 328 us -> 305 us
  local copies, waits for them, and re-layouts: 38.8 us -> 22.5 us
  Pallas kernels: 230 us -> 219 us
  other arithmetic: 6.81 us -> 13.2 us
    pallas_call x1, Pallas kernels: 147 us -> 136 us  [reduce_gradients(): pl.pallas_call(reduce_kernel, out_shape=[jax.ShapeDtypeStruct((4 * BLOCK,...]
    transpose x4 -> x0, local copies, waits for them, and re-layouts: 8.07 us -> none  [the longest x2 4.59 us: per_device(): wide[8:11].transpose(1, 0, 2).reshape(w_qkv.shape)]
    convert_element_type x1 -> x4, other arithmetic: 2.64 us -> 8.24 us  [per_device(): total.astype(jnp.float32)]
    unnamed x60 -> x62, local copies, waits for them, and re-layouts: 9.34 us -> 4.07 us
where the time goes in v3:
time: 306 us; the launch traced here: 305 us
  Pallas kernels  219 us (72%)
  matrix products  49.5 us (16%)
  local copies, waits for them, and re-layouts  22.5 us (7%)
  other arithmetic  13.2 us (4%)
    pallas_call x1, Pallas kernels, reduce_gradients(): pl.pallas_call(reduce_kernel, out_shape=[jax.ShapeDtypeStruct((4 * BLOCK,...  136 us
    pallas_call x1, Pallas kernels, gather_weights(): pl.pallas_call(gather_kernel, out_shape=[jax.ShapeDtypeStruct((w.shape[0]...  82.8 us
    dot_general x1, matrix products, forward(): up_in = jnp.dot(normed_mid, full_up, preferred_element_type=jnp.float32)  8.6 us
    convert_element_type x4, other arithmetic, per_device(): total.astype(jnp.float32)  8.24 us
    dot_general x1, matrix products, per_device(): jnp.dot(grad_up_in, full_up.T, preferred_element_type=jnp.float32)  7.73 us
    dot_general x2, matrix products, put_rows(): jnp.dot(hit.astype(jnp.bfloat16), rows, preferred_element_type=jnp.float32)  7.18 us

profile of v3, /device:TPU:0, one launch (start us, length us, event | category | flops | bytes accessed | tf_op | source)
XLA Modules:
  0.0 305.4 jit_solution(7332141325078415281)
XLA Ops:
  0.7 0.7 compare_select_fusion
  1.4 0.0 copy-start.21
  1.4 4.3 %gather_fusion = bf16[256,1024]{1,0:T(8,128)(2,1)S(1)} fusion(bf16[2048,1024]{1,0:T(8,128)(2,1)} %param.11, s32[1024]{0:T(1024)S(1)} %pad_clamp_fusion), kind=kCustom, calls=%fused_computation | custom fusion | bytes 1049600 | tf_op jit(solution)/shard_map/gather | solution.py:24
  5.7 0.2 fusion.28
  5.9 0.0 copy-done.20
  5.9 0.5 fusion.53
  6.4 4.3 %gather_fusion.1 = bf16[256,1024]{1,0:T(8,128)(2,1)S(1)} fusion(bf16[2048,1024]{1,0:T(8,128)(2,1)} %param.12, s32[1024]{0:T(1024)S(1)} %pad_clamp_fusion), kind=kCustom, calls=%fused_computation.1 | custom fusion | bytes 1049600 | tf_op jit(solution)/shard_map/gather | solution.py:685
  10.7 1.1 fusion.20
  11.8 82.8 %gather_weights.1 = (bf16[1024,3072]{1,0:T(8,128)(2,1)}, bf16[1024,1024]{1,0:T(8,128)(2,1)}, bf16[1024,4096]{1,0:T(8,128)(2,1)}, bf16[4096,1024]{1,0:T(8,128)(2,1)}) custom-call(bf16[128,3072]{1,0:T(8,128)(2,1)} %refs_0_.1, bf16[128,1024]{1,0:T(8,128)(2,1)} %refs_1_.1, bf16[128,4096]{1,0:T(8,128)(2,1)} %refs_2_.1, bf16[512,1024]{1,0:T(8,128)(2,1)} %refs_3_.1), custom_call_target="tpu_custom_call" | custom-call | tf_op jit(solution)/shard_map/gather_weights/pallas_call | solution.py:298
  94.7 0.0 copy-start.19
  94.7 5.7 %convolution_convert_fusion = bf16[256,3072]{1,0:T(8,128)(2,1)} fusion(bf16[256,1024]{1,0:T(8,128)(2,1)S(1)} %get-tuple-element.48.refs_2_, bf16[1024,3072]{1,0:T(8,128)(2,1)} %get-tuple-element.18), kind=kOutput, calls=%fused_computation.19 | convolution fusion | flops 1611399168 | bytes 8388608 | tf_op jit(solution)/shard_map/dot_general | solution.py:28
  100.4 1.9 copy.39
  102.3 0.1 compare_and_fusion
  102.5 0.0 slice-start
  102.5 0.8 fusion.7
  103.3 0.0 copy-start
  103.3 0.9 exponential_reduce_fusion
  104.2 0.0 copy-start.22
  104.3 0.0 slice-start.1
  104.3 1.1 convolution_convert_fusion.3
  105.4 0.1 copy-done
  105.5 1.6 copy-done.9
  107.0 0.8 multiply_reduce_fusion.3
  107.9 0.2 multiply_convert_fusion.2.refs_1_
  108.1 0.4 slice-done.1
  108.5 2.4 fusion.54
  110.9 8.6 %fusion.6 = (bf16[256,4096]{1,0:T(8,128)(2,1)S(1)}, bf16[256,4096]{1,0:T(8,128)(2,1)S(1)}) fusion(f32[256,4096]{1,0:T(8,128)S(1)} %fusion.54, bf16[256,1024]{1,0:T(8,128)(2,1)S(1)} %multiply_convert_fusion.2.refs_1_, bf16[1024,4096]{1,0:T(8,128)(2,1)} %get-tuple-element.20), kind=kOutput, calls=%fused_computation.10 | convolution fusion | flops 2170552320 | bytes 17301504 | tf_op jit(solution)/shard_map/dot_general | solution.py:47
  119.5 0.0 copy-start.13
  119.5 0.0 copy-start.14
  119.5 0.0 copy-start.5
  119.6 7.7 %multiply_reduce_fusion.1 = (f32[1024]{0:T(1024)S(1)}, f32[256]{0:T(256)S(1)}, f32[256,1024]{1,0:T(8,128)S(1)}) fusion(f32[256]{0:T(256)S(1)} %fusion.46, f32[256,1024]{1,0:T(8,128)S(1)} %get-tuple-element.41, bf16[256,1024]{1,0:T(8,128)(2,1)S(1)} %gather_fusion, f32[1024]{0:T(1024)S(1)} %copy-done.22, bf16[256,4096]{1,0:T(8,128)(2,1)S(1)} %get-tuple-element.31.refs_5_, ...), kind=kOutput, calls=%fused_computation.62 | convolution fusion | flops 2149579520 | bytes 13117440 | tf_op jit(solution)/shard_map/dot_general | solution.py:693
  127.3 0.0 copy-done.13
  127.3 3.7 %fusion.24 = (f32[256]{0:T(256)S(1)}, bf16[256,1024]{1,0:T(8,128)(2,1)S(1)}, f32[256,1024]{1,0:T(8,128)}) fusion(bf16[256,1024]{1,0:T(8,128)(2,1)S(1)} %copy-done.5, f32[256]{0:T(256)S(1)} %fusion.47, f32[256]{0:T(256)S(1)} %multiply_multiply_fusion.3, f32[256,1024]{1,0:T(8,128)S(1)} %get-tuple-element.41, bf16[256,1024]{1,0:T(8,128)(2,1)S(1)} %gather_fusion, ...), kind=kOutput, calls=%fused_computation.55 | convolution fusion | flops 2151415552 | bytes 15213568 | tf_op jit(solution)/shard_map/dot_general | solution.py:49
  131.0 0.0 copy-done.24
  131.0 0.8 copy-done.16
  131.8 1.5 convolution_convert_fusion.2
  133.3 2.0 copy.41
  135.4 3.9 %multiply_reduce_fusion = (f32[16,256]{1,0:T(8,128)S(1)}, f32[16,256,256]{1,2,0:T(8,128)S(1)}) fusion(f32[16,256,256]{1,2,0:T(8,128)} %copy-done, f32[16,256]{1,0:T(8,128)S(1)} %log_add_fusion, pred[256,256]{0,1:T(8,128)(4,1)S(1)} %compare_and_fusion, bf16[256,16,64]{0,2,1:T(8,128)(2,1)} %bitcast.83, bf16[256,3,16,64]{0,3,2,1:T(8,128)(2,1)S(1)} %bitcast.76), kind=kOutput, calls=%fused_computation.13 | convolution fusion | flops 139456512 | bytes 9535488 | tf_op jit(solution)/shard_map/qhd,khd->hqk/dot_general | solution.py:701
  139.3 1.2 multiply_convert_fusion
  140.5 0.5 fusion.17
  141.0 0.0 slice-start.2
  141.0 0.8 fusion.16
  141.8 0.0 slice-start.3
  141.8 1.1 fusion.18
  142.9 0.2 pad_maximum_fusion
  143.1 1.1 slice-done.3
  144.1 2.9 fusion.23
  147.0 0.3 fusion.55
  147.4 0.6 stack.33.refs_8_
  148.0 1.7 copy.46.refs_6_
  149.7 2.0 copy.45.refs_3_
  151.8 136.2 %reduce_gradients.1 = (bf16[512,1024]{1,0:T(8,128)(2,1)}, bf16[128,4096]{1,0:T(8,128)(2,1)}, bf16[128,3072]{1,0:T(8,128)(2,1)}, bf16[128,1024]{1,0:T(8,128)(2,1)}, f32[8,1024]{1,0:T(8,128)}) custom-call(bf16[256,4096]{1,0:T(8,128)(2,1)} %copy-done.14, bf16[256,1024]{1,0:T(8,128)(2,1)} %copy-done.12, bf16[256,1024]{1,0:T(8,128)(2,1)} %copy-done.8, ...), custom_call_target="tpu_custom_call" | custom-call | tf_op jit(solution)/shard_map/reduce_gradients/pallas_call | solution.py:608
  288.0 0.0 copy-start.2
  288.1 0.0 copy-start.26
  288.1 2.9 convert_element_type.102
  291.0 3.2 %convert_element_type.103 = f32[512,1024]{1,0:T(8,128)} convert(bf16[512,1024]{1,0:T(8,128)(2,1)} %get-tuple-element.25) | non-fusion elementwise | flops 524288 | bytes 3145728 | tf_op jit(solution)/shard_map/convert_element_type | solution.py:731
  294.2 1.3 convert_element_type.100
  295.5 0.8 convert_element_type.101
  296.3 1.5 fusion.52
  297.8 0.4 fusion.9
  298.2 0.0 copy-start.3
  298.2 0.0 copy-start.23
  298.2 4.1 %convert_select_fusion = bf16[2048,1024]{1,0:T(8,128)(2,1)} fusion(bf16[2048,1024]{1,0:T(8,128)(2,1)S(1)} %copy-done.2, pred[2048]{0:T(1024)(128)(4,1)S(1)} %fusion.9, s32[256]{0:T(256)S(1)} %bitcast.93, bf16[256,1024]{1,0:T(8,128)(2,1)S(1)} %copy-done.6, bf16[256,1024]{1,0:T(8,128)(2,1)S(1)} %gather_fusion, f32[256,1024]{1,0:T(8,128)S(1)} %copy-done.26, ...), kind=kOutput, calls=%fused_computation.11 | convolution fusion | flops 1083179008 | bytes 12603392 | tf_op jit(solution)/shard_map/dot_general | solution.py:653
  302.4 3.1 %convert_select_fusion.1 = bf16[2048,1024]{1,0:T(8,128)(2,1)} fusion(bf16[2048,1024]{1,0:T(8,128)(2,1)S(1)} %copy-done.3, pred[2048]{0:T(1024)(128)(4,1)S(1)} %fusion.9, s32[256]{0:T(256)S(1)} %bitcast.94, bf16[256,1024]{1,0:T(8,128)(2,1)S(1)} %gather_fusion, f32[256,1024]{1,0:T(8,128)S(1)} %copy-done.23, f32[256]{0:T(256)S(1)} %broadcast_select_fusion), kind=kOutput, calls=%fused_computation.14 | convolution fusion | flops 1079508992 | bytes 9965568 | tf_op jit(solution)/shard_map/dot_general | solution.py:653
  (51 shorter events, 0.2 us)
Async XLA Ops:
  0.6 5.2 %copy-start.20 = (f32[1024]{0:T(1024)S(1)}, f32[1024]{0:T(1024)}, u32[]{:S(2)}) copy-start(f32[1024]{0:T(1024)} %param.19) | copy-start | bytes 12292
  1.3 9.4 %copy-start.18 = (s32[1,256]{1,0:T(1,128)S(1)}, s32[1,256]{1,0:T(1,128)}, u32[]{:S(2)}) copy-start(s32[1,256]{1,0:T(1,128)} %param.14) | copy-start | bytes 3076
  1.4 9.4 %copy-start.21 = (f32[1024]{0:T(1024)S(1)}, f32[1024]{0:T(1024)}, u32[]{:S(2)}) copy-start(f32[1024]{0:T(1024)} %param.20) | copy-start | bytes 12292
  10.7 84.0 %copy-start.4 = (bf16[256,1024]{1,0:T(8,128)(2,1)}, bf16[256,1024]{1,0:T(8,128)(2,1)S(1)}, u32[]{:S(2)}) copy-start(bf16[256,1024]{1,0:T(8,128)(2,1)S(1)} %gather_fusion.1) | copy-start | bytes 1572868
  11.8 82.9 %copy-start.8 = (bf16[256,1024]{1,0:T(8,128)(2,1)}, bf16[256,1024]{1,0:T(8,128)(2,1)S(1)}, u32[]{:S(2)}) copy-start(bf16[256,1024]{1,0:T(8,128)(2,1)S(1)} %get-tuple-element.48.refs_2_) | copy-start | bytes 1572868
  94.7 7.6 %copy-start.19 = (s32[1,256]{1,0:T(1,128)S(1)}, s32[1,256]{1,0:T(1,128)}, u32[]{:S(2)}) copy-start(s32[1,256]{1,0:T(1,128)} %param.13) | copy-start | bytes 3076
  102.5 5.6 %slice-start = ((s8[8388608]{0:T(1024)(128)(4,1)}), s8[4194304]{0:T(1024)(128)(4,1)S(1)}, s32[]{:S(2)}) async-start(s8[8388608]{0:T(1024)(128)(4,1)} %bitcast.103), calls=%async_computation | async-start | bytes 8388608
  103.3 2.1 copy-start
  104.2 2.8 copy-start.9
  104.2 3.6 %copy-start.22 = (f32[1024]{0:T(1024)S(1)}, f32[1024]{0:T(1024)}, u32[]{:S(2)}) copy-start(f32[1024]{0:T(1024)} %param.21) | copy-start | bytes 12292
  104.3 4.2 %slice-start.1 = ((s8[8388608]{0:T(1024)(128)(4,1)}), s8[4194304]{0:T(1024)(128)(4,1)S(1)}, s32[]{:S(2)}) async-start(s8[8388608]{0:T(1024)(128)(4,1)} %bitcast.103), calls=%async_computation.1 | async-start | bytes 8388608
  105.5 5.4 %copy-start.10 = (bf16[16,64,256]{2,1,0:T(8,128)(2,1)}, bf16[16,64,256]{2,1,0:T(8,128)(2,1)S(1)}, u32[]{:S(2)}) copy-start(bf16[16,64,256]{2,1,0:T(8,128)(2,1)S(1)} %convolution_convert_fusion.3) | copy-start | bytes 1572868
  105.5 3.0 copy-start.7
  108.1 2.8 copy-start.12
  119.5 7.8 %copy-start.13 = (bf16[256,4096]{1,0:T(8,128)(2,1)}, bf16[256,4096]{1,0:T(8,128)(2,1)S(1)}, u32[]{:S(2)}) copy-start(bf16[256,4096]{1,0:T(8,128)(2,1)S(1)} %get-tuple-element.31.refs_5_) | copy-start | bytes 6291460
  119.5 7.8 %copy-start.14 = (bf16[256,4096]{1,0:T(8,128)(2,1)}, bf16[256,4096]{1,0:T(8,128)(2,1)S(1)}, u32[]{:S(2)}) copy-start(bf16[256,4096]{1,0:T(8,128)(2,1)S(1)} %get-tuple-element.32.refs_0_) | copy-start | bytes 6291460
  119.5 7.8 %copy-start.5 = (bf16[256,1024]{1,0:T(8,128)(2,1)S(1)}, bf16[256,1024]{1,0:T(8,128)(2,1)}, u32[]{:S(2)}) copy-start(bf16[256,1024]{1,0:T(8,128)(2,1)} %copy-done.4) | copy-start | bytes 1572868
  127.3 3.7 %copy-start.24 = (f32[256,1024]{1,0:T(8,128)}, f32[256,1024]{1,0:T(8,128)S(1)}, u32[]{:S(2)}) copy-start(f32[256,1024]{1,0:T(8,128)S(1)} %get-tuple-element.42) | copy-start | bytes 3145732
  131.0 0.8 copy-start.16
  135.4 3.9 %copy-start.1 = (f32[16,256,256]{1,2,0:T(8,128)S(1)}, f32[16,256,256]{1,2,0:T(8,128)}, u32[]{:S(2)}) copy-start(f32[16,256,256]{1,2,0:T(8,128)} %copy-done) | copy-start | bytes 12582916
  140.5 1.3 copy-start.11
  141.0 2.0 slice-start.2
  141.8 2.3 slice-start.3
  288.0 6.2 %copy-start.15 = (bf16[128,3072]{1,0:T(8,128)(2,1)S(1)}, bf16[128,3072]{1,0:T(8,128)(2,1)}, u32[]{:S(2)}) copy-start(bf16[128,3072]{1,0:T(8,128)(2,1)} %get-tuple-element.22) | copy-start | bytes 2359300
  288.0 7.5 %copy-start.17 = (bf16[128,1024]{1,0:T(8,128)(2,1)S(1)}, bf16[128,1024]{1,0:T(8,128)(2,1)}, u32[]{:S(2)}) copy-start(bf16[128,1024]{1,0:T(8,128)(2,1)} %get-tuple-element.23) | copy-start | bytes 786436
  288.0 10.1 %copy-start.2 = (bf16[2048,1024]{1,0:T(8,128)(2,1)S(1)}, bf16[2048,1024]{1,0:T(8,128)(2,1)}, u32[]{:S(2)}) copy-start(bf16[2048,1024]{1,0:T(8,128)(2,1)} %param.12) | copy-start | bytes 12582916
  288.1 10.1 %copy-start.6 = (bf16[256,1024]{1,0:T(8,128)(2,1)S(1)}, bf16[256,1024]{1,0:T(8,128)(2,1)}, u32[]{:S(2)}) copy-start(bf16[256,1024]{1,0:T(8,128)(2,1)} %copy-done.4) | copy-start | bytes 1572868
  288.1 10.1 %copy-start.25 = (f32[256,1024]{1,0:T(8,128)S(1)}, f32[256,1024]{1,0:T(8,128)}, u32[]{:S(2)}) copy-start(f32[256,1024]{1,0:T(8,128)} %copy-done.24) | copy-start | bytes 3145732
  288.1 10.1 %copy-start.26 = (f32[256,1024]{1,0:T(8,128)S(1)}, f32[256,1024]{1,0:T(8,128)}, u32[]{:S(2)}) copy-start(f32[256,1024]{1,0:T(8,128)} %get-tuple-element.46) | copy-start | bytes 3145732
  298.2 4.1 %copy-start.3 = (bf16[2048,1024]{1,0:T(8,128)(2,1)S(1)}, bf16[2048,1024]{1,0:T(8,128)(2,1)}, u32[]{:S(2)}) copy-start(bf16[2048,1024]{1,0:T(8,128)(2,1)} %param.11) | copy-start | bytes 12582916
  298.2 4.1 %copy-start.23 = (f32[256,1024]{1,0:T(8,128)S(1)}, f32[256,1024]{1,0:T(8,128)}, u32[]{:S(2)}) copy-start(f32[256,1024]{1,0:T(8,128)} %get-tuple-element.43) | copy-start | bytes 3145732

commit v4 on v3

--- a/solution.py
+++ b/solution.py
@@ -194,13 +194,55 @@
 GATHER_KINDS = 13
 
 
-def gather_kernel(*refs):
-    shards, fulls, kept = refs[0:4], refs[4:8], refs[8:12]
-    kept_in, kept_out, send, recv = refs[12:16]
+ROOT = 0.7978845608028654
+CUBE = 0.044715
+EPSILON = 1e-06
+
+
+def tile(i, size):
+    return pl.ds(pl.multiple_of(i * size, size), size)
+
+
+def each(count, fn):
+    def step(i, carry):
+        fn(i)
+        return carry
+
+    lax.fori_loop(0, count, step, 0)
+
+
+def dot(left, right, dims=((1,), (0,))):
+    return lax.dot_general(left, right, (dims, ((), ())), preferred_element_type=jnp.float32)
+
+
+def inverse_size(values):
+    return lax.rsqrt(jnp.mean(values * values, axis=-1, keepdims=True) + EPSILON)
+
+
+def lane_half(shape):
+    return lax.broadcasted_iota(jnp.int32, shape, 1) < HEAD
+
+
+def head_probs(query, keys, allowed):
+    scores = jnp.where(allowed, dot(query, keys, ((1,), (1,))) * 0.125, -1000000000.0)
+    raised = jnp.exp(scores - jnp.max(scores, axis=-1, keepdims=True))
+    return raised / jnp.sum(raised, axis=-1, keepdims=True)
+
+
+def forward_kernel(*refs):
+    shards = refs[0:4]
+    hidden, cotangent, pos_col, pos_row, doc_col, doc_row, router, gain_one, gain_two = refs[4:13]
+    outs = refs[13:30]
+    fulls = refs[30:34]
+    (tokens, cotokens, hit, routed, taken, normed_in, packed, attended, attn_out, middle) = refs[34:44]
+    (normed_mid, slope, activated, grad_mlp, grad_branch, rows_out, score, gate) = refs[44:52]
+    own_in, token_in, out_sem, send, recv = refs[52:57]
     z, f, core, along_x, along_y, across = places()
     pair = flip(z, 1)
     at_core, at_x, at_y, at_z = (z, core), (z, along_x), (z, along_y), (pair, f)
     greet((at_core, at_x, at_y, at_z))
+    count = routed.shape[0]
+    part = count // 4
 
     def rows_of(w, origin, start, size):
         rows = shards[w].shape[0]
@@ -263,57 +305,188 @@
             plan[w][kind].wait_recv()
             plan[w][onward].start()
 
-    loads = [pltpu.make_async_copy(shards[w], kept[w], kept_in.at[w]) for w in range(4)]
-    stores = [
-        pltpu.make_async_copy(kept[w], fulls[w].at[rows_of(w, f, 0, shards[w].shape[0])], kept_out.at[w])
+    def finish(w):
+        loads[w].wait()
+        for kind in (2,) + tuple(range(7, GATHER_KINDS)):
+            plan[w][kind].wait_recv()
+        put(w, fulls[w])
+
+    def put(i, source):
+        pltpu.make_async_copy(source, outs[i], out_sem.at[i]).start()
+
+    def settle(i, source):
+        pltpu.make_async_copy(source, outs[i], out_sem.at[i]).wait()
+
+    loads = [
+        pltpu.make_async_copy(
+            shards[w], fulls[w].at[rows_of(w, f, 0, shards[w].shape[0])], own_in.at[w]
+        )
         for w in range(4)
     ]
-    order = (1,0,2,3)
-    first(order[0])
-    first(order[1])
+    token_loads = [
+        pltpu.make_async_copy(hidden, tokens, token_in.at[0]),
+        pltpu.make_async_copy(cotangent, cotokens, token_in.at[1]),
+    ]
+    first(0)
+    first(1)
+    for load in token_loads + loads:
+        load.start()
+
+    def mark(i):
+        slots = lax.broadcasted_iota(jnp.int32, (part, hit.shape[1]), 1)
+        hit[tile(i, part)] = (slots == pos_col[tile(i, part)]).astype(jnp.bfloat16)
+
+    each(4, mark)
+
+    def take(source, target):
+        def columns(n):
+            target[:, tile(n, 256)] = dot(hit[...], source[:, tile(n, 256)]).astype(target.dtype)
+
+        each(D // 256, columns)
+
+    token_loads[0].wait()
+    take(tokens, routed)
+    token_loads[1].wait()
+    take(cotokens, taken)
+
+    def open_rows(i):
+        at = tile(i, part)
+        rows = routed[at]
+        normed_in[at] = (rows * inverse_size(rows) * gain_one[...]).astype(jnp.bfloat16)
+        router_out = jnp.sum(rows * router[...], axis=-1, keepdims=True)
+        gate_rows = jnp.where(doc_col[at] < 2, router_out, 0.0)
+        gate[at] = jnp.broadcast_to(gate_rows, (part, 128))
+        grad_rows = taken[at].astype(jnp.float32) * gate_rows
+        grad_branch[at] = grad_rows
+        grad_mlp[at] = grad_rows.astype(jnp.bfloat16)
+
+    each(4, open_rows)
+    for i, source in ((4, routed), (5, taken), (6, normed_in), (13, grad_mlp), (14, grad_branch)):
+        put(i, source)
+    second(0)
+    first(2)
+    second(1)
+    first(3)
+    third(0)
+    finish(0)
+
+    def pack(n):
+        packed[:, tile(n, 512)] = dot(normed_in[...], fulls[0][:, tile(n, 512)]).astype(jnp.bfloat16)
+
+    each(6, pack)
+    put(7, packed)
+    second(2)
+
+    def attend(i):
+        query, keys, values = (packed[:, tile(i + 8 * k, 128)] for k in range(3))
+        allowed = (doc_col[...] == doc_row[...]) & (pos_row[...] <= pos_col[...])
+        low = lane_half(query.shape)
+        zero = jnp.zeros_like(query)
+        mixed = [
+            dot(head_probs(jnp.where(keep, query, zero), keys, allowed).astype(jnp.bfloat16), values)
+            for keep in (low, ~low)
+        ]
+        attended[:, tile(i, 128)] = jnp.where(low, mixed[0], mixed[1]).astype(jnp.bfloat16)
+
+    each(HEADS // 2, attend)
+    put(8, attended)
+    third(1)
+    finish(1)
+
+    def project(n):
+        attn_out[:, tile(n, 256)] = dot(attended[...], fulls[1][:, tile(n, 256)])
+
+    each(4, project)
+
+    def middle_rows(i):
+        at = tile(i, part)
+        rows = routed[at] + attn_out[at]
+        middle[at] = rows
+        normed_mid[at] = (rows * inverse_size(rows) * gain_two[...]).astype(jnp.bfloat16)
+
+    each(4, middle_rows)
+    put(9, middle)
+    put(10, normed_mid)
+    second(3)
+    third(2)
+    finish(2)
+
+    def raise_up(n):
+        at = tile(n, 256)
+        up = dot(normed_mid[...], fulls[2][:, at])
+        square = up * up
+        bend = jnp.tanh(ROOT * (up + CUBE * (square * up)))
+        ahead = 0.5 * (1.0 + bend)
+        activated[:, at] = (up * ahead).astype(jnp.bfloat16)
+        slope[:, at] = ahead + 0.5 * up * (1.0 - bend * bend) * (ROOT * (1.0 + 3.0 * CUBE * square))
+
+    each(16, raise_up)
+    put(11, activated)
+    put(12, slope)
+    third(3)
+    finish(3)
+
+    def lower(n):
+        at = tile(n, 256)
+        attn_out[:, at] = attn_out[:, at] + dot(activated[...], fulls[3][:, at])
+
+    each(4, lower)
+
+    def close_rows(i):
+        at = tile(i, part)
+        branch = attn_out[at]
+        rows_out[at] = (routed[at] + gate[at, 0:1] * branch).astype(jnp.bfloat16)
+        grad_add = jnp.where(doc_col[at] < 2, taken[at].astype(jnp.float32), 0.0)
+        total = jnp.sum(grad_add * branch, axis=-1, keepdims=True)
+        score[at] = jnp.broadcast_to(total, (part, 128))
+
+    each(4, close_rows)
+    put(15, rows_out)
+    put(16, score)
+    kept = (routed, taken, normed_in, packed, attended, middle, normed_mid, activated, slope)
+    for i, source in enumerate(tuple(fulls) + kept + (grad_mlp, grad_branch, rows_out, score)):
+        settle(i, source)
     for w in range(4):
-        loads[w].start()
-    for w in range(4):
-        loads[w].wait()
-        stores[w].start()
-    second(order[0])
-    first(order[2])
-    second(order[1])
-    first(order[3])
-    third(order[0])
-    second(order[2])
-    third(order[1])
-    second(order[3])
-    third(order[2])
-    third(order[3])
-    for w in range(4):
-        stores[w].wait()
         for kind in range(GATHER_KINDS):
-            if kind == 2 or kind >= 7:
-                plan[w][kind].wait_recv()
             plan[w][kind].wait_send()
 
 
-def gather_weights(weights, parts):
+def run_forward(weights, parts, hidden, cotangent, positions, documents, router, gain_one, gain_two):
+    bf16, f32, dma = jnp.bfloat16, jnp.float32, pltpu.SemaphoreType.DMA
+    count, wide = positions.shape[0], weights[2].shape[1]
+    full = [((w.shape[0] * parts, w.shape[1]), w.dtype) for w in weights]
+    row, head_row, wide_row = (count, D), (count, 3 * D), (count, wide)
+    kept = [(row, f32), (row, bf16), (row, bf16), (head_row, bf16), (row, bf16), (row, f32)]
+    kept += [(row, bf16), (wide_row, bf16), (wide_row, f32), (row, bf16), (row, f32), (row, bf16)]
+    kept += [((count, 128), f32)]
+    held = [(hidden.shape, bf16)] * 2 + [((count, hidden.shape[0]), bf16), (row, f32), (row, bf16)]
+    held += [(row, bf16), (head_row, bf16), (row, bf16), (row, f32), (row, f32), (row, bf16)]
+    held += [(wide_row, f32), (wide_row, bf16), (row, bf16), (row, f32), (row, bf16)]
+    held += [((count, 128), f32)] * 2
     return pl.pallas_call(
-        gather_kernel,
-        out_shape=[
-            jax.ShapeDtypeStruct((w.shape[0] * parts, w.shape[1]), w.dtype) for w in weights
-        ],
-        in_specs=[pl.BlockSpec(memory_space=ANY)] * 4,
-        out_specs=[pl.BlockSpec(memory_space=ANY)] * 4,
-        scratch_shapes=[pltpu.VMEM(w.shape, w.dtype) for w in weights]
-        + [
-            pltpu.SemaphoreType.DMA((4,)),
-            pltpu.SemaphoreType.DMA((4,)),
-            pltpu.SemaphoreType.DMA((4, GATHER_KINDS)),
-            pltpu.SemaphoreType.DMA((4, GATHER_KINDS)),
-        ],
+        forward_kernel,
+        out_shape=[jax.ShapeDtypeStruct(*each_one) for each_one in full + kept],
+        in_specs=[pl.BlockSpec(memory_space=ANY)] * 6
+        + [pl.BlockSpec(memory_space=pltpu.VMEM)] * 7,
+        out_specs=[pl.BlockSpec(memory_space=ANY)] * 17,
+        scratch_shapes=[pltpu.VMEM(*each_one) for each_one in full + held]
+        + [dma((4,)), dma((2,)), dma((17,)), dma((4, GATHER_KINDS)), dma((4, GATHER_KINDS))],
         compiler_params=pltpu.CompilerParams(
             collective_id=1, has_side_effects=True, vmem_limit_bytes=60 * 1024 * 1024
         ),
-        name="gather_weights",
-    )(*weights)
+        name="gather_and_forward",
+    )(
+        *weights,
+        hidden,
+        cotangent,
+        positions[:, None],
+        positions[None],
+        documents[:, None],
+        documents[None],
+        router[None],
+        gain_one[None],
+        gain_two[None],
+    )
 
 
 CHUNKS = 24
@@ -659,37 +832,50 @@
 ):
     positions = route_pos[0]
     documents = route_doc[0]
-    live_mask = (documents < 2).astype(jnp.float32)[:, None]
-    weights = gather_weights((w_qkv, w_out, w_up, w_down), 8)
-    state = forward(hidden, positions, documents, weights, router, gain_one, gain_two)
-    full_qkv, full_out, full_up, full_down = weights
     (
+        full_qkv,
+        full_out,
+        full_up,
+        full_down,
         routed,
-        router_out,
+        taken,
         normed_in,
-        heads,
-        prob_rows,
-        prob_low,
+        packed,
         attended,
-        attn_out,
         middle,
         normed_mid,
-        up_in,
         activated,
-        mlp_out,
-    ) = state
+        slope,
+        grad_mlp,
+        grad_branch,
+        rows_out,
+        score,
+    ) = run_forward(
+        (w_qkv, w_out, w_up, w_down),
+        8,
+        hidden,
+        cotangent,
+        positions,
+        documents,
+        router,
+        gain_one,
+        gain_two,
+    )
     row_count = routed.shape[0]
-    branch_out = attn_out + mlp_out
-    added = live_mask * router_out[:, None] * branch_out
-    output = put_rows(hidden, (routed + added).astype(jnp.bfloat16), positions)
-    taken = cotangent[positions].astype(jnp.float32)
-    grad_add = live_mask * taken
-    grad_branch = grad_add * router_out[:, None]
-    grad_score = jnp.sum(grad_add * branch_out, axis=-1)
-    grad_mlp = grad_branch.astype(jnp.bfloat16)
+    output = put_rows(hidden, rows_out, positions)
+    grad_score = score[:, 0]
+    heads = packed.reshape(row_count, 3, HEADS, HEAD)
+    allowed = (documents[:, None] == documents[None, :]) & (
+        positions[None, :] <= positions[:, None]
+    )
+    scores = (
+        jnp.einsum("qhd,khd->hqk", heads[:, 0], heads[:, 1], preferred_element_type=jnp.float32)
+        * 0.125
+    )
+    prob_rows = jax.nn.softmax(jnp.where(allowed[None], scores, -1000000000.0), axis=-1)
+    prob_low = prob_rows.astype(jnp.bfloat16)
     grad_act = jnp.dot(grad_mlp, full_down.T, preferred_element_type=jnp.float32)
-    _, gelu_pull = jax.vjp(jax.nn.gelu, up_in)
-    grad_up_in = gelu_pull(grad_act)[0].astype(jnp.bfloat16)
+    grad_up_in = (grad_act * slope).astype(jnp.bfloat16)
     grad_norm_mid = jnp.dot(grad_up_in, full_up.T, preferred_element_type=jnp.float32)
     _, second_pull = jax.vjp(rms_scale, middle, gain_two)
     grad_middle, grad_gain_two = second_pull(grad_norm_mid)
@@ -721,7 +907,7 @@
     grad_routed, grad_gain_one = first_pull(grad_norm_in)
     grad_routed = grad_routed + grad_middle + grad_score[:, None] * router[None, :]
     grad_router = jnp.dot(grad_score, routed, precision=lax.Precision.HIGHEST)
-    grad_hidden = put_rows(cotangent, (taken + grad_routed).astype(jnp.bfloat16), positions)
+    grad_hidden = put_rows(cotangent, (taken.astype(jnp.float32) + grad_routed).astype(jnp.bfloat16), positions)
     small = jnp.stack([grad_router, grad_gain_one, grad_gain_two] + [jnp.zeros_like(grad_router)] * 5)
     *sums, small_sums = reduce_gradients(
         (activated, normed_mid, normed_in, attended),

time: 306 us -> 292 us (0.954)
  matrix products: 49.5 us -> 34.8 us
  Pallas kernels: 219 us -> 231 us
  local copies, waits for them, and re-layouts: 22.5 us -> 13.3 us
    dot_general x7 -> x1, matrix products: 21.2 us -> 0.76 us  [per_device(): jnp.einsum('qhd,khd->hqk', heads[:, 0], heads[:, 1], preferred_element_ty...]
    pallas_call x1, Pallas kernels: 82.8 us -> 93.5 us  [run_forward(): pl.pallas_call(forward_kernel, out_shape=[jax.ShapeDtypeStruct(*each_one)...]
    gather x2 -> x0, local copies, waits for them, and re-layouts: 8.6 us -> none  [the longest x1 4.31 us: per_device(): taken = cotangent[positions].astype(jnp.float32)]
    dot_general x1, matrix products: 2.39 us -> 7.03 us  [per_device(): jnp.dot(grad_mlp, full_down.T, preferred_element_type=jnp.float32)]
    convert_element_type x2 -> x0, local copies, waits for them, and re-layouts: 3.92 us -> none  [the longest x1 2.04 us: forward(): attended = attended.reshape(row_count, D).astype(jnp.bfloat16)]
    dot_general x2, matrix products: 7.18 us -> 10.8 us  [put_rows(): jnp.dot(hit.astype(jnp.bfloat16), rows, preferred_element_type=jnp.float32)]
    dot_general x1, matrix products: 3.92 us -> 0.84 us  [per_device(): jnp.einsum('qhd,khd->hqk', grad_attended, heads[:, 2], preferred_element_...]
where the time goes in v4:
time: 292 us
  Pallas kernels  231 us (79%)
  matrix products  34.8 us (12%)
  local copies, waits for them, and re-layouts  13.3 us (5%)
  other arithmetic  11.4 us (4%)
    pallas_call x1, Pallas kernels, reduce_gradients(): pl.pallas_call(reduce_kernel, out_shape=[jax.ShapeDtypeStruct((4 * BLOCK,...  138 us
    pallas_call x1, Pallas kernels, run_forward(): pl.pallas_call(forward_kernel, out_shape=[jax.ShapeDtypeStruct(*each_one)...  93.5 us
    dot_general x2, matrix products, put_rows(): jnp.dot(hit.astype(jnp.bfloat16), rows, preferred_element_type=jnp.float32)  10.8 us
    dot_general x1, matrix products, per_device(): jnp.dot(grad_mlp, full_down.T, preferred_element_type=jnp.float32)  7.03 us
    dot_general x1, matrix products, per_device(): jnp.dot(grad_up_in, full_up.T, preferred_element_type=jnp.float32)  7.03 us

profile of v4, /device:TPU:0, one launch (start us, length us, event | category | flops | bytes accessed | tf_op | source)
XLA Modules:
  0.0 291.9 jit_solution(12558805244824554173)
XLA Ops:
  0.6 1.0 fusion.7
  1.7 0.9 compare_and_fusion
  2.6 1.5 copy.38.refs_8_
  4.1 1.5 copy.37.refs_6_
  5.5 93.5 %gather_and_forward.1 = (bf16[1024,3072]{1,0:T(8,128)(2,1)}, bf16[1024,1024]{1,0:T(8,128)(2,1)}, bf16[1024,4096]{1,0:T(8,128)(2,1)}, bf16[4096,1024]{1,0:T(8,128...) custom-call(bf16[128,3072]{1,0:T(8,128)(2,1)} %refs_0_.1, ...), custom_call_target="tpu_custom_call" | custom-call | tf_op jit(solution)/shard_map/gather_and_forward/pallas_call | solution.py:466
  99.0 0.0 copy-start.10
  99.0 1.1 slice_reduce_fusion
  100.1 1.4 multiply_reduce_fusion.6
  101.5 1.8 fusion.39
  103.3 1.7 copy.39
  105.0 0.0 copy-done.10
  105.1 0.0 copy-start.1
  105.1 0.0 copy-start.13
  105.1 7.0 %fusion.1.refs_5_ = bf16[256,4096]{1,0:T(8,128)(2,1)S(1)} fusion(f32[256,4096]{1,0:T(8,128)} %get-tuple-element.37, bf16[256,1024]{1,0:T(8,128)(2,1)S(1)} %copy-done.10, bf16[4096,1024]{1,0:T(8,128)(2,1)} %get-tuple-element.36), kind=kOutput, calls=%fused_computation.2 | convolution fusion | flops 2149580800 | bytes 15204352 | tf_op jit(solution)/shard_map/dot_general | solution.py:877
  112.1 0.0 copy-done.1
  112.1 0.0 copy-done.13
  112.1 0.0 copy-start.3
  112.1 0.0 copy-start
  112.2 0.0 copy-start.8
  112.2 7.0 %multiply_reduce_fusion.1 = (f32[1024]{0:T(1024)S(1)}, f32[256]{0:T(256)S(1)}, f32[256,1024]{1,0:T(8,128)S(1)}) fusion(f32[256,1024]{1,0:T(8,128)S(1)} %copy-done.1, f32[256]{0:T(256)S(1)} %fusion.33, f32[1024]{0:T(1024)S(1)} %copy-done.13, bf16[256,4096]{1,0:T(8,128)(2,1)S(1)} %fusion.1.refs_5_, bf16[1024,4096]{1,0:T(8,128)(2,1)} %get-tuple-element.38), kind=kOutput, calls=%fused_computation.34 | convolution fusion | flops 2149055232 | bytes 12593152 | tf_op jit(solution)/shard_map/dot_general | solution.py:879
  119.2 0.0 copy-done.3
  119.2 0.0 copy-start.7
  119.2 0.0 copy-start.17
  119.2 0.0 copy-done
  119.2 0.0 copy-done.8
  119.3 0.0 copy-start.14
  119.3 0.4 multiply_reduce_fusion.4
  119.7 0.5 copy-done.7
  120.2 1.0 copy-done.17
  121.2 1.5 convolution_convert_fusion
  122.8 2.0 copy.40
  124.8 0.0 copy-done.14
  124.8 4.5 %convert_select_fusion.1 = bf16[2048,1024]{1,0:T(8,128)(2,1)} fusion(bf16[2048,1024]{1,0:T(8,128)(2,1)} %refs_4_.1, pred[2048]{0:T(1024)(128)(4,1)S(1)} %fusion.7, bf16[256,1024]{1,0:T(8,128)(2,1)} %get-tuple-element.31, s32[256]{0:T(256)S(1)} %bitcast.71), kind=kOutput, calls=%fused_computation.8 | convolution fusion | flops 1078460416 | bytes 8915968 | tf_op jit(solution)/shard_map/dot_general | solution.py:826
  129.3 0.0 copy-done.4
  129.3 0.8 fusion.32
  130.0 0.0 copy-start.11
  130.0 1.4 fusion.38
  131.4 0.0 copy-done.11
  131.4 0.8 fusion.16
  132.2 0.0 slice-start
  132.2 0.8 multiply_reduce_fusion
  133.1 0.0 slice-start.1
  133.1 0.9 multiply_convert_fusion
  134.0 0.0 copy-start.16
  134.0 0.8 fusion.14
  134.8 0.5 fusion.15
  135.3 0.2 pad_maximum_fusion
  135.5 2.9 multiply_reduce_fusion.2
  138.4 1.7 copy.44.refs_6_
  140.1 0.7 stack.33.refs_8_
  140.8 137.9 %reduce_gradients.1 = (bf16[512,1024]{1,0:T(8,128)(2,1)}, bf16[128,4096]{1,0:T(8,128)(2,1)}, bf16[128,3072]{1,0:T(8,128)(2,1)}, bf16[128,1024]{1,0:T(8,128)(2,1)}, f32[8,1024]{1,0:T(8,128)}) custom-call(bf16[256,4096]{1,0:T(8,128)(2,1)} %get-tuple-element.44.refs_0_, bf16[256,1024]{1,0:T(8,128)(2,1)} %get-tuple-element.45.refs_1_, ...), custom_call_target="tpu_custom_call" | custom-call | tf_op jit(solution)/shard_map/reduce_gradients/pallas_call | solution.py:781
  278.7 0.0 copy-done.2
  278.7 0.0 copy-done.15
  278.7 0.0 copy-start.12
  278.7 0.0 copy-start.9
  278.8 0.0 copy-start.6
  278.8 6.4 %convert_select_fusion = bf16[2048,1024]{1,0:T(8,128)(2,1)} fusion(bf16[2048,1024]{1,0:T(8,128)(2,1)} %refs_5_.1, pred[2048]{0:T(1024)(128)(4,1)S(1)} %fusion.7, s32[256]{0:T(256)S(1)} %bitcast.72, f32[256,1024]{1,0:T(8,128)S(1)} %copy-done, bf16[256,1024]{1,0:T(8,128)(2,1)} %get-tuple-element.32, f32[256,1024]{1,0:T(8,128)} %get-tuple-element.65, ...), kind=kOutput, calls=%fused_computation.3 | convolution fusion | flops 1082654720 | bytes 13127680 | tf_op jit(solution)/shard_map/dot_general | solution.py:826
  285.2 1.5 fusion.37
  286.6 0.8 convert_element_type.55
  287.5 0.0 copy-done.9
  287.5 1.3 convert_element_type.54
  288.8 0.0 copy-done.6
  288.8 1.5 convert_element_type.56
  290.3 1.6 convert_element_type.57
  (16 shorter events, 0.1 us)
Async XLA Ops:
  99.0 6.0 %copy-start.10 = (bf16[256,1024]{1,0:T(8,128)(2,1)S(1)}, bf16[256,1024]{1,0:T(8,128)(2,1)}, u32[]{:S(2)}) copy-start(bf16[256,1024]{1,0:T(8,128)(2,1)} %get-tuple-element.35.refs_4_) | copy-start | bytes 1572868
  105.1 7.1 %copy-start.1 = (f32[256,1024]{1,0:T(8,128)S(1)}, f32[256,1024]{1,0:T(8,128)}, u32[]{:S(2)}) copy-start(f32[256,1024]{1,0:T(8,128)} %get-tuple-element.39) | copy-start | bytes 3145732
  105.1 7.1 %copy-start.13 = (f32[1024]{0:T(1024)S(1)}, f32[1024]{0:T(1024)}, u32[]{:S(2)}) copy-start(f32[1024]{0:T(1024)} %param.21) | copy-start | bytes 12292
  112.1 7.1 %copy-start.3 = (bf16[256,4096]{1,0:T(8,128)(2,1)}, bf16[256,4096]{1,0:T(8,128)(2,1)S(1)}, u32[]{:S(2)}) copy-start(bf16[256,4096]{1,0:T(8,128)(2,1)S(1)} %fusion.1.refs_5_) | copy-start | bytes 6291460
  112.1 7.1 %copy-start = (f32[256,1024]{1,0:T(8,128)S(1)}, f32[256,1024]{1,0:T(8,128)}, u32[]{:S(2)}) copy-start(f32[256,1024]{1,0:T(8,128)} %get-tuple-element.42) | copy-start | bytes 3145732
  112.2 7.1 %copy-start.8 = (f32[256,1024]{1,0:T(8,128)S(1)}, f32[256,1024]{1,0:T(8,128)}, u32[]{:S(2)}) copy-start(f32[256,1024]{1,0:T(8,128)} %get-tuple-element.34) | copy-start | bytes 3145732
  119.2 1.0 copy-start.7
  119.2 2.0 copy-start.17
  119.3 5.6 %copy-start.14 = (s32[1,256]{1,0:T(1,128)S(1)}, s32[1,256]{1,0:T(1,128)}, u32[]{:S(2)}) copy-start(s32[1,256]{1,0:T(1,128)} %refs_7_.1) | copy-start | bytes 3076
  120.2 9.1 %copy-start.4 = (bf16[256,1024]{1,0:T(8,128)(2,1)}, bf16[256,1024]{1,0:T(8,128)(2,1)S(1)}, u32[]{:S(2)}) copy-start(bf16[256,1024]{1,0:T(8,128)(2,1)S(1)} %get-tuple-element.67.refs_7_) | copy-start | bytes 1572868
  130.0 1.4 copy-start.11
  132.2 3.2 %slice-start = ((s8[6291456]{0:T(1024)(128)(4,1)}), s8[4194304]{0:T(1024)(128)(4,1)S(1)}, s32[]{:S(2)}) async-start(s8[6291456]{0:T(1024)(128)(4,1)} %bitcast.81), calls=%async_computation | async-start | bytes 8388608
  133.1 2.4 slice-start.1
  134.0 1.5 copy-start.16
  140.8 138.0 %copy-start.2 = (f32[256,1024]{1,0:T(8,128)S(1)}, f32[256,1024]{1,0:T(8,128)}, u32[]{:S(2)}) copy-start(f32[256,1024]{1,0:T(8,128)} %get-tuple-element.39) | copy-start | bytes 3145732
  140.8 138.0 %copy-start.15 = (f32[1024]{0:T(1024)S(1)}, f32[1024]{0:T(1024)}, u32[]{:S(2)}) copy-start(f32[1024]{0:T(1024)} %param.19) | copy-start | bytes 12292
  278.7 7.9 %copy-start.12 = (bf16[128,1024]{1,0:T(8,128)(2,1)S(1)}, bf16[128,1024]{1,0:T(8,128)(2,1)}, u32[]{:S(2)}) copy-start(bf16[128,1024]{1,0:T(8,128)(2,1)} %get-tuple-element.49) | copy-start | bytes 786436
  278.7 8.7 %copy-start.9 = (bf16[128,3072]{1,0:T(8,128)(2,1)S(1)}, bf16[128,3072]{1,0:T(8,128)(2,1)}, u32[]{:S(2)}) copy-start(bf16[128,3072]{1,0:T(8,128)(2,1)} %get-tuple-element.48) | copy-start | bytes 2359300
  278.8 10.0 %copy-start.6 = (bf16[128,4096]{1,0:T(8,128)(2,1)S(1)}, bf16[128,4096]{1,0:T(8,128)(2,1)}, u32[]{:S(2)}) copy-start(bf16[128,4096]{1,0:T(8,128)(2,1)} %get-tuple-element.50) | copy-start | bytes 3145732
  285.2 5.2 %copy-start.5 = (bf16[512,1024]{1,0:T(8,128)(2,1)S(1)}, bf16[512,1024]{1,0:T(8,128)(2,1)}, u32[]{:S(2)}) copy-start(bf16[512,1024]{1,0:T(8,128)(2,1)} %get-tuple-element.51) | copy-start | bytes 3145732

commit v5 on v4

--- a/solution.py
+++ b/solution.py
@@ -496,15 +496,15 @@
 BLOCK = 128
 WIDE = 512
 FULL = 1024
-LAST = 7
+PARTS = 12
 
 
 def left_of(t):
-    return jnp.where(t < 8, t // 2, jnp.where(t < 16, 4, jnp.where(t < 22, 5, 6)))
+    return jnp.where(t < 8, t // 2, jnp.where(t < 16, 4, jnp.where(t < 18, 6, 5)))
 
 
 def right_of(t):
-    return jnp.where(t < 8, 0, t // 2 - 3)
+    return jnp.where(t < 8, 0, jnp.where(t < 16, t // 2 - 3, jnp.where(t < 18, 8, t // 2 - 4)))
 
 
 def add_rows(target, sources, rows):
@@ -520,13 +520,18 @@
 
 
 def reduce_kernel(*refs):
-    activated, normed_mid, normed_in, attended, grad_mlp, grad_up_in, grad_packed, grad_attn = refs[:8]
-    small, out_down, out_up, out_qkv, out_out, small_sums = refs[8:14]
-    sums, stored = refs[35:37]
-    (left, right, part, from_x, from_y, last_x, last_y, from_pair, from_far) = refs[14:23]
-    small_sent, small_got = refs[23:25]
-    (in_own, in_send, in_recv, rin_own, rin_send, rin_recv) = refs[25:31]
-    send, recv, small_send, small_recv = refs[31:35]
+    activated, normed_mid, normed_in, attended, grad_mlp = refs[:5]
+    sources, weights = refs[5:12], refs[12:16]
+    pos_col, pos_row, doc_col, doc_row, router, gain_one, gain_two = refs[16:23]
+    out_down, out_up, out_qkv, out_out, out_rows, small_sums = refs[23:29]
+    (left, right, part, from_x, from_y, last_x, last_y, from_pair, from_far, sums) = refs[29:39]
+    held = refs[39:46]
+    slope, packed, middle, routed, taken, grad_branch, score = held
+    (tall, broad, grad_norm, grad_middle, grad_attended, partial) = refs[46:52]
+    small_sent, small_got = refs[52:54]
+    (in_own, in_send, in_recv, rin_own, rin_send, rin_recv) = refs[54:60]
+    send, recv, small_send, small_recv, stored, held_in, tall_in, broad_in = refs[60:68]
+    full_qkv, full_out, full_up, full_down = weights
 
     z, f, core, along_x, along_y, across = places()
     pair, far = flip(z, 1), 3 - z
@@ -546,14 +551,6 @@
             return activated, 4 * BLOCK, i * BLOCK
         return (normed_mid, normed_in, attended)[i - 4], BLOCK, 0
 
-    def right_source(i):
-        if i == 0:
-            return grad_mlp, 0
-        if i < 5:
-            return grad_up_in, (i - 1) * FULL
-        if i < 8:
-            return grad_packed, (i - 5) * FULL
-        return grad_attn, 0
 
     def spread(index):
         return (index, flip(index, 2), flip(index, 4), flip(flip(index, 2), 4))
@@ -583,30 +580,191 @@
         return here + there
 
     def right_copies(i):
-        source, offset = right_source(i)
-        source = source.at[:, pl.ds(offset, FULL)]
         target = right.at[i, mine]
-        return [
-            pltpu.make_async_copy(source, target, rin_own.at[i]),
-            pltpu.make_async_remote_copy(
-                src_ref=source,
-                dst_ref=target,
-                send_sem=rin_send.at[i],
-                recv_sem=rin_recv.at[i],
-                device_id=at_core,
-                device_id_type=MESH,
-            ),
-        ]
+        source = grad_mlp if i == 0 else target
+        there = pltpu.make_async_remote_copy(
+            src_ref=source,
+            dst_ref=target,
+            send_sem=rin_send.at[i],
+            recv_sem=rin_recv.at[i],
+            device_id=at_core,
+            device_id_type=MESH,
+        )
+        return [there] if i else [there, pltpu.make_async_copy(source, target, rin_own.at[0])]
 
     lefts = [left_copies(i) for i in range(LEFTS)]
     rights = [right_copies(i) for i in range(RIGHTS)]
-    new_left = {0: 0, 2: 1, 4: 2, 6: 3, 8: 4, 16: 5, 22: 6}
-    new_right = {0: 0, 8: 1, 10: 2, 12: 3, 14: 4, 16: 5, 18: 6, 20: 7, 22: 8}
+    new_left = {0: 0, 2: 1, 4: 2, 6: 3, 8: 4, 16: 6, 18: 5}
+    new_right = {0: 0, 8: 1, 10: 2, 12: 3, 14: 4, 16: 8, 18: 5, 20: 6, 22: 7}
     for t in range(CHUNKS):
         for copy in lefts[new_left[t]] if t in new_left else ():
             copy.start()
-        for copy in rights[new_right[t]] if t in new_right else ():
+        for copy in rights[0] if t == 0 else ():
             copy.start()
+
+    loads = [pltpu.make_async_copy(sources[i], held[i], held_in.at[i]) for i in range(7)]
+    for load in loads:
+        load.start()
+
+    def tall_copy(source, j, slot):
+        return pltpu.make_async_copy(source.at[tile(j, 512)], tall.at[slot], tall_in.at[slot])
+
+    def broad_copy(source, j, slot):
+        target = broad.at[slot, :, pl.ds(0, source.shape[1])]
+        return pltpu.make_async_copy(source.at[tile(j, 256)], target, broad_in.at[slot])
+
+    def turn_down(t):
+        for k in range(2):
+            slot = t % 2 * 2 + k
+            tall_copy(full_down, 2 * t + k, slot).wait()
+            at = pl.ds(k * 512, 512)
+            grown = dot(right[0, mine], tall[slot], ((1,), (1,)))
+            grown = grown * slope[:, tile(2 * t + k, 512)]
+            right[t + 1, mine, at] = grown.astype(jnp.bfloat16)
+
+    def turn_up(t):
+        slot = t % 2
+        broad_copy(full_up, t, slot).wait()
+        total = dot(right[1, mine], broad[slot, :, 0:FULL], ((1,), (1,)))
+        for k in range(1, 4):
+            total += dot(right[1 + k, mine], broad[slot, :, k * FULL : (k + 1) * FULL], ((1,), (1,)))
+        grad_norm[:, tile(t, 256)] = total
+
+    def norm_turn(values, ahead, gain):
+        inverse = inverse_size(values)
+        scaled = ahead * gain
+        mean = jnp.mean(scaled * values, axis=-1, keepdims=True)
+        back = inverse * scaled - values * (inverse * inverse * inverse * mean)
+        return back, jnp.sum(ahead * values * inverse, axis=0, keepdims=True)
+
+    def turn_middle(i):
+        at = tile(i, 64)
+        back, gain_part = norm_turn(middle[at], grad_norm[at], gain_two[...])
+        grad_middle[at] = back
+        lower = pl.ds(pl.multiple_of((f % 2) * rows + i * 64, 64), 64)
+        right[8, lower] = (grad_branch[at] + back).astype(jnp.bfloat16)
+        partial[2:3] += gain_part
+        partial[0:1] += jnp.sum(score[at, 0:1] * routed[at], axis=0, keepdims=True)
+
+    def turn_out():
+        for k in range(2):
+            tall_copy(full_out, k, k).wait()
+            grad_attended[:, k * 512 : (k + 1) * 512] = dot(
+                right[8, mine], tall[k], ((1,), (1,))
+            ).astype(jnp.bfloat16)
+
+    def turn_heads(i):
+        query, keys, values = (packed[:, tile(i + 8 * k, 128)] for k in range(3))
+        ahead = grad_attended[:, tile(i, 128)]
+        allowed = (doc_col[...] == doc_row[...]) & (pos_row[...] <= pos_col[...])
+        low = lane_half(query.shape)
+        zero = jnp.zeros_like(query)
+        found = []
+        for keep in (low, ~low):
+            probs = head_probs(jnp.where(keep, query, zero), keys, allowed)
+            grad_prob = dot(jnp.where(keep, ahead, zero), values, ((1,), (1,)))
+            row_dot = jnp.sum(grad_prob * probs, axis=-1, keepdims=True)
+            grad_scores = (probs * (grad_prob - row_dot)).astype(jnp.bfloat16)
+            found.append(
+                (
+                    dot(grad_scores, keys) * 0.125,
+                    dot(grad_scores, query, ((0,), (0,))) * 0.125,
+                    dot(probs.astype(jnp.bfloat16), ahead, ((0,), (0,))),
+                )
+            )
+        for k in range(3):
+            mixed = jnp.where(low, found[0][k], found[1][k]).astype(jnp.bfloat16)
+            right[5 + k, mine, tile(i, 128)] = mixed
+
+    def turn_in(t):
+        slot = t % 2
+        broad_copy(full_qkv, t, slot).wait()
+        total = dot(right[5, mine], broad[slot, :, 0:FULL], ((1,), (1,)))
+        for k in range(1, 3):
+            total += dot(right[5 + k, mine], broad[slot, :, k * FULL : (k + 1) * FULL], ((1,), (1,)))
+        grad_norm[:, tile(t, 256)] = total
+
+    def turn_rows(i):
+        at = tile(i, 64)
+        back, gain_part = norm_turn(routed[at], grad_norm[at], gain_one[...])
+        partial[1:2] += gain_part
+        total = back + grad_middle[at] + score[at, 0:1] * router[...]
+        grad_attended[at] = (taken[at].astype(jnp.float32) + total).astype(jnp.bfloat16)
+
+    def work(t):
+        @pl.when(t == 0)
+        def _():
+            loads[0].wait()
+
+        @pl.when(t < 3)
+        def _():
+            for k in range(2):
+                tall_copy(full_down, 2 * t + 2 + k, (t + 1) % 2 * 2 + k).start()
+
+        @pl.when(t < 4)
+        def _():
+            turn_down(t)
+            for i in range(4):
+
+                @pl.when(t == i)
+                def _(i=i):
+                    rights[1 + i][0].start()
+
+        @pl.when((t >= 3) & (t < 7))
+        def _():
+            broad_copy(full_up, t - 3, (t - 3) % 2).start()
+
+        @pl.when((t >= 4) & (t < 8))
+        def _():
+            turn_up(t - 4)
+
+        @pl.when(t == 7)
+        def _():
+            for k in range(2):
+                tall_copy(full_out, k, k).start()
+            for load in loads[1:]:
+                load.wait()
+
+        @pl.when(t == 8)
+        def _():
+            partial[...] = jnp.zeros_like(partial)
+            each(4, turn_middle)
+            rights[8][0].start()
+
+        @pl.when(t == 9)
+        def _():
+            turn_out()
+
+        @pl.when((t >= 10) & (t < 18))
+        def _():
+            turn_heads(t - 10)
+
+        @pl.when(t == 17)
+        def _():
+            for i in (5, 6, 7):
+                rights[i][0].start()
+
+        @pl.when((t >= 17) & (t < 21))
+        def _():
+            broad_copy(full_qkv, t - 17, (t - 17) % 2).start()
+
+        @pl.when((t >= 18) & (t < 22))
+        def _():
+            turn_in(t - 18)
+
+        @pl.when(t == 22)
+        def _():
+            each(4, turn_rows)
+            small_sent[0] = partial[...]
+            small_copy(0).start()
+            pltpu.make_async_copy(grad_attended, out_rows, held_in.at[0]).start()
+
+        @pl.when(t == 28)
+        def _():
+            pltpu.make_async_copy(grad_attended, out_rows, held_in.at[0]).wait()
+
+    for k in range(2):
+        tall_copy(full_down, k, k).start()
 
     def remote(t, kind, source, target, peer):
         return pltpu.make_async_remote_copy(
@@ -620,14 +778,14 @@
 
     def moved(t, kind):
         source, target, peer = (
-            lambda: (part.at[t, 1, top], from_x.at[t, 0], at_x),
-            lambda: (part.at[t, 3, top], from_x.at[t, 1], at_x),
-            lambda: (part.at[t, 2, bottom], from_y.at[t, 0], at_y),
-            lambda: (part.at[t, 3, bottom], from_y.at[t, 1], at_y),
-            lambda: (part.at[t, 1, bottom], last_x.at[t], at_x),
-            lambda: (part.at[t, 2, top], last_y.at[t], at_y),
-            lambda: (part.at[t, 0], from_pair.at[t], at_pair),
-            lambda: (part.at[t, 0], from_far.at[t], at_far),
+            lambda: (part.at[t % PARTS, 1, top], from_x.at[t, 0], at_x),
+            lambda: (part.at[t % PARTS, 3, top], from_x.at[t, 1], at_x),
+            lambda: (part.at[t % PARTS, 2, bottom], from_y.at[t, 0], at_y),
+            lambda: (part.at[t % PARTS, 3, bottom], from_y.at[t, 1], at_y),
+            lambda: (part.at[t % PARTS, 1, bottom], last_x.at[t], at_x),
+            lambda: (part.at[t % PARTS, 2, top], last_y.at[t], at_y),
+            lambda: (part.at[t % PARTS, 0], from_pair.at[t], at_pair),
+            lambda: (part.at[t % PARTS, 0], from_far.at[t], at_far),
             lambda: (sums.at[t], sums.at[t], at_pair),
         )[kind]()
         return remote(t, kind, source, target, peer)
@@ -642,26 +800,26 @@
                 preferred_element_type=jnp.float32,
             ).astype(jnp.bfloat16)
             for slot in range(4):
-                part[t, slot, :, column : column + 256] = block[slot * BLOCK : (slot + 1) * BLOCK]
+                part[t % PARTS, slot, :, column : column + 256] = block[slot * BLOCK : (slot + 1) * BLOCK]
         for kind in (1, 3, 0, 2):
             moved(t, kind).start()
 
     def stage_turn(t):
         moved(t, 1).wait_recv()
-        add_rows(part.at[t, 2, top], (part.at[t, 2, top], from_x.at[t, 1]), half)
+        add_rows(part.at[t % PARTS, 2, top], (part.at[t % PARTS, 2, top], from_x.at[t, 1]), half)
         moved(t, 5).start()
         moved(t, 3).wait_recv()
-        add_rows(part.at[t, 1, bottom], (part.at[t, 1, bottom], from_y.at[t, 1]), half)
+        add_rows(part.at[t % PARTS, 1, bottom], (part.at[t % PARTS, 1, bottom], from_y.at[t, 1]), half)
         moved(t, 4).start()
 
     def stage_plane(t):
         moved(t, 0).wait_recv()
         moved(t, 5).wait_recv()
-        add_rows(part.at[t, 0, top], (part.at[t, 0, top], from_x.at[t, 0], last_y.at[t]), half)
+        add_rows(part.at[t % PARTS, 0, top], (part.at[t % PARTS, 0, top], from_x.at[t, 0], last_y.at[t]), half)
         moved(t, 2).wait_recv()
         moved(t, 4).wait_recv()
         add_rows(
-            part.at[t, 0, bottom], (part.at[t, 0, bottom], from_y.at[t, 0], last_x.at[t]), half
+            part.at[t % PARTS, 0, bottom], (part.at[t % PARTS, 0, bottom], from_y.at[t, 0], last_x.at[t]), half
         )
 
         @pl.when(outer)
@@ -672,14 +830,14 @@
         @pl.when(inner)
         def _():
             moved(t, 6).wait_recv()
-            add_rows(part.at[t, 0], (part.at[t, 0], from_pair.at[t]), BLOCK)
+            add_rows(part.at[t % PARTS, 0], (part.at[t % PARTS, 0], from_pair.at[t]), BLOCK)
             moved(t, 7).start()
 
     def stage_far(t):
         @pl.when(inner)
         def _():
             moved(t, 7).wait_recv()
-            add_rows(sums.at[t], (part.at[t, 0], from_far.at[t]), BLOCK)
+            add_rows(sums.at[t], (part.at[t % PARTS, 0], from_far.at[t]), BLOCK)
             moved(t, 8).start()
 
     def stage_end(t):
@@ -702,8 +860,8 @@
         for low, high, target in (
             (0, 8, lambda i: out_down.at[pl.ds(pl.multiple_of(i // 2 * BLOCK, BLOCK), BLOCK), columns(i % 2)]),
             (8, 16, lambda i: out_up.at[:, columns(i)]),
-            (16, 22, lambda i: out_qkv.at[:, columns(i)]),
-            (22, 24, lambda i: out_out.at[:, columns(i)]),
+            (16, 18, lambda i: out_out.at[:, columns(i)]),
+            (18, 24, lambda i: out_qkv.at[:, columns(i)]),
         ):
 
             @pl.when((t >= low) & (t < high))
@@ -729,8 +887,6 @@
             device_id_type=MESH,
         )
 
-    small_sent[0] = small[...]
-    small_copy(0).start()
     stages = (stage_turn, stage_plane, stage_pair, stage_far, stage_end, stage_stored)
 
     def tick(t, carry):
@@ -752,6 +908,7 @@
         def _():
             stage_product(t)
 
+        work(t)
         for lag, stage in zip(LAGS, stages):
 
             @pl.when((t >= lag) & (t < CHUNKS + lag))
@@ -760,7 +917,7 @@
 
         for j in range(5):
 
-            @pl.when(t == j)
+            @pl.when(t == 23 + j)
             def _(j=j):
                 small_copy(j).wait()
                 total = small_sent[j] + small_got[j]
@@ -775,50 +932,61 @@
     lax.fori_loop(0, CHUNKS + LAGS[-1], tick, 0)
 
 
-def reduce_gradients(lefts, rights, small):
-    rows = lefts[0].shape[0]
-    bf16, dma = jnp.bfloat16, pltpu.SemaphoreType.DMA
+def run_backward(lefts, grad_mlp, sources, weights, positions, documents, router, gain_one, gain_two):
+    rows = grad_mlp.shape[0]
+    bf16, f32, dma = jnp.bfloat16, jnp.float32, pltpu.SemaphoreType.DMA
+    chunk, half_chunk = (CHUNKS, BLOCK, WIDE), (CHUNKS, BLOCK // 2, WIDE)
+    held = [
+        ((LEFTS, 2 * rows, 4 * BLOCK), bf16),
+        ((RIGHTS, 2 * rows, FULL), bf16),
+        ((PARTS, 4, BLOCK, WIDE), bf16),
+        ((CHUNKS, 2, BLOCK // 2, WIDE), bf16),
+        ((CHUNKS, 2, BLOCK // 2, WIDE), bf16),
+        (half_chunk, bf16),
+        (half_chunk, bf16),
+        (chunk, bf16),
+        (chunk, bf16),
+        (chunk, bf16),
+    ]
+    held += [(source.shape, source.dtype) for source in sources]
+    held += [
+        ((4, 512, FULL), bf16),
+        ((2, 256, 4 * FULL), bf16),
+        ((rows, FULL), f32),
+        ((rows, FULL), f32),
+        ((rows, FULL), bf16),
+        ((8, FULL), f32),
+        ((5, 8, FULL), f32),
+        ((5, 8, FULL), f32),
+    ]
+    counts = [(LEFTS, 4)] * 3 + [(RIGHTS,)] * 3 + [(CHUNKS, 9)] * 2 + [(5,)] * 2
+    counts += [(CHUNKS,), (7,), (4,), (2,)]
+    shapes = [(4 * BLOCK, FULL), (BLOCK, 4 * FULL), (BLOCK, 3 * FULL), (BLOCK, FULL), (rows, FULL)]
     return pl.pallas_call(
         reduce_kernel,
-        out_shape=[
-            jax.ShapeDtypeStruct((4 * BLOCK, FULL), bf16),
-            jax.ShapeDtypeStruct((BLOCK, 4 * FULL), bf16),
-            jax.ShapeDtypeStruct((BLOCK, 3 * FULL), bf16),
-            jax.ShapeDtypeStruct((BLOCK, FULL), bf16),
-            jax.ShapeDtypeStruct(small.shape, jnp.float32),
-        ],
-        in_specs=[pl.BlockSpec(memory_space=ANY)] * 8 + [pl.BlockSpec(memory_space=pltpu.VMEM)],
-        out_specs=[pl.BlockSpec(memory_space=ANY)] * 4 + [pl.BlockSpec(memory_space=pltpu.VMEM)],
-        scratch_shapes=[
-            pltpu.VMEM((LEFTS, 2 * rows, 4 * BLOCK), bf16),
-            pltpu.VMEM((RIGHTS, 2 * rows, FULL), bf16),
-            pltpu.VMEM((CHUNKS, 4, BLOCK, WIDE), bf16),
-            pltpu.VMEM((CHUNKS, 2, BLOCK // 2, WIDE), bf16),
-            pltpu.VMEM((CHUNKS, 2, BLOCK // 2, WIDE), bf16),
-            pltpu.VMEM((CHUNKS, BLOCK // 2, WIDE), bf16),
-            pltpu.VMEM((CHUNKS, BLOCK // 2, WIDE), bf16),
-            pltpu.VMEM((CHUNKS, BLOCK, WIDE), bf16),
-            pltpu.VMEM((CHUNKS, BLOCK, WIDE), bf16),
-            pltpu.VMEM((5,) + small.shape, jnp.float32),
-            pltpu.VMEM((5,) + small.shape, jnp.float32),
-            dma((LEFTS, 4)),
-            dma((LEFTS, 4)),
-            dma((LEFTS, 4)),
-            dma((RIGHTS,)),
-            dma((RIGHTS,)),
-            dma((RIGHTS,)),
-            dma((CHUNKS, 9)),
-            dma((CHUNKS, 9)),
-            dma((5,)),
-            dma((5,)),
-            pltpu.VMEM((CHUNKS, BLOCK, WIDE), bf16),
-            dma((CHUNKS,)),
-        ],
+        out_shape=[jax.ShapeDtypeStruct(shape, bf16) for shape in shapes]
+        + [jax.ShapeDtypeStruct((8, FULL), f32)],
+        in_specs=[pl.BlockSpec(memory_space=ANY)] * 16
+        + [pl.BlockSpec(memory_space=pltpu.VMEM)] * 7,
+        out_specs=[pl.BlockSpec(memory_space=ANY)] * 5 + [pl.BlockSpec(memory_space=pltpu.VMEM)],
+        scratch_shapes=[pltpu.VMEM(*each_one) for each_one in held] + [dma(count) for count in counts],
         compiler_params=pltpu.CompilerParams(
-            collective_id=2, has_side_effects=True, vmem_limit_bytes=60 * 1024 * 1024
+            collective_id=2, has_side_effects=True, vmem_limit_bytes=62 * 1024 * 1024
         ),
-        name="reduce_gradients",
-    )(*lefts, *rights, small)
+        name="backward_and_reduce",
+    )(
+        *lefts,
+        grad_mlp,
+        *sources,
+        *weights,
+        positions[:, None],
+        positions[None],
+        documents[:, None],
+        documents[None],
+        router[None],
+        gain_one[None],
+        gain_two[None],
+    )
 
 
 def put_rows(tokens, rows, positions):
@@ -861,59 +1029,19 @@
         gain_one,
         gain_two,
     )
-    row_count = routed.shape[0]
     output = put_rows(hidden, rows_out, positions)
-    grad_score = score[:, 0]
-    heads = packed.reshape(row_count, 3, HEADS, HEAD)
-    allowed = (documents[:, None] == documents[None, :]) & (
-        positions[None, :] <= positions[:, None]
-    )
-    scores = (
-        jnp.einsum("qhd,khd->hqk", heads[:, 0], heads[:, 1], preferred_element_type=jnp.float32)
-        * 0.125
-    )
-    prob_rows = jax.nn.softmax(jnp.where(allowed[None], scores, -1000000000.0), axis=-1)
-    prob_low = prob_rows.astype(jnp.bfloat16)
-    grad_act = jnp.dot(grad_mlp, full_down.T, preferred_element_type=jnp.float32)
-    grad_up_in = (grad_act * slope).astype(jnp.bfloat16)
-    grad_norm_mid = jnp.dot(grad_up_in, full_up.T, preferred_element_type=jnp.float32)
-    _, second_pull = jax.vjp(rms_scale, middle, gain_two)
-    grad_middle, grad_gain_two = second_pull(grad_norm_mid)
-    grad_attn = (grad_branch + grad_middle).astype(jnp.bfloat16)
-    grad_attended = jnp.dot(grad_attn, full_out.T, preferred_element_type=jnp.float32).astype(
-        jnp.bfloat16
-    )
-    grad_attended = grad_attended.reshape(row_count, HEADS, HEAD)
-    grad_prob = jnp.einsum(
-        "qhd,khd->hqk", grad_attended, heads[:, 2], preferred_element_type=jnp.float32
-    )
-    grad_value = jnp.einsum(
-        "hqk,qhd->khd", prob_low, grad_attended, preferred_element_type=jnp.float32
-    )
-    row_dot = jnp.sum(grad_prob * prob_rows, axis=-1, keepdims=True)
-    grad_scores = (prob_rows * (grad_prob - row_dot)).astype(jnp.bfloat16)
-    grad_query = (
-        jnp.einsum("hqk,khd->qhd", grad_scores, heads[:, 1], preferred_element_type=jnp.float32)
-        * 0.125
-    )
-    grad_key = (
-        jnp.einsum("hqk,qhd->khd", grad_scores, heads[:, 0], preferred_element_type=jnp.float32)
-        * 0.125
-    )
-    grad_packed = jnp.stack([grad_query, grad_key, grad_value], axis=1).reshape(row_count, 3 * D)
-    grad_packed = grad_packed.astype(jnp.bfloat16)
-    grad_norm_in = jnp.dot(grad_packed, full_qkv.T, preferred_element_type=jnp.float32)
-    _, first_pull = jax.vjp(rms_scale, routed, gain_one)
-    grad_routed, grad_gain_one = first_pull(grad_norm_in)
-    grad_routed = grad_routed + grad_middle + grad_score[:, None] * router[None, :]
-    grad_router = jnp.dot(grad_score, routed, precision=lax.Precision.HIGHEST)
-    grad_hidden = put_rows(cotangent, (taken.astype(jnp.float32) + grad_routed).astype(jnp.bfloat16), positions)
-    small = jnp.stack([grad_router, grad_gain_one, grad_gain_two] + [jnp.zeros_like(grad_router)] * 5)
-    *sums, small_sums = reduce_gradients(
+    *sums, grad_rows, small_sums = run_backward(
         (activated, normed_mid, normed_in, attended),
-        (grad_mlp, grad_up_in, grad_packed, grad_attn),
-        small,
-    )
+        grad_mlp,
+        (slope, packed, middle, routed, taken, grad_branch, score),
+        (full_qkv, full_out, full_up, full_down),
+        positions,
+        documents,
+        router,
+        gain_one,
+        gain_two,
+    )
+    grad_hidden = put_rows(cotangent, grad_rows, positions)
     sum_down, sum_up, sum_qkv, sum_out = (total.astype(jnp.float32) for total in sums)
     return (
         output,

time: 292 us -> 244 us (0.84)
  matrix products: 34.8 us -> 7.41 us
  local copies, waits for them, and re-layouts: 13.3 us -> 4.45 us
  other arithmetic: 11.4 us -> 5.6 us
  Pallas kernels: 231 us -> 226 us
    dot_general x10 -> x0, matrix products: 23.9 us -> none  [the longest x1 7.03 us: per_device(): jnp.dot(grad_mlp, full_down.T, preferred_element_type=jnp.float32)]
    pallas_call x1, Pallas kernels: 138 us -> 132 us  [run_backward(): pl.pallas_call(reduce_kernel, out_shape=[jax.ShapeDtypeStruct(shape, bf16...]
    convert_element_type x2 -> x0, local copies, waits for them, and re-layouts: 3.77 us -> none  [the longest x1 2.04 us: per_device(): jnp.dot(grad_attn, full_out.T, preferred_element_type=jnp.float32)]
    dot_general x2, matrix products: 10.8 us -> 7.41 us  [put_rows(): jnp.dot(hit.astype(jnp.bfloat16), rows, preferred_element_type=jnp.float32)]
where the time goes in v5:
time: 244 us
  Pallas kernels  226 us (93%)
  matrix products  7.41 us (3%)
  other arithmetic  5.6 us (2%)
  local copies, waits for them, and re-layouts  4.45 us (2%)
    pallas_call x1, Pallas kernels, run_backward(): pl.pallas_call(reduce_kernel, out_shape=[jax.ShapeDtypeStruct(shape, bf16...  132 us
    pallas_call x1, Pallas kernels, run_forward(): pl.pallas_call(forward_kernel, out_shape=[jax.ShapeDtypeStruct(*each_one)...  93.5 us
    dot_general x2, matrix products, put_rows(): jnp.dot(hit.astype(jnp.bfloat16), rows, preferred_element_type=jnp.float32)  7.41 us
    convert_element_type x4, other arithmetic, per_device(): total.astype(jnp.float32)  5.25 us

profile of v5, /device:TPU:0, one launch (start us, length us, event | category | flops | bytes accessed | tf_op | source)
XLA Modules:
  0.0 243.9 jit_solution(1835886678280885668)
XLA Ops:
  0.6 1.5 copy.24.refs_6_.refs_16_
  2.1 1.5 copy.25.refs_8_.refs_18_
  3.6 93.5 %gather_and_forward.1 = (bf16[1024,3072]{1,0:T(8,128)(2,1)}, bf16[1024,1024]{1,0:T(8,128)(2,1)}, bf16[1024,4096]{1,0:T(8,128)(2,1)}, bf16[4096,1024]{1,0:T(8,128...) custom-call(bf16[128,3072]{1,0:T(8,128)(2,1)} %refs_0_.1, ...), custom_call_target="tpu_custom_call" | custom-call | tf_op jit(solution)/shard_map/gather_and_forward/pallas_call | solution.py:466
  97.1 0.0 copy-start.5
  97.1 132.3 %backward_and_reduce.1 = (bf16[512,1024]{1,0:T(8,128)(2,1)}, bf16[128,4096]{1,0:T(8,128)(2,1)}, bf16[128,3072]{1,0:T(8,128)(2,1)}, bf16[128,1024]{1,0:T(8,128)(2...) custom-call(bf16[256,4096]{1,0:T(8,128)(2,1)} %get-tuple-element.33.refs_0_, ...), custom_call_target="tpu_custom_call" | custom-call | tf_op jit(solution)/shard_map/backward_and_reduce/pallas_call | solution.py:965
  229.4 0.0 copy-done.5
  229.4 0.4 fusion
  229.7 0.0 copy-start.2
  229.7 0.0 copy-start.1
  229.7 4.6 %convert_select_fusion = bf16[2048,1024]{1,0:T(8,128)(2,1)} fusion(bf16[2048,1024]{1,0:T(8,128)(2,1)} %refs_5_.1, pred[2048]{0:T(1024)(128)(4,1)S(1)} %fusion, bf16[256,1024]{1,0:T(8,128)(2,1)} %get-tuple-element.49, s32[256]{0:T(256)S(1)} %bitcast.20), kind=kOutput, calls=%fused_computation | convolution fusion | flops 1078460416 | bytes 8915968 | tf_op jit(solution)/shard_map/dot_general | solution.py:994
  234.3 0.0 copy-start.3
  234.4 0.0 copy-done.2
  234.4 0.0 copy-start.4
  234.4 0.0 copy-start
  234.4 0.0 copy-start.6
  234.4 1.5 convert_element_type.24
  235.9 0.0 copy-done.1
  235.9 1.6 convert_element_type.25
  237.5 0.0 copy-done.3
  237.5 1.3 convert_element_type.22
  238.8 0.0 copy-done.4
  238.8 0.8 convert_element_type.23
  239.6 1.5 fusion.3
  241.1 0.0 copy-done
  241.1 0.0 copy-done.6
  241.1 2.8 %convert_select_fusion.1 = bf16[2048,1024]{1,0:T(8,128)(2,1)} fusion(bf16[2048,1024]{1,0:T(8,128)(2,1)S(1)} %copy-done, pred[2048]{0:T(1024)(128)(4,1)S(1)} %fusion, bf16[256,1024]{1,0:T(8,128)(2,1)S(1)} %copy-done.6, s32[256]{0:T(256)S(1)} %bitcast.21), kind=kOutput, calls=%fused_computation.1 | convolution fusion | flops 1078460416 | bytes 8915968 | tf_op jit(solution)/shard_map/dot_general | solution.py:994
Async XLA Ops:
  97.1 132.3 %copy-start.5 = (s32[1,256]{1,0:T(1,128)S(1)}, s32[1,256]{1,0:T(1,128)}, u32[]{:S(2)}) copy-start(s32[1,256]{1,0:T(1,128)} %refs_17_.1) | copy-start | bytes 3076
  229.7 4.6 %copy-start.2 = (bf16[128,4096]{1,0:T(8,128)(2,1)S(1)}, bf16[128,4096]{1,0:T(8,128)(2,1)}, u32[]{:S(2)}) copy-start(bf16[128,4096]{1,0:T(8,128)(2,1)} %get-tuple-element.52) | copy-start | bytes 3145732
  229.7 6.2 %copy-start.1 = (bf16[512,1024]{1,0:T(8,128)(2,1)S(1)}, bf16[512,1024]{1,0:T(8,128)(2,1)}, u32[]{:S(2)}) copy-start(bf16[512,1024]{1,0:T(8,128)(2,1)} %get-tuple-element.53) | copy-start | bytes 3145732
  234.3 3.1 %copy-start.3 = (bf16[128,3072]{1,0:T(8,128)(2,1)S(1)}, bf16[128,3072]{1,0:T(8,128)(2,1)}, u32[]{:S(2)}) copy-start(bf16[128,3072]{1,0:T(8,128)(2,1)} %get-tuple-element.50) | copy-start | bytes 2359300
  234.4 4.4 %copy-start.4 = (bf16[128,1024]{1,0:T(8,128)(2,1)S(1)}, bf16[128,1024]{1,0:T(8,128)(2,1)}, u32[]{:S(2)}) copy-start(bf16[128,1024]{1,0:T(8,128)(2,1)} %get-tuple-element.51) | copy-start | bytes 786436
  234.4 6.8 %copy-start = (bf16[2048,1024]{1,0:T(8,128)(2,1)S(1)}, bf16[2048,1024]{1,0:T(8,128)(2,1)}, u32[]{:S(2)}) copy-start(bf16[2048,1024]{1,0:T(8,128)(2,1)} %refs_4_.1) | copy-start | bytes 12582916
  234.4 6.7 %copy-start.6 = (bf16[256,1024]{1,0:T(8,128)(2,1)S(1)}, bf16[256,1024]{1,0:T(8,128)(2,1)}, u32[]{:S(2)}) copy-start(bf16[256,1024]{1,0:T(8,128)(2,1)} %get-tuple-element.32) | copy-start | bytes 1572868

commit v6 on v5

--- a/solution.py
+++ b/solution.py
@@ -219,6 +219,10 @@
     return lax.rsqrt(jnp.mean(values * values, axis=-1, keepdims=True) + EPSILON)
 
 
+def upright(row):
+    return jnp.broadcast_to(row.astype(jnp.float32), (128, row.shape[1])).T.astype(jnp.int32)
+
+
 def lane_half(shape):
     return lax.broadcasted_iota(jnp.int32, shape, 1) < HEAD
 
@@ -231,12 +235,13 @@
 
 def forward_kernel(*refs):
     shards = refs[0:4]
-    hidden, cotangent, pos_col, pos_row, doc_col, doc_row, router, gain_one, gain_two = refs[4:13]
-    outs = refs[13:30]
-    fulls = refs[30:34]
-    (tokens, cotokens, hit, routed, taken, normed_in, packed, attended, attn_out, middle) = refs[34:44]
-    (normed_mid, slope, activated, grad_mlp, grad_branch, rows_out, score, gate) = refs[44:52]
-    own_in, token_in, out_sem, send, recv = refs[52:57]
+    hidden, cotangent, pos_row, doc_row, router, gain_one, gain_two = refs[4:11]
+    outs = refs[11:28]
+    fulls = refs[28:31] + (outs[3],)
+    (tokens, cotokens, hit, routed, taken, normed_in, packed, attended, attn_out, middle) = refs[31:41]
+    (normed_mid, slope, activated, grad_mlp, grad_branch, gate) = refs[41:47]
+    kept_down, pos_col, doc_col = refs[47:50]
+    own_in, token_in, out_sem, send, recv = refs[50:55]
     z, f, core, along_x, along_y, across = places()
     pair = flip(z, 1)
     at_core, at_x, at_y, at_z = (z, core), (z, along_x), (z, along_y), (pair, f)
@@ -306,10 +311,14 @@
             plan[w][onward].start()
 
     def finish(w):
-        loads[w].wait()
+        if w < 3:
+            loads[w].wait()
+        else:
+            store_down.wait()
         for kind in (2,) + tuple(range(7, GATHER_KINDS)):
             plan[w][kind].wait_recv()
-        put(w, fulls[w])
+        if w < 3:
+            put(w, fulls[w])
 
     def put(i, source):
         pltpu.make_async_copy(source, outs[i], out_sem.at[i]).start()
@@ -317,24 +326,26 @@
     def settle(i, source):
         pltpu.make_async_copy(source, outs[i], out_sem.at[i]).wait()
 
+    own_places = [fulls[w].at[rows_of(w, f, 0, shards[w].shape[0])] for w in range(4)]
     loads = [
-        pltpu.make_async_copy(
-            shards[w], fulls[w].at[rows_of(w, f, 0, shards[w].shape[0])], own_in.at[w]
-        )
+        pltpu.make_async_copy(shards[w], kept_down if w == 3 else own_places[w], own_in.at[w])
         for w in range(4)
     ]
+    store_down = pltpu.make_async_copy(kept_down, own_places[3], own_in.at[4])
     token_loads = [
         pltpu.make_async_copy(hidden, tokens, token_in.at[0]),
         pltpu.make_async_copy(cotangent, cotokens, token_in.at[1]),
     ]
+    first(1)
     first(0)
-    first(1)
     for load in token_loads + loads:
         load.start()
+    pos_col[...] = upright(pos_row[...])
+    doc_col[...] = upright(doc_row[...])
 
     def mark(i):
         slots = lax.broadcasted_iota(jnp.int32, (part, hit.shape[1]), 1)
-        hit[tile(i, part)] = (slots == pos_col[tile(i, part)]).astype(jnp.bfloat16)
+        hit[tile(i, part)] = (slots == pos_col[tile(i, part), 0:1]).astype(jnp.bfloat16)
 
     each(4, mark)
 
@@ -354,7 +365,7 @@
         rows = routed[at]
         normed_in[at] = (rows * inverse_size(rows) * gain_one[...]).astype(jnp.bfloat16)
         router_out = jnp.sum(rows * router[...], axis=-1, keepdims=True)
-        gate_rows = jnp.where(doc_col[at] < 2, router_out, 0.0)
+        gate_rows = jnp.where(doc_col[at, 0:1] < 2, router_out, 0.0)
         gate[at] = jnp.broadcast_to(gate_rows, (part, 128))
         grad_rows = taken[at].astype(jnp.float32) * gate_rows
         grad_branch[at] = grad_rows
@@ -363,10 +374,16 @@
     each(4, open_rows)
     for i, source in ((4, routed), (5, taken), (6, normed_in), (13, grad_mlp), (14, grad_branch)):
         put(i, source)
+    put(16, gate)
+    loads[3].wait()
+    store_down.start()
+    second(1)
+    first(2)
     second(0)
-    first(2)
-    second(1)
     first(3)
+    second(2)
+    third(1)
+    finish(1)
     third(0)
     finish(0)
 
@@ -375,11 +392,10 @@
 
     each(6, pack)
     put(7, packed)
-    second(2)
 
     def attend(i):
         query, keys, values = (packed[:, tile(i + 8 * k, 128)] for k in range(3))
-        allowed = (doc_col[...] == doc_row[...]) & (pos_row[...] <= pos_col[...])
+        allowed = (doc_col[:, 0:1] == doc_row[...]) & (pos_row[...] <= pos_col[:, 0:1])
         low = lane_half(query.shape)
         zero = jnp.zeros_like(query)
         mixed = [
@@ -388,10 +404,10 @@
         ]
         attended[:, tile(i, 128)] = jnp.where(low, mixed[0], mixed[1]).astype(jnp.bfloat16)
 
-    each(HEADS // 2, attend)
+    each(HEADS // 4, attend)
+    second(3)
+    each(HEADS // 4, lambda i: attend(i + HEADS // 4))
     put(8, attended)
-    third(1)
-    finish(1)
 
     def project(n):
         attn_out[:, tile(n, 256)] = dot(attended[...], fulls[1][:, tile(n, 256)])
@@ -406,8 +422,8 @@
 
     each(4, middle_rows)
     put(9, middle)
+    put(15, attn_out)
     put(10, normed_mid)
-    second(3)
     third(2)
     finish(2)
 
@@ -426,26 +442,10 @@
     third(3)
     finish(3)
 
-    def lower(n):
-        at = tile(n, 256)
-        attn_out[:, at] = attn_out[:, at] + dot(activated[...], fulls[3][:, at])
-
-    each(4, lower)
-
-    def close_rows(i):
-        at = tile(i, part)
-        branch = attn_out[at]
-        rows_out[at] = (routed[at] + gate[at, 0:1] * branch).astype(jnp.bfloat16)
-        grad_add = jnp.where(doc_col[at] < 2, taken[at].astype(jnp.float32), 0.0)
-        total = jnp.sum(grad_add * branch, axis=-1, keepdims=True)
-        score[at] = jnp.broadcast_to(total, (part, 128))
-
-    each(4, close_rows)
-    put(15, rows_out)
-    put(16, score)
     kept = (routed, taken, normed_in, packed, attended, middle, normed_mid, activated, slope)
-    for i, source in enumerate(tuple(fulls) + kept + (grad_mlp, grad_branch, rows_out, score)):
-        settle(i, source)
+    for i, source in enumerate(fulls + kept + (grad_mlp, grad_branch, attn_out, gate)):
+        if i != 3:
+            settle(i, source)
     for w in range(4):
         for kind in range(GATHER_KINDS):
             plan[w][kind].wait_send()
@@ -457,20 +457,20 @@
     full = [((w.shape[0] * parts, w.shape[1]), w.dtype) for w in weights]
     row, head_row, wide_row = (count, D), (count, 3 * D), (count, wide)
     kept = [(row, f32), (row, bf16), (row, bf16), (head_row, bf16), (row, bf16), (row, f32)]
-    kept += [(row, bf16), (wide_row, bf16), (wide_row, f32), (row, bf16), (row, f32), (row, bf16)]
+    kept += [(row, bf16), (wide_row, bf16), (wide_row, f32), (row, bf16), (row, f32), (row, f32)]
     kept += [((count, 128), f32)]
     held = [(hidden.shape, bf16)] * 2 + [((count, hidden.shape[0]), bf16), (row, f32), (row, bf16)]
     held += [(row, bf16), (head_row, bf16), (row, bf16), (row, f32), (row, f32), (row, bf16)]
-    held += [(wide_row, f32), (wide_row, bf16), (row, bf16), (row, f32), (row, bf16)]
-    held += [((count, 128), f32)] * 2
+    held += [(wide_row, f32), (wide_row, bf16), (row, bf16), (row, f32)]
+    held += [((count, 128), f32), (weights[3].shape, bf16)] + [((count, 128), jnp.int32)] * 2
     return pl.pallas_call(
         forward_kernel,
         out_shape=[jax.ShapeDtypeStruct(*each_one) for each_one in full + kept],
         in_specs=[pl.BlockSpec(memory_space=ANY)] * 6
-        + [pl.BlockSpec(memory_space=pltpu.VMEM)] * 7,
+        + [pl.BlockSpec(memory_space=pltpu.VMEM)] * 5,
         out_specs=[pl.BlockSpec(memory_space=ANY)] * 17,
-        scratch_shapes=[pltpu.VMEM(*each_one) for each_one in full + held]
-        + [dma((4,)), dma((2,)), dma((17,)), dma((4, GATHER_KINDS)), dma((4, GATHER_KINDS))],
+        scratch_shapes=[pltpu.VMEM(*each_one) for each_one in full[:3] + held]
+        + [dma((5,)), dma((2,)), dma((17,)), dma((4, GATHER_KINDS)), dma((4, GATHER_KINDS))],
         compiler_params=pltpu.CompilerParams(
             collective_id=1, has_side_effects=True, vmem_limit_bytes=60 * 1024 * 1024
         ),
@@ -479,9 +479,7 @@
         *weights,
         hidden,
         cotangent,
-        positions[:, None],
         positions[None],
-        documents[:, None],
         documents[None],
         router[None],
         gain_one[None],
@@ -521,16 +519,16 @@
 
 def reduce_kernel(*refs):
     activated, normed_mid, normed_in, attended, grad_mlp = refs[:5]
-    sources, weights = refs[5:12], refs[12:16]
-    pos_col, pos_row, doc_col, doc_row, router, gain_one, gain_two = refs[16:23]
-    out_down, out_up, out_qkv, out_out, out_rows, small_sums = refs[23:29]
+    sources, weights = refs[5:13] + refs[0:1], refs[13:17]
+    pos_row, doc_row, router, gain_one, gain_two = refs[17:22]
+    out_down, out_up, out_qkv, out_out, out_first, out_rows, small_sums = refs[22:29]
     (left, right, part, from_x, from_y, last_x, last_y, from_pair, from_far, sums) = refs[29:39]
-    held = refs[39:46]
-    slope, packed, middle, routed, taken, grad_branch, score = held
-    (tall, broad, grad_norm, grad_middle, grad_attended, partial) = refs[46:52]
-    small_sent, small_got = refs[52:54]
-    (in_own, in_send, in_recv, rin_own, rin_send, rin_recv) = refs[54:60]
-    send, recv, small_send, small_recv, stored, held_in, tall_in, broad_in = refs[60:68]
+    held = refs[39:48]
+    slope, branch, packed, middle, routed, taken, grad_branch, gate, wide = held
+    (tall, broad, grad_norm, grad_middle, grad_attended, partial) = refs[48:54]
+    small_sent, small_got, score, pos_col, doc_col = refs[54:59]
+    (in_own, in_send, in_recv, rin_own, rin_send, rin_recv) = refs[59:65]
+    send, recv, small_send, small_recv, stored, held_in, tall_in, broad_in = refs[65:73]
     full_qkv, full_out, full_up, full_down = weights
 
     z, f, core, along_x, along_y, across = places()
@@ -602,9 +600,11 @@
         for copy in rights[0] if t == 0 else ():
             copy.start()
 
-    loads = [pltpu.make_async_copy(sources[i], held[i], held_in.at[i]) for i in range(7)]
-    for load in loads:
-        load.start()
+    loads = [pltpu.make_async_copy(sources[i], held[i], held_in.at[i]) for i in range(9)]
+    for i in (0, 8, 1, 2, 3, 4, 5, 6, 7):
+        loads[i].start()
+    pos_col[...] = upright(pos_row[...])
+    doc_col[...] = upright(doc_row[...])
 
     def tall_copy(source, j, slot):
         return pltpu.make_async_copy(source.at[tile(j, 512)], tall.at[slot], tall_in.at[slot])
@@ -621,6 +621,7 @@
             grown = dot(right[0, mine], tall[slot], ((1,), (1,)))
             grown = grown * slope[:, tile(2 * t + k, 512)]
             right[t + 1, mine, at] = grown.astype(jnp.bfloat16)
+            branch[...] += dot(wide[:, tile(2 * t + k, 512)], tall[slot])
 
     def turn_up(t):
         slot = t % 2
@@ -644,7 +645,13 @@
         lower = pl.ds(pl.multiple_of((f % 2) * rows + i * 64, 64), 64)
         right[8, lower] = (grad_branch[at] + back).astype(jnp.bfloat16)
         partial[2:3] += gain_part
-        partial[0:1] += jnp.sum(score[at, 0:1] * routed[at], axis=0, keepdims=True)
+        added = branch[at]
+        rows_at = routed[at]
+        grad_attended[at] = (rows_at + gate[at, 0:1] * added).astype(jnp.bfloat16)
+        grad_add = jnp.where(doc_col[at, 0:1] < 2, taken[at].astype(jnp.float32), 0.0)
+        grad_score = jnp.sum(grad_add * added, axis=-1, keepdims=True)
+        score[at] = jnp.broadcast_to(grad_score, (64, 128))
+        partial[0:1] += jnp.sum(grad_score * rows_at, axis=0, keepdims=True)
 
     def turn_out():
         for k in range(2):
@@ -656,7 +663,7 @@
     def turn_heads(i):
         query, keys, values = (packed[:, tile(i + 8 * k, 128)] for k in range(3))
         ahead = grad_attended[:, tile(i, 128)]
-        allowed = (doc_col[...] == doc_row[...]) & (pos_row[...] <= pos_col[...])
+        allowed = (doc_col[:, 0:1] == doc_row[...]) & (pos_row[...] <= pos_col[:, 0:1])
         low = lane_half(query.shape)
         zero = jnp.zeros_like(query)
         found = []
@@ -694,7 +701,8 @@
     def work(t):
         @pl.when(t == 0)
         def _():
-            loads[0].wait()
+            for i in (0, 8, 1):
+                loads[i].wait()
 
         @pl.when(t < 3)
         def _():
@@ -722,7 +730,7 @@
         def _():
             for k in range(2):
                 tall_copy(full_out, k, k).start()
-            for load in loads[1:]:
+            for load in loads[2:8]:
                 load.wait()
 
         @pl.when(t == 8)
@@ -730,9 +738,11 @@
             partial[...] = jnp.zeros_like(partial)
             each(4, turn_middle)
             rights[8][0].start()
+            pltpu.make_async_copy(grad_attended, out_first, held_in.at[1]).start()
 
         @pl.when(t == 9)
         def _():
+            pltpu.make_async_copy(grad_attended, out_first, held_in.at[1]).wait()
             turn_out()
 
         @pl.when((t >= 10) & (t < 18))
@@ -948,7 +958,7 @@
         (chunk, bf16),
         (chunk, bf16),
     ]
-    held += [(source.shape, source.dtype) for source in sources]
+    held += [(source.shape, source.dtype) for source in (*sources, lefts[0])]
     held += [
         ((4, 512, FULL), bf16),
         ((2, 256, 4 * FULL), bf16),
@@ -958,17 +968,20 @@
         ((8, FULL), f32),
         ((5, 8, FULL), f32),
         ((5, 8, FULL), f32),
+        ((rows, 128), f32),
+        ((rows, 128), jnp.int32),
+        ((rows, 128), jnp.int32),
     ]
     counts = [(LEFTS, 4)] * 3 + [(RIGHTS,)] * 3 + [(CHUNKS, 9)] * 2 + [(5,)] * 2
-    counts += [(CHUNKS,), (7,), (4,), (2,)]
-    shapes = [(4 * BLOCK, FULL), (BLOCK, 4 * FULL), (BLOCK, 3 * FULL), (BLOCK, FULL), (rows, FULL)]
+    counts += [(CHUNKS,), (9,), (4,), (2,)]
+    shapes = [(4 * BLOCK, FULL), (BLOCK, 4 * FULL), (BLOCK, 3 * FULL), (BLOCK, FULL)] + [(rows, FULL)] * 2
     return pl.pallas_call(
         reduce_kernel,
         out_shape=[jax.ShapeDtypeStruct(shape, bf16) for shape in shapes]
         + [jax.ShapeDtypeStruct((8, FULL), f32)],
-        in_specs=[pl.BlockSpec(memory_space=ANY)] * 16
-        + [pl.BlockSpec(memory_space=pltpu.VMEM)] * 7,
-        out_specs=[pl.BlockSpec(memory_space=ANY)] * 5 + [pl.BlockSpec(memory_space=pltpu.VMEM)],
+        in_specs=[pl.BlockSpec(memory_space=ANY)] * 17
+        + [pl.BlockSpec(memory_space=pltpu.VMEM)] * 5,
+        out_specs=[pl.BlockSpec(memory_space=ANY)] * 6 + [pl.BlockSpec(memory_space=pltpu.VMEM)],
         scratch_shapes=[pltpu.VMEM(*each_one) for each_one in held] + [dma(count) for count in counts],
         compiler_params=pltpu.CompilerParams(
             collective_id=2, has_side_effects=True, vmem_limit_bytes=62 * 1024 * 1024
@@ -979,9 +992,7 @@
         grad_mlp,
         *sources,
         *weights,
-        positions[:, None],
         positions[None],
-        documents[:, None],
         documents[None],
         router[None],
         gain_one[None],
@@ -1016,8 +1027,8 @@
         slope,
         grad_mlp,
         grad_branch,
-        rows_out,
-        score,
+        attn_out,
+        gate,
     ) = run_forward(
         (w_qkv, w_out, w_up, w_down),
         8,
@@ -1029,11 +1040,10 @@
         gain_one,
         gain_two,
     )
-    output = put_rows(hidden, rows_out, positions)
-    *sums, grad_rows, small_sums = run_backward(
+    *sums, rows_out, grad_rows, small_sums = run_backward(
         (activated, normed_mid, normed_in, attended),
         grad_mlp,
-        (slope, packed, middle, routed, taken, grad_branch, score),
+        (slope, attn_out, packed, middle, routed, taken, grad_branch, gate),
         (full_qkv, full_out, full_up, full_down),
         positions,
         documents,
@@ -1041,6 +1051,7 @@
         gain_one,
         gain_two,
     )
+    output = put_rows(hidden, rows_out, positions)
     grad_hidden = put_rows(cotangent, grad_rows, positions)
     sum_down, sum_up, sum_qkv, sum_out = (total.astype(jnp.float32) for total in sums)
     return (

time: 244 us -> 234 us (0.959)
  Pallas kernels: 226 us -> 218 us
  local copies, waits for them, and re-layouts: 4.45 us -> 1.51 us
    pallas_call x1, Pallas kernels: 93.5 us -> 83.4 us  [run_forward(): pl.pallas_call(forward_kernel, out_shape=[jax.ShapeDtypeStruct(*each_one)...]
    another operation x2 -> x0, local copies, waits for them, and re-layouts: 2.95 us -> none  [the longest x1 1.47 us: run_forward(): positions[:, None]]
where the time goes in v6:
time: 234 us; the launch traced here: 233 us
  Pallas kernels  218 us (93%)
  matrix products  7.41 us (3%)
  other arithmetic  5.6 us (2%)
    pallas_call x1, Pallas kernels, run_backward(): pl.pallas_call(reduce_kernel, out_shape=[jax.ShapeDtypeStruct(shape, bf16...  135 us
    pallas_call x1, Pallas kernels, run_forward(): pl.pallas_call(forward_kernel, out_shape=[jax.ShapeDtypeStruct(*each_one)...  83.4 us
    dot_general x2, matrix products, put_rows(): jnp.dot(hit.astype(jnp.bfloat16), rows, preferred_element_type=jnp.float32)  7.41 us
    convert_element_type x4, other arithmetic, per_device(): total.astype(jnp.float32)  5.25 us

profile of v6, /device:TPU:0, one launch (start us, length us, event | category | flops | bytes accessed | tf_op | source)
XLA Modules:
  0.0 233.4 jit_solution(18088442823658636344)
XLA Ops:
  0.6 83.4 %gather_and_forward.1 = (bf16[1024,3072]{1,0:T(8,128)(2,1)}, bf16[1024,1024]{1,0:T(8,128)(2,1)}, bf16[1024,4096]{1,0:T(8,128)(2,1)}, bf16[4096,1024]{1,0:T(8,128...) custom-call(bf16[128,3072]{1,0:T(8,128)(2,1)} %refs_0_.1, ...), custom_call_target="tpu_custom_call" | custom-call | tf_op jit(solution)/shard_map/gather_and_forward/pallas_call | solution.py:466
  84.1 0.0 copy-start.5
  84.1 134.7 %backward_and_reduce.1 = (bf16[512,1024]{1,0:T(8,128)(2,1)}, bf16[128,4096]{1,0:T(8,128)(2,1)}, bf16[128,3072]{1,0:T(8,128)(2,1)}, bf16[128,1024]{1,0:T(8,128)(2...) custom-call(bf16[256,4096]{1,0:T(8,128)(2,1)} %get-tuple-element.33.refs_0_, ...), custom_call_target="tpu_custom_call" | custom-call | tf_op jit(solution)/shard_map/backward_and_reduce/pallas_call | solution.py:978
  218.8 0.0 copy-done.5
  218.8 0.4 fusion
  219.2 0.0 copy-start
  219.2 0.0 copy-start.6
  219.2 4.6 %convert_select_fusion = bf16[2048,1024]{1,0:T(8,128)(2,1)} fusion(bf16[2048,1024]{1,0:T(8,128)(2,1)} %refs_5_.1, pred[2048]{0:T(1024)(128)(4,1)S(1)} %fusion, bf16[256,1024]{1,0:T(8,128)(2,1)} %get-tuple-element.51, s32[256]{0:T(256)S(1)} %bitcast.16), kind=kOutput, calls=%fused_computation | convolution fusion | flops 1078460416 | bytes 8915968 | tf_op jit(solution)/shard_map/dot_general | solution.py:1005
  223.8 0.0 copy-done
  223.8 0.0 copy-done.6
  223.8 0.0 copy-start.2
  223.8 0.0 copy-start.1
  223.8 2.8 %convert_select_fusion.1 = bf16[2048,1024]{1,0:T(8,128)(2,1)} fusion(bf16[2048,1024]{1,0:T(8,128)(2,1)S(1)} %copy-done, pred[2048]{0:T(1024)(128)(4,1)S(1)} %fusion, bf16[256,1024]{1,0:T(8,128)(2,1)S(1)} %copy-done.6, s32[256]{0:T(256)S(1)} %bitcast.17), kind=kOutput, calls=%fused_computation.1 | convolution fusion | flops 1078460416 | bytes 8915968 | tf_op jit(solution)/shard_map/dot_general | solution.py:1005
  226.7 0.0 copy-start.3
  226.7 0.0 copy-done.2
  226.7 0.0 copy-start.4
  226.7 1.5 convert_element_type.24
  228.2 0.0 copy-done.1
  228.2 1.6 convert_element_type.25
  229.8 0.0 copy-done.3
  229.8 1.3 convert_element_type.22
  231.1 0.0 copy-done.4
  231.1 0.8 convert_element_type.23
  231.9 1.5 fusion.3
Async XLA Ops:
  84.1 134.7 %copy-start.5 = (s32[1,256]{1,0:T(1,128)S(1)}, s32[1,256]{1,0:T(1,128)}, u32[]{:S(2)}) copy-start(s32[1,256]{1,0:T(1,128)} %refs_17_.1) | copy-start | bytes 3076
  219.2 4.6 %copy-start = (bf16[2048,1024]{1,0:T(8,128)(2,1)S(1)}, bf16[2048,1024]{1,0:T(8,128)(2,1)}, u32[]{:S(2)}) copy-start(bf16[2048,1024]{1,0:T(8,128)(2,1)} %refs_4_.1) | copy-start | bytes 12582916
  219.2 4.6 %copy-start.6 = (bf16[256,1024]{1,0:T(8,128)(2,1)S(1)}, bf16[256,1024]{1,0:T(8,128)(2,1)}, u32[]{:S(2)}) copy-start(bf16[256,1024]{1,0:T(8,128)(2,1)} %get-tuple-element.50) | copy-start | bytes 1572868
  223.8 2.8 %copy-start.2 = (bf16[128,4096]{1,0:T(8,128)(2,1)S(1)}, bf16[128,4096]{1,0:T(8,128)(2,1)}, u32[]{:S(2)}) copy-start(bf16[128,4096]{1,0:T(8,128)(2,1)} %get-tuple-element.54) | copy-start | bytes 3145732
  223.8 4.4 %copy-start.1 = (bf16[512,1024]{1,0:T(8,128)(2,1)S(1)}, bf16[512,1024]{1,0:T(8,128)(2,1)}, u32[]{:S(2)}) copy-start(bf16[512,1024]{1,0:T(8,128)(2,1)} %get-tuple-element.55) | copy-start | bytes 3145732
  226.7 3.1 %copy-start.3 = (bf16[128,3072]{1,0:T(8,128)(2,1)S(1)}, bf16[128,3072]{1,0:T(8,128)(2,1)}, u32[]{:S(2)}) copy-start(bf16[128,3072]{1,0:T(8,128)(2,1)} %get-tuple-element.52) | copy-start | bytes 2359300
  226.7 4.4 %copy-start.4 = (bf16[128,1024]{1,0:T(8,128)(2,1)S(1)}, bf16[128,1024]{1,0:T(8,128)(2,1)}, u32[]{:S(2)}) copy-start(bf16[128,1024]{1,0:T(8,128)(2,1)} %get-tuple-element.53) | copy-start | bytes 786436
